TPU v7x, 256 devices: a whole 4x4x8 slice. The times are simulated.
256 devices in a mesh: blk: 256 (over y, z, x, core).
Axes of the slice: x: 4, y: 4, z: 8, core: 2. Of those that a mesh axis runs over, the one named last changes fastest.
Arguments:
- image_features: bfloat16 [65536, 1536], P('blk'), may hold values from -0.5 to 0.5
- head_weight: bfloat16 [1536, 1152], P('blk'), may hold values from -0.15625 to 0.15625
- text_embeds: bfloat16 [65536, 1152], P('blk'), may hold values from -0.29882812 to 0.29882812
- natural_exponent_factor: float32 [1], replicated, may hold values from 1.6 to 2.6
- logit_bias: float32 [1], replicated, may hold values from -4 to -1
Outputs:
- grad_features: bfloat16 [65536, 1536], P('blk')
- grad_text: bfloat16 [65536, 1152], P('blk')
- grad_weight: float32 [1536, 1152], P('blk')
All inputs are finite; a program needn't handle non-finite values.
Results may differ from a plain program's by a relative error of at most 0.0085.
Values may be sent and summed in bfloat16 or wider, within the bound.
No kernel may reach another device: no remote copies, remote signals or barrier semaphores. Data moves between devices by JAX's collectives and lax.ppermute only.
A program may use at most 64 MiB of HBM per device.

v0:
```python
import functools

import jax
import jax.numpy as jnp
from jax import lax
from jax.experimental import pallas as pl
from jax.experimental.pallas import tpu as pltpu
from jax.sharding import Mesh
from jax.sharding import PartitionSpec as P


S = 4
EPS = 1e-06
NY, NZ, NX, NC = 4, 8, 4, 2
NDEV = NY * NZ * NX * NC
AXES = ("y", "z", "x", "c")
R, D, E = 256, 1536, 1152
HALF = D // 2
PIECE = HALF // 4
SUB = PIECE // 4
OWN = D // NDEV
F32, BF16 = jnp.float32, jnp.bfloat16
NN = (((1,), (0,)), ((), ()))
NT = (((1,), (1,)), ((), ()))
COLS = 384


def mm(a, b, dims=NN):
    return lax.dot_general(a, b, dims, preferred_element_type=F32)


def index(y, z, x, c):
    return ((y % NY * NZ + z % NZ) * NX + x % NX) * NC + c % NC


def coords(i):
    return i // (NZ * NX * NC), i // (NX * NC) % NZ, i // NC % NX, i % NC


def fetch(value, where):
    return lax.ppermute(value, AXES, [(index(*where(*coords(i))), i) for i in range(NDEV)])


def along_z(d):
    return lambda y, z, x, c: (y, z + d, x, c)


def along_first(d):
    return lambda y, z, x, c: (y, z, x + d, c) if c == 0 else (y + d, z, x, c)


def along_second(d):
    return lambda y, z, x, c: (y + d, z, x, c) if c == 0 else (y, z, x + d, c)


def sibling(y, z, x, c):
    return y, z, x, 1 - c


def along_blocks(d):
    return lambda y, z, x, c: coords((index(y, z, x, c) + d) % NDEV)


def call(body, outs, *args, flops=0, scratch=(), smem=(), limit=16):
    def spec(i):
        return pl.BlockSpec(memory_space=pltpu.SMEM if i in smem else pltpu.VMEM)

    return pl.pallas_call(
        body,
        out_shape=[pltpu.VMEM(s, d) for s, d in outs],
        in_specs=[spec(i) for i in range(len(args))],
        out_specs=[pl.BlockSpec(memory_space=pltpu.VMEM) for _ in outs],
        scratch_shapes=list(scratch),
        compiler_params=pltpu.CompilerParams(vmem_limit_bytes=limit << 20),
        cost_estimate=pl.CostEstimate(flops=flops, bytes_accessed=0, transcendentals=0),
    )(*(a if i in smem else pltpu.with_memory_space_constraint(a, pltpu.VMEM) for i, a in enumerate(args)))


def text_body(raw_ref, low_ref, length_ref):
    raw = raw_ref[...].astype(F32)
    length = jnp.sqrt(jnp.sum(raw * raw, axis=1, keepdims=True) + EPS)
    length_ref[...] = length
    low_ref[...] = (raw / length).astype(BF16)


def order_body(coord_ref, x_ref, pick_ref, xp_ref, xpt_ref):
    y, z, x, c = (coord_ref[i] for i in range(4))
    row = lax.broadcasted_iota(jnp.int32, (SUB, 1), 0)
    within = (z + row // OWN + (NZ - 3)) % NZ * (NX * NC * OWN) + row % OWN
    lanes = lax.broadcasted_iota(jnp.int32, (SUB, D), 1)

    @pl.loop(0, D // COLS)
    def _(i):
        for j in range(COLS // SUB):
            group = i * (COLS // SUB) + j
            core = (c + group // 16) % NC
            second, first = group // 4 % 4, group % 4
            at_y = (y + jnp.where(core == 0, second, first)) % NY
            at_x = (x + jnp.where(core == 0, first, second)) % NX
            base = (at_y * (NZ * NX * NC) + at_x * NC + core) * OWN
            chosen = jnp.where(lanes == within + base, 1.0, 0.0).astype(BF16)
            pick_ref[pl.ds(pl.multiple_of(i * COLS + j * SUB, 16), SUB), :] = chosen
        rows = pl.ds(pl.multiple_of(i * COLS, COLS), COLS)
        xpt_ref[rows, :] = mm(pick_ref[rows, :], x_ref[...], NT).astype(BF16)
        xp_ref[:, rows] = mm(x_ref[...], pick_ref[rows, :], NT).astype(BF16)


def embed_body(xp_ref, *refs):
    pieces, (w_ref, unit_ref, low_ref, length_ref) = refs[:8], refs[8:]
    for i, piece in enumerate(pieces):
        w_ref[pl.ds(i * PIECE, PIECE), :] = piece[...]
    squares = jnp.zeros((R, 1), F32)
    for at in range(0, E, COLS):
        cols = pl.ds(at, COLS)
        part = mm(xp_ref[...], w_ref[:, cols])
        unit_ref[:, cols] = part
        squares = squares + jnp.sum(part * part, axis=1, keepdims=True)
    length = jnp.sqrt(squares + EPS)
    length_ref[...] = length
    unit = unit_ref[...] / length
    unit_ref[...] = unit
    low_ref[...] = unit.astype(BF16)


def derivative(rows, columns, scale, bias, diagonal):
    logits = scale * mm(rows, columns, NT) + bias
    if not diagonal:
        return (scale * jax.nn.sigmoid(logits)).astype(BF16)
    matched = lax.broadcasted_iota(jnp.int32, logits.shape, 0) == lax.broadcasted_iota(
        jnp.int32, logits.shape, 1
    )
    polarity = jnp.where(matched, 1.0, -1.0)
    return (-scale * polarity * jax.nn.sigmoid(-polarity * logits)).astype(BF16)


def image_body(scalar_ref, low_ref, unit_ref, length_ref, t0, t1, t2, t3, xpt_ref, eg_ref, gw_ref, grad, pair):
    scale, bias = scalar_ref[0], scalar_ref[1]
    texts = (t0, t1, t2, t3)
    for k, text in enumerate(texts):
        pair[k] = derivative(low_ref[...], text[...], scale, bias, k == 0)
    inner = jnp.zeros((R, 1), F32)
    for at in range(0, E, COLS):
        cols = pl.ds(at, COLS)
        part = mm(pair[0], t0[:, cols])
        for k in range(1, S):
            part = part + mm(pair[k], texts[k][:, cols])
        grad[:, cols] = part
        inner = inner + jnp.sum(part * unit_ref[:, cols], axis=1, keepdims=True)
    eg_ref[...] = ((grad[...] - unit_ref[...] * inner) / length_ref[...]).astype(BF16)

    @pl.loop(0, HALF // PIECE)
    def _(i):
        at = pl.multiple_of(i * PIECE, PIECE)
        part = mm(xpt_ref[pl.ds(HALF + at, PIECE), :], eg_ref[...])
        gw_ref[pl.ds(at, PIECE), :] = part.astype(BF16)


def weight_body(xpt_ref, eg_ref, came_ref, *outs):
    for i, out in enumerate(outs):
        rows = pl.ds(i * PIECE, PIECE)
        out[...] = (mm(xpt_ref[rows, :], eg_ref[...]) + came_ref[rows, :].astype(F32)).astype(BF16)


def features_body(eg_ref, w_ref, pick_ref, out_ref, mixed):
    @pl.loop(0, D // COLS)
    def _(i):
        rows = pl.ds(pl.multiple_of(i * COLS, COLS), COLS)
        mixed[:, rows] = mm(eg_ref[...], w_ref[rows, :], NT).astype(BF16)

    @pl.loop(0, D // COLS)
    def _(i):
        cols = pl.ds(pl.multiple_of(i * COLS, COLS), COLS)
        out_ref[:, cols] = mm(mixed[...], pick_ref[:, cols]).astype(BF16)


def text_grad_body(scalar_ref, raw_ref, low_ref, length_ref, p0, p1, p2, p3, out_ref, grad, pair):
    scale, bias = scalar_ref[0], scalar_ref[1]
    images = (p0, p1, p2, p3)
    for k, image in enumerate(images):
        pair[k] = derivative(low_ref[...], image[...], scale, bias, k == 0)
    length = length_ref[...]
    inner = jnp.zeros((R, 1), F32)
    for at in range(0, E, COLS):
        cols = pl.ds(at, COLS)
        part = mm(pair[0], p0[:, cols])
        for k in range(1, S):
            part = part + mm(pair[k], images[k][:, cols])
        grad[:, cols] = part
        inner = inner + jnp.sum(part * (raw_ref[:, cols].astype(F32) / length), axis=1, keepdims=True)
    out_ref[...] = ((grad[...] - raw_ref[...].astype(F32) / length * inner) / length).astype(BF16)


def sum_body(*refs, cuts):
    ins, outs = refs[:4], refs[4:]
    total = ins[0][...].astype(F32)
    for ref in ins[1:]:
        total = total + ref[...].astype(F32)
    for out, (lo, hi) in zip(outs, cuts, strict=True):
        out[...] = total[lo:hi].astype(BF16)


def near_body(mid_ref, low_ref, high_ref, *outs):
    mid, low, high = (ref[...].astype(F32) for ref in (mid_ref, low_ref, high_ref))
    outs[0][...] = (mid[:OWN] + low[:OWN] + high[:OWN]).astype(BF16)
    outs[1][...] = mid[OWN : 2 * OWN] + low[OWN:] + high[OWN : 2 * OWN]
    outs[2][...] = (mid[2 * OWN :] + high[2 * OWN :]).astype(BF16)


def gather_weight(w):
    before, after = fetch(w, along_z(-1)), fetch(w, along_z(1))
    near = jnp.concatenate([before, w, after], 0)
    high, low = fetch(near, along_z(3)), fetch(near, along_z(-2))
    ring = jnp.concatenate([low[: 2 * OWN], near, high], 0)
    plane = [fetch(ring, along_first(d)) for d in (1, 2, 3)]
    plane = jnp.concatenate([ring] + plane, 0)
    half = [plane] + [fetch(plane, along_second(d)) for d in (1, 2, 3)]
    return half + [fetch(piece, sibling) for piece in half]


def scatter_weight(pieces):
    got = [pieces[0]] + [fetch(pieces[d], along_second(-d)) for d in (1, 2, 3)]
    cuts = [(i * SUB, (i + 1) * SUB) for i in range(4)]
    pieces = call(functools.partial(sum_body, cuts=cuts), [((SUB, E), BF16)] * 4, *got, flops=10**8)
    got = [pieces[0]] + [fetch(pieces[d], along_first(-d)) for d in (1, 2, 3)]
    cuts = [(0, 2 * OWN), (2 * OWN, 5 * OWN), (5 * OWN, 8 * OWN)]
    low, mid, high = call(
        functools.partial(sum_body, cuts=cuts), [((hi - lo, E), BF16) for lo, hi in cuts], *got, flops=10**8
    )
    high, low = fetch(high, along_z(-3)), fetch(low, along_z(2))
    before, own, after = call(
        near_body, [((OWN, E), BF16), ((OWN, E), F32), ((OWN, E), BF16)], mid, low, high, flops=10**8
    )
    before, after = fetch(before, along_z(1)), fetch(after, along_z(-1))
    return own + before.astype(F32) + after.astype(F32)


def on_device(image_features, head_weight, text_embeds, natural_exponent_factor, logit_bias):
    scalars = jnp.concatenate([jnp.exp(natural_exponent_factor), logit_bias])
    place = jnp.stack([lax.axis_index(a) for a in AXES]).astype(jnp.int32)
    weight = gather_weight(head_weight)
    text_low, text_length = call(
        text_body, [((R, E), BF16), ((R, 1), F32)], text_embeds, flops=10**8
    )
    texts = [text_low]
    for _ in range(1, S):
        texts.append(fetch(texts[-1], along_blocks(1)))
    pick, xp, xpt = call(
        order_body, [((D, D), BF16), ((R, D), BF16), ((D, R), BF16)], place, image_features,
        flops=4 * D * D * R, smem=(0,),
    )
    full, unit, low, length = call(
        embed_body, [((D, E), BF16), ((R, E), F32), ((R, E), BF16), ((R, 1), F32)], xp, *weight,
        flops=2 * R * D * E,
    )
    images = [low]
    for _ in range(1, S):
        images.append(fetch(images[-1], along_blocks(-1)))
    work = [pltpu.VMEM((R, E), F32), pltpu.VMEM((S, R, R), BF16)]
    eg, sent = call(
        image_body, [((R, E), BF16), ((HALF, E), BF16)], scalars, low, unit, length, *texts, xpt,
        flops=16 * R * R * E + 2 * R * HALF * E, scratch=work, smem=(0,),
    )
    came = fetch(sent, sibling)
    (grad_features,) = call(
        features_body, [((R, D), BF16)], eg, full, pick, flops=2 * R * D * E + 2 * R * D * D,
        scratch=[pltpu.VMEM((R, D), BF16)],
    )
    pieces = call(weight_body, [((PIECE, E), BF16)] * 4, xpt, eg, came, flops=2 * R * HALF * E)
    grad_weight = scatter_weight(pieces)
    (grad_text,) = call(
        text_grad_body, [((R, E), BF16)], scalars, text_embeds, text_low, text_length, *images,
        flops=16 * R * R * E, scratch=work, smem=(0,),
    )
    return grad_features, grad_text, grad_weight


def solution(mesh):
    finer = Mesh(mesh.devices.reshape(NY, NZ, NX, NC), AXES)
    rows = P(AXES, None)

    return jax.shard_map(
        on_device,
        mesh=finer,
        in_specs=(rows, rows, rows, P(), P()),
        out_specs=(rows, rows, rows),
        check_vma=False,
    )
```

profile of v0, /device:TPU:1, one launch (start us, length us, event | category | flops | bytes accessed | tf_op | source)
XLA Modules:
  0.0 139.9 jit_solution(6765462453929674177)
XLA Ops:
  0.6 1.1 copy-done
  1.7 0.2 shard_map.78
  1.9 3.3 %collective-permute-start.14 = (bf16[256,1152]{1,0:T(8,128)(2,1)S(1)}, bf16[256,1152]{1,0:T(8,128)(2,1)}, u32[]{:S(2)}, u32[]{:S(2)}) collective-permute-start(bf16[256,1152]{1,0:T(8,128)(2,1)S(1)} %get-tuple-element.32.t0.low_ref), channel_id=1, source_target_pairs={{1,0},{2,1},{3,2},{4,3},{5,4},{6,5},{7,6},{8,7},{9,8},{10,9},{11,1... | collective-permute-start | bytes 1769480 | tf_op jit(solution)/shard_map/ppermute | solution.py:41
  5.2 3.9 %collective-permute-start.1 = (bf16[6,1152]{1,0:T(8,128)(2,1)}, bf16[6,1152]{1,0:T(8,128)(2,1)S(1)}, u32[]{:S(2)}, u32[]{:S(2)}) collective-permute-start(bf16[6,1152]{1,0:T(8,128)(2,1)} %param.6), channel_id=1, source_target_pairs={{8,0},{9,1},{10,2},{11,3},{12,4},{13,5},{14,6},{15,7},{16,8},{17,9... | collective-permute-start | bytes 41480 | tf_op jit(solution)/shard_map/ppermute | solution.py:41
  9.1 3.2 %collective-permute-done.14.t1 = bf16[256,1152]{1,0:T(8,128)(2,1)} collective-permute-done((bf16[256,1152]{1,0:T(8,128)(2,1)S(1)}, bf16[256,1152]{1,0:T(8,128)(2,1)}, u32[]{:S(2)}, u32[]{:S(2)}) %collective-permute-start.14) | collective-permute-done | bytes 589856 | tf_op jit(solution)/shard_map/ppermute | solution.py:41
  12.3 8.6 %collective-permute-start.15 = (bf16[256,1152]{1,0:T(8,128)(2,1)}, bf16[256,1152]{1,0:T(8,128)(2,1)}, u32[]{:S(2)}, u32[]{:S(2)}) collective-permute-start(bf16[256,1152]{1,0:T(8,128)(2,1)} %collective-permute-done.14.t1), channel_id=1, source_target_pairs={{1,0},{2,1},{3,2},{4,3},{5,4},{6,5},{7,6},{8,7},{9,8},{10,9},{11,1... | collective-permute-start | bytes 1769480 | tf_op jit(solution)/shard_map/ppermute | solution.py:41
  20.9 0.7 pad_maximum_fusion
  21.7 0.3 collective-permute-start.3
  22.0 4.8 %collective-permute-done.2 = bf16[18,1152]{1,0:T(8,128)(2,1)S(1)} collective-permute-done((bf16[18,1152]{1,0:T(8,128)(2,1)S(1)}, bf16[18,1152]{1,0:T(8,128)(2,1)S(1)}, u32[]{:S(2)}, u32[]{:S(2)}) %collective-permute-start.2) | collective-permute-done | bytes 41504 | tf_op jit(solution)/shard_map/ppermute | solution.py:41
  26.8 0.9 collective-permute-done.3
  27.8 1.1 concatenate.16
  28.9 0.4 collective-permute-start.4
  29.3 0.2 collective-permute-start.5
  29.5 0.9 collective-permute-start.6
  30.5 2.1 %collective-permute-done.4 = bf16[48,1152]{1,0:T(8,128)(2,1)S(1)} collective-permute-done((bf16[48,1152]{1,0:T(8,128)(2,1)S(1)}, bf16[48,1152]{1,0:T(8,128)(2,1)S(1)}, u32[]{:S(2)}, u32[]{:S(2)}) %collective-permute-start.4) | collective-permute-done | bytes 110624 | tf_op jit(solution)/shard_map/ppermute | solution.py:41
  32.6 2.1 %collective-permute-done.5 = bf16[48,1152]{1,0:T(8,128)(2,1)S(1)} collective-permute-done((bf16[48,1152]{1,0:T(8,128)(2,1)S(1)}, bf16[48,1152]{1,0:T(8,128)(2,1)S(1)}, u32[]{:S(2)}, u32[]{:S(2)}) %collective-permute-start.5) | collective-permute-done | bytes 110624 | tf_op jit(solution)/shard_map/ppermute | solution.py:41
  34.7 0.9 collective-permute-done.6
  35.6 1.2 concatenate.17.refs_0_
  36.8 4.6 %collective-permute-start.7 = (bf16[192,1152]{1,0:T(8,128)(2,1)S(1)}, bf16[192,1152]{1,0:T(8,128)(2,1)S(1)}, u32[]{:S(2)}, u32[]{:S(2)}) collective-permute-start(bf16[192,1152]{1,0:T(8,128)(2,1)S(1)} %concatenate.17.refs_0_), channel_id=1, source_target_pairs={{64,0},{3,1},{66,2},{5,3},{68,4},{7,5},{70,6},{1,7},{72,8},{11,9},... | collective-permute-start | bytes 1327112 | tf_op jit(solution)/shard_map/ppermute | solution.py:41
  41.4 0.7 collective-permute-start.9
  42.0 7.7 %collective-permute-start.16 = (bf16[256,1152]{1,0:T(8,128)(2,1)}, bf16[256,1152]{1,0:T(8,128)(2,1)}, u32[]{:S(2)}, u32[]{:S(2)}) collective-permute-start(bf16[256,1152]{1,0:T(8,128)(2,1)} %collective-permute-done.15.t2), channel_id=1, source_target_pairs={{1,0},{2,1},{3,2},{4,3},{5,4},{6,5},{7,6},{8,7},{9,8},{10,9},{11,1... | collective-permute-start | bytes 1769480 | tf_op jit(solution)/shard_map/ppermute | solution.py:41
  51.2 1.3 collective-permute-done.7.refs_1_
  52.5 3.5 %collective-permute-start.11 = (bf16[192,1152]{1,0:T(8,128)(2,1)S(1)}, bf16[192,1152]{1,0:T(8,128)(2,1)S(1)}, u32[]{:S(2)}, u32[]{:S(2)}) collective-permute-start(bf16[192,1152]{1,0:T(8,128)(2,1)S(1)} %collective-permute-done.7.refs_1_), channel_id=1, source_target_pairs={{1,0},{0,1},{3,2},{2,3},{5,4},{4,5},{7,6},{6,7},{9,8},{8,9},{11,10... | collective-permute-start | bytes 1327112 | tf_op jit(solution)/shard_map/ppermute | solution.py:41
  56.0 1.7 %collective-permute-start.12 = (bf16[192,1152]{1,0:T(8,128)(2,1)S(1)}, bf16[192,1152]{1,0:T(8,128)(2,1)S(1)}, u32[]{:S(2)}, u32[]{:S(2)}) collective-permute-start(bf16[192,1152]{1,0:T(8,128)(2,1)S(1)} %collective-permute-done.8.refs_2_), channel_id=1, source_target_pairs={{1,0},{0,1},{3,2},{2,3},{5,4},{4,5},{7,6},{6,7},{9,8},{8,9},{11,10... | collective-permute-start | bytes 1327112 | tf_op jit(solution)/shard_map/ppermute | solution.py:41
  57.7 4.6 %collective-permute-start.13 = (bf16[192,1152]{1,0:T(8,128)(2,1)S(1)}, bf16[192,1152]{1,0:T(8,128)(2,1)S(1)}, u32[]{:S(2)}, u32[]{:S(2)}) collective-permute-start(bf16[192,1152]{1,0:T(8,128)(2,1)S(1)} %collective-permute-done.9.refs_3_), channel_id=1, source_target_pairs={{1,0},{0,1},{3,2},{2,3},{5,4},{4,5},{7,6},{6,7},{9,8},{8,9},{11,10... | collective-permute-start | bytes 1327112 | tf_op jit(solution)/shard_map/ppermute | solution.py:41
  62.5 5.9 %shard_map.76 = (bf16[1536,1536]{1,0:T(8,128)(2,1)S(1)}, bf16[256,1536]{1,0:T(8,128)(2,1)S(1)}, bf16[1536,256]{1,0:T(8,128)(2,1)S(1)}) custom-call(s32[4]{0:T(128)S(1)} %pad_add_fusion.coord_ref, bf16[256,1536]{1,0:T(8,128)(2,1)S(1)} %copy-done.2), custom_call_target="tpu_custom_call" | custom-call | flops 2415919104 | tf_op jit(solution)/shard_map/pallas_call | solution.py:68
  68.5 1.6 %shard_map.77 = (bf16[1536,1152]{1,0:T(8,128)(2,1)S(1)}, f32[256,1152]{1,0:T(8,128)S(1)}, bf16[256,1152]{1,0:T(8,128)(2,1)S(1)}, f32[256,1]{1,0:T(8,128)S(1)}) custom-call(bf16[256,1536]{1,0:T(8,128)(2,1)S(1)} %get-tuple-element.28.xp_ref, bf16[192,1152]{1,0:T(8,128)(2,1)S(1)} %concatenate.17.refs_0_, bf16[192,1152]{1,0:T(8,128)(2,1)S(1)} %collective-permute-done.7.refs_1_, ...), custom_call_target="tpu_custom_call" | custom-call | flops 905969664 | tf_op jit(solution)/shard_map/pallas_call | solution.py:68
  70.1 4.6 %shard_map.79 = (bf16[256,1152]{1,0:T(8,128)(2,1)S(1)}, bf16[768,1152]{1,0:T(8,128)(2,1)S(1)}) custom-call(f32[2]{0:T(128)S(1)} %pad_maximum_fusion.1.scalar_ref, bf16[256,1152]{1,0:T(8,128)(2,1)S(1)} %get-tuple-element.29.low_ref.p0, f32[256,1152]{1,0:T(8,128)S(1)} %get-tuple-element.30.unit_ref, f32[256,1]{1,0:T(8,128)S(1)} %get-tuple-element.31.length_ref, ...), custom_call_target="tpu_custom_call" | custom-call | flops 1660944384 | tf_op jit(solution)/shard_map/pallas_call | solution.py:68
  74.7 0.1 collective-permute-start.20
  74.8 1.5 %collective-permute-start.17 = (bf16[256,1152]{1,0:T(8,128)(2,1)S(1)}, bf16[256,1152]{1,0:T(8,128)(2,1)S(1)}, u32[]{:S(2)}, u32[]{:S(2)}) collective-permute-start(bf16[256,1152]{1,0:T(8,128)(2,1)S(1)} %get-tuple-element.29.low_ref.p0), channel_id=1, source_target_pairs={{255,0},{0,1},{1,2},{2,3},{3,4},{4,5},{5,6},{6,7},{7,8},{8,9},{9,1... | collective-permute-start | bytes 1769480 | tf_op jit(solution)/shard_map/ppermute | solution.py:41
  76.2 6.8 %collective-permute-done.17.p1 = bf16[256,1152]{1,0:T(8,128)(2,1)S(1)} collective-permute-done((bf16[256,1152]{1,0:T(8,128)(2,1)S(1)}, bf16[256,1152]{1,0:T(8,128)(2,1)S(1)}, u32[]{:S(2)}, u32[]{:S(2)}) %collective-permute-start.17) | collective-permute-done | bytes 589856 | tf_op jit(solution)/shard_map/ppermute | solution.py:41
  83.1 2.5 %collective-permute-start.18 = (bf16[256,1152]{1,0:T(8,128)(2,1)S(1)}, bf16[256,1152]{1,0:T(8,128)(2,1)S(1)}, u32[]{:S(2)}, u32[]{:S(2)}) collective-permute-start(bf16[256,1152]{1,0:T(8,128)(2,1)S(1)} %collective-permute-done.17.p1), channel_id=1, source_target_pairs={{255,0},{0,1},{1,2},{2,3},{3,4},{4,5},{5,6},{6,7},{7,8},{8,9},{9,1... | collective-permute-start | bytes 1769480 | tf_op jit(solution)/shard_map/ppermute | solution.py:41
  85.6 0.7 shard_map.82
  86.4 10.4 %collective-permute-start.22 = (bf16[192,1152]{1,0:T(8,128)(2,1)S(1)}, bf16[192,1152]{1,0:T(8,128)(2,1)S(1)}, u32[]{:S(2)}, u32[]{:S(2)}) collective-permute-start(bf16[192,1152]{1,0:T(8,128)(2,1)S(1)} %get-tuple-element.41), channel_id=1, source_target_pairs={{128,0},{5,1},{130,2},{7,3},{132,4},{1,5},{134,6},{3,7},{136,8},{1... | collective-permute-start | bytes 1327112 | tf_op jit(solution)/shard_map/ppermute | solution.py:41
  96.8 18.0 %collective-permute-done.21.refs_1_ = bf16[192,1152]{1,0:T(8,128)(2,1)S(1)} collective-permute-done((bf16[192,1152]{1,0:T(8,128)(2,1)S(1)}, bf16[192,1152]{1,0:T(8,128)(2,1)S(1)}, u32[]{:S(2)}, u32[]{:S(2)}) %collective-permute-start.21) | collective-permute-done | bytes 442400 | tf_op jit(solution)/shard_map/ppermute | solution.py:41
  114.9 0.2 shard_map.83
  115.1 3.7 %collective-permute-start.24 = (bf16[48,1152]{1,0:T(8,128)(2,1)S(1)}, bf16[48,1152]{1,0:T(8,128)(2,1)S(1)}, u32[]{:S(2)}, u32[]{:S(2)}) collective-permute-start(bf16[48,1152]{1,0:T(8,128)(2,1)S(1)} %get-tuple-element.44), channel_id=1, source_target_pairs={{6,0},{193,1},{0,2},{195,3},{2,4},{197,5},{4,6},{199,7},{14,8},{20... | collective-permute-start | bytes 331784 | tf_op jit(solution)/shard_map/ppermute | solution.py:41
  118.8 2.5 %collective-permute-start.26 = (bf16[48,1152]{1,0:T(8,128)(2,1)S(1)}, bf16[48,1152]{1,0:T(8,128)(2,1)S(1)}, u32[]{:S(2)}, u32[]{:S(2)}) collective-permute-start(bf16[48,1152]{1,0:T(8,128)(2,1)S(1)} %get-tuple-element.46), channel_id=1, source_target_pairs={{2,0},{65,1},{4,2},{67,3},{6,4},{69,5},{0,6},{71,7},{10,8},{73,9},... | collective-permute-start | bytes 331784 | tf_op jit(solution)/shard_map/ppermute | solution.py:41
  121.3 2.7 %collective-permute-done.24.refs_1_ = bf16[48,1152]{1,0:T(8,128)(2,1)S(1)} collective-permute-done((bf16[48,1152]{1,0:T(8,128)(2,1)S(1)}, bf16[48,1152]{1,0:T(8,128)(2,1)S(1)}, u32[]{:S(2)}, u32[]{:S(2)}) %collective-permute-start.24) | collective-permute-done | bytes 110624 | tf_op jit(solution)/shard_map/ppermute | solution.py:41
  124.0 0.9 collective-permute-start.28
  124.9 4.3 %collective-permute-start.27 = (bf16[12,1152]{1,0:T(8,128)(2,1)S(1)}, bf16[12,1152]{1,0:T(8,128)(2,1)S(1)}, u32[]{:S(2)}, u32[]{:S(2)}) collective-permute-start(bf16[12,1152]{1,0:T(8,128)(2,1)S(1)} %get-tuple-element.48), channel_id=1, source_target_pairs={{16,0},{17,1},{18,2},{19,3},{20,4},{21,5},{22,6},{23,7},{24,8},{25... | collective-permute-start | bytes 82952 | tf_op jit(solution)/shard_map/ppermute | solution.py:41
  129.2 4.3 %shard_map.80 = bf16[256,1536]{1,0:T(8,128)(2,1)S(1)} custom-call(bf16[256,1152]{1,0:T(8,128)(2,1)S(1)} %get-tuple-element.34.eg_ref, bf16[1536,1152]{1,0:T(8,128)(2,1)S(1)} %get-tuple-element.35.w_ref, bf16[1536,1536]{1,0:T(8,128)(2,1)S(1)} %get-tuple-element.36.pick_ref), custom_call_target="tpu_custom_call" | custom-call | flops 2113929216 | tf_op jit(solution)/shard_map/pallas_call | solution.py:68
  133.5 0.9 copy.8
  134.5 0.1 collective-permute-start.29
  134.6 1.4 %collective-permute-start.30 = (bf16[6,1152]{1,0:T(8,128)(2,1)S(1)}, bf16[6,1152]{1,0:T(8,128)(2,1)S(1)}, u32[]{:S(2)}, u32[]{:S(2)}) collective-permute-start(bf16[6,1152]{1,0:T(8,128)(2,1)S(1)} %get-tuple-element.52), channel_id=1, source_target_pairs={{56,0},{57,1},{58,2},{59,3},{60,4},{61,5},{62,6},{63,7},{0,8},{1,9... | collective-permute-start | bytes 41480 | tf_op jit(solution)/shard_map/ppermute | solution.py:41
  136.0 2.4 %shard_map.81 = bf16[256,1152]{1,0:T(8,128)(2,1)S(1)} custom-call(f32[2]{0:T(128)S(1)} %pad_maximum_fusion.1.scalar_ref, bf16[256,1152]{1,0:T(8,128)(2,1)S(1)} %copy-done.1, bf16[256,1152]{1,0:T(8,128)(2,1)S(1)} %get-tuple-element.32.t0.low_ref, f32[256,1]{1,0:T(8,128)S(1)} %get-tuple-element.37.length_ref, ...), custom_call_target="tpu_custom_call" | custom-call | flops 1207959552 | tf_op jit(solution)/shard_map/pallas_call | solution.py:68
  138.5 0.8 copy.9
  139.3 0.6 convert_add_fusion
  (39 shorter events, 0.6 us)
Async XLA Ops:
  0.6 1.1 copy-start
  1.7 60.8 %copy-start.2 = (bf16[256,1536]{1,0:T(8,128)(2,1)S(1)}, bf16[256,1536]{1,0:T(8,128)(2,1)}, u32[]{:S(2)}) copy-start(bf16[256,1536]{1,0:T(8,128)(2,1)} %x_ref.1) | copy-start | bytes 2359300
  1.9 10.3 %collective-permute-start.14 = (bf16[256,1152]{1,0:T(8,128)(2,1)S(1)}, bf16[256,1152]{1,0:T(8,128)(2,1)}, u32[]{:S(2)}, u32[]{:S(2)}) collective-permute-start(bf16[256,1152]{1,0:T(8,128)(2,1)S(1)} %get-tuple-element.32.t0.low_ref), channel_id=1, source_target_pairs={{1,0},{2,1},{3,2},{4,3},{5,4},{6,5},{7,6},{8,7},{9,8},{10,9},{11,1... | collective-permute-start | bytes 1769480 | tf_op jit(solution)/shard_map/ppermute | solution.py:41
  5.2 15.6 %collective-permute-start = (bf16[6,1152]{1,0:T(8,128)(2,1)}, bf16[6,1152]{1,0:T(8,128)(2,1)S(1)}, u32[]{:S(2)}, u32[]{:S(2)}) collective-permute-start(bf16[6,1152]{1,0:T(8,128)(2,1)} %param.6), channel_id=1, source_target_pairs={{56,0},{57,1},{58,2},{59,3},{60,4},{61,5},{62,6},{63,7},{0,8},{1,9... | collective-permute-start | bytes 41480 | tf_op jit(solution)/shard_map/ppermute | solution.py:41
  5.2 15.6 %collective-permute-start.1 = (bf16[6,1152]{1,0:T(8,128)(2,1)}, bf16[6,1152]{1,0:T(8,128)(2,1)S(1)}, u32[]{:S(2)}, u32[]{:S(2)}) collective-permute-start(bf16[6,1152]{1,0:T(8,128)(2,1)} %param.6), channel_id=1, source_target_pairs={{8,0},{9,1},{10,2},{11,3},{12,4},{13,5},{14,6},{15,7},{16,8},{17,9... | collective-permute-start | bytes 41480 | tf_op jit(solution)/shard_map/ppermute | solution.py:41
  12.3 29.8 %collective-permute-start.15 = (bf16[256,1152]{1,0:T(8,128)(2,1)}, bf16[256,1152]{1,0:T(8,128)(2,1)}, u32[]{:S(2)}, u32[]{:S(2)}) collective-permute-start(bf16[256,1152]{1,0:T(8,128)(2,1)} %collective-permute-done.14.t1), channel_id=1, source_target_pairs={{1,0},{2,1},{3,2},{4,3},{5,4},{6,5},{7,6},{8,7},{9,8},{10,9},{11,1... | collective-permute-start | bytes 1769480 | tf_op jit(solution)/shard_map/ppermute | solution.py:41
  21.6 5.2 %collective-permute-start.2 = (bf16[18,1152]{1,0:T(8,128)(2,1)S(1)}, bf16[18,1152]{1,0:T(8,128)(2,1)S(1)}, u32[]{:S(2)}, u32[]{:S(2)}) collective-permute-start(bf16[18,1152]{1,0:T(8,128)(2,1)S(1)} %pad_maximum_fusion), channel_id=1, source_target_pairs={{48,0},{49,1},{50,2},{51,3},{52,4},{53,5},{54,6},{55,7},{56,8},{57... | collective-permute-start | bytes 124424 | tf_op jit(solution)/shard_map/ppermute | solution.py:41
  21.7 6.1 %collective-permute-start.3 = (bf16[18,1152]{1,0:T(8,128)(2,1)S(1)}, bf16[18,1152]{1,0:T(8,128)(2,1)S(1)}, u32[]{:S(2)}, u32[]{:S(2)}) collective-permute-start(bf16[18,1152]{1,0:T(8,128)(2,1)S(1)} %pad_maximum_fusion), channel_id=1, source_target_pairs={{24,0},{25,1},{26,2},{27,3},{28,4},{29,5},{30,6},{31,7},{32,8},{33... | collective-permute-start | bytes 124424 | tf_op jit(solution)/shard_map/ppermute | solution.py:41
  28.9 3.7 %collective-permute-start.4 = (bf16[48,1152]{1,0:T(8,128)(2,1)S(1)}, bf16[48,1152]{1,0:T(8,128)(2,1)S(1)}, u32[]{:S(2)}, u32[]{:S(2)}) collective-permute-start(bf16[48,1152]{1,0:T(8,128)(2,1)S(1)} %concatenate.16), channel_id=1, source_target_pairs={{2,0},{65,1},{4,2},{67,3},{6,4},{69,5},{0,6},{71,7},{10,8},{73,9},... | collective-permute-start | bytes 331784 | tf_op jit(solution)/shard_map/ppermute | solution.py:41
  29.3 5.4 %collective-permute-start.5 = (bf16[48,1152]{1,0:T(8,128)(2,1)S(1)}, bf16[48,1152]{1,0:T(8,128)(2,1)S(1)}, u32[]{:S(2)}, u32[]{:S(2)}) collective-permute-start(bf16[48,1152]{1,0:T(8,128)(2,1)S(1)} %concatenate.16), channel_id=1, source_target_pairs={{4,0},{129,1},{6,2},{131,3},{0,4},{133,5},{2,6},{135,7},{12,8},{13... | collective-permute-start | bytes 331784 | tf_op jit(solution)/shard_map/ppermute | solution.py:41
  29.5 6.1 %collective-permute-start.6 = (bf16[48,1152]{1,0:T(8,128)(2,1)S(1)}, bf16[48,1152]{1,0:T(8,128)(2,1)S(1)}, u32[]{:S(2)}, u32[]{:S(2)}) collective-permute-start(bf16[48,1152]{1,0:T(8,128)(2,1)S(1)} %concatenate.16), channel_id=1, source_target_pairs={{6,0},{193,1},{0,2},{195,3},{2,4},{197,5},{4,6},{199,7},{14,8},{20... | collective-permute-start | bytes 331784 | tf_op jit(solution)/shard_map/ppermute | solution.py:41
  36.8 15.7 %collective-permute-start.7 = (bf16[192,1152]{1,0:T(8,128)(2,1)S(1)}, bf16[192,1152]{1,0:T(8,128)(2,1)S(1)}, u32[]{:S(2)}, u32[]{:S(2)}) collective-permute-start(bf16[192,1152]{1,0:T(8,128)(2,1)S(1)} %concatenate.17.refs_0_), channel_id=1, source_target_pairs={{64,0},{3,1},{66,2},{5,3},{68,4},{7,5},{70,6},{1,7},{72,8},{11,9},... | collective-permute-start | bytes 1327112 | tf_op jit(solution)/shard_map/ppermute | solution.py:41
  41.4 14.7 %collective-permute-start.8 = (bf16[192,1152]{1,0:T(8,128)(2,1)S(1)}, bf16[192,1152]{1,0:T(8,128)(2,1)S(1)}, u32[]{:S(2)}, u32[]{:S(2)}) collective-permute-start(bf16[192,1152]{1,0:T(8,128)(2,1)S(1)} %concatenate.17.refs_0_), channel_id=1, source_target_pairs={{128,0},{5,1},{130,2},{7,3},{132,4},{1,5},{134,6},{3,7},{136,8},{1... | collective-permute-start | bytes 1327112 | tf_op jit(solution)/shard_map/ppermute | solution.py:41
  41.4 16.4 %collective-permute-start.9 = (bf16[192,1152]{1,0:T(8,128)(2,1)S(1)}, bf16[192,1152]{1,0:T(8,128)(2,1)S(1)}, u32[]{:S(2)}, u32[]{:S(2)}) collective-permute-start(bf16[192,1152]{1,0:T(8,128)(2,1)S(1)} %concatenate.17.refs_0_), channel_id=1, source_target_pairs={{192,0},{7,1},{194,2},{1,3},{196,4},{3,5},{198,6},{5,7},{200,8},{1... | collective-permute-start | bytes 1327112 | tf_op jit(solution)/shard_map/ppermute | solution.py:41
  42.0 28.1 %collective-permute-start.16 = (bf16[256,1152]{1,0:T(8,128)(2,1)}, bf16[256,1152]{1,0:T(8,128)(2,1)}, u32[]{:S(2)}, u32[]{:S(2)}) collective-permute-start(bf16[256,1152]{1,0:T(8,128)(2,1)} %collective-permute-done.15.t2), channel_id=1, source_target_pairs={{1,0},{2,1},{3,2},{4,3},{5,4},{6,5},{7,6},{8,7},{9,8},{10,9},{11,1... | collective-permute-start | bytes 1769480 | tf_op jit(solution)/shard_map/ppermute | solution.py:41
  51.1 17.4 %collective-permute-start.10 = (bf16[192,1152]{1,0:T(8,128)(2,1)S(1)}, bf16[192,1152]{1,0:T(8,128)(2,1)S(1)}, u32[]{:S(2)}, u32[]{:S(2)}) collective-permute-start(bf16[192,1152]{1,0:T(8,128)(2,1)S(1)} %concatenate.17.refs_0_), channel_id=1, source_target_pairs={{1,0},{0,1},{3,2},{2,3},{5,4},{4,5},{7,6},{6,7},{9,8},{8,9},{11,10... | collective-permute-start | bytes 1327112 | tf_op jit(solution)/shard_map/ppermute | solution.py:41
  52.5 15.9 %collective-permute-start.11 = (bf16[192,1152]{1,0:T(8,128)(2,1)S(1)}, bf16[192,1152]{1,0:T(8,128)(2,1)S(1)}, u32[]{:S(2)}, u32[]{:S(2)}) collective-permute-start(bf16[192,1152]{1,0:T(8,128)(2,1)S(1)} %collective-permute-done.7.refs_1_), channel_id=1, source_target_pairs={{1,0},{0,1},{3,2},{2,3},{5,4},{4,5},{7,6},{6,7},{9,8},{8,9},{11,10... | collective-permute-start | bytes 1327112 | tf_op jit(solution)/shard_map/ppermute | solution.py:41
  56.0 12.4 %collective-permute-start.12 = (bf16[192,1152]{1,0:T(8,128)(2,1)S(1)}, bf16[192,1152]{1,0:T(8,128)(2,1)S(1)}, u32[]{:S(2)}, u32[]{:S(2)}) collective-permute-start(bf16[192,1152]{1,0:T(8,128)(2,1)S(1)} %collective-permute-done.8.refs_2_), channel_id=1, source_target_pairs={{1,0},{0,1},{3,2},{2,3},{5,4},{4,5},{7,6},{6,7},{9,8},{8,9},{11,10... | collective-permute-start | bytes 1327112 | tf_op jit(solution)/shard_map/ppermute | solution.py:41
  57.7 10.7 %collective-permute-start.13 = (bf16[192,1152]{1,0:T(8,128)(2,1)S(1)}, bf16[192,1152]{1,0:T(8,128)(2,1)S(1)}, u32[]{:S(2)}, u32[]{:S(2)}) collective-permute-start(bf16[192,1152]{1,0:T(8,128)(2,1)S(1)} %collective-permute-done.9.refs_3_), channel_id=1, source_target_pairs={{1,0},{0,1},{3,2},{2,3},{5,4},{4,5},{7,6},{6,7},{9,8},{8,9},{11,10... | collective-permute-start | bytes 1327112 | tf_op jit(solution)/shard_map/ppermute | solution.py:41
  74.7 10.9 %collective-permute-start.20 = (bf16[768,1152]{1,0:T(8,128)(2,1)S(1)}, bf16[768,1152]{1,0:T(8,128)(2,1)S(1)}, u32[]{:S(2)}, u32[]{:S(2)}) collective-permute-start(bf16[768,1152]{1,0:T(8,128)(2,1)S(1)} %get-tuple-element.38), channel_id=1, source_target_pairs={{1,0},{0,1},{3,2},{2,3},{5,4},{4,5},{7,6},{6,7},{9,8},{8,9},{11,10... | collective-permute-start | bytes 5308424 | tf_op jit(solution)/shard_map/ppermute | solution.py:41
  74.8 8.3 %collective-permute-start.17 = (bf16[256,1152]{1,0:T(8,128)(2,1)S(1)}, bf16[256,1152]{1,0:T(8,128)(2,1)S(1)}, u32[]{:S(2)}, u32[]{:S(2)}) collective-permute-start(bf16[256,1152]{1,0:T(8,128)(2,1)S(1)} %get-tuple-element.29.low_ref.p0), channel_id=1, source_target_pairs={{255,0},{0,1},{1,2},{2,3},{3,4},{4,5},{5,6},{6,7},{7,8},{8,9},{9,1... | collective-permute-start | bytes 1769480 | tf_op jit(solution)/shard_map/ppermute | solution.py:41
  83.1 13.8 %collective-permute-start.18 = (bf16[256,1152]{1,0:T(8,128)(2,1)S(1)}, bf16[256,1152]{1,0:T(8,128)(2,1)S(1)}, u32[]{:S(2)}, u32[]{:S(2)}) collective-permute-start(bf16[256,1152]{1,0:T(8,128)(2,1)S(1)} %collective-permute-done.17.p1), channel_id=1, source_target_pairs={{255,0},{0,1},{1,2},{2,3},{3,4},{4,5},{5,6},{6,7},{7,8},{8,9},{9,1... | collective-permute-start | bytes 1769480 | tf_op jit(solution)/shard_map/ppermute | solution.py:41
  86.3 28.6 %collective-permute-start.21 = (bf16[192,1152]{1,0:T(8,128)(2,1)S(1)}, bf16[192,1152]{1,0:T(8,128)(2,1)S(1)}, u32[]{:S(2)}, u32[]{:S(2)}) collective-permute-start(bf16[192,1152]{1,0:T(8,128)(2,1)S(1)} %get-tuple-element.40), channel_id=1, source_target_pairs={{192,0},{7,1},{194,2},{1,3},{196,4},{3,5},{198,6},{5,7},{200,8},{1... | collective-permute-start | bytes 1327112 | tf_op jit(solution)/shard_map/ppermute | solution.py:41
  86.4 28.5 %collective-permute-start.22 = (bf16[192,1152]{1,0:T(8,128)(2,1)S(1)}, bf16[192,1152]{1,0:T(8,128)(2,1)S(1)}, u32[]{:S(2)}, u32[]{:S(2)}) collective-permute-start(bf16[192,1152]{1,0:T(8,128)(2,1)S(1)} %get-tuple-element.41), channel_id=1, source_target_pairs={{128,0},{5,1},{130,2},{7,3},{132,4},{1,5},{134,6},{3,7},{136,8},{1... | collective-permute-start | bytes 1327112 | tf_op jit(solution)/shard_map/ppermute | solution.py:41
  96.8 18.0 %collective-permute-start.23 = (bf16[192,1152]{1,0:T(8,128)(2,1)S(1)}, bf16[192,1152]{1,0:T(8,128)(2,1)S(1)}, u32[]{:S(2)}, u32[]{:S(2)}) collective-permute-start(bf16[192,1152]{1,0:T(8,128)(2,1)S(1)} %get-tuple-element.42), channel_id=1, source_target_pairs={{64,0},{3,1},{66,2},{5,3},{68,4},{7,5},{70,6},{1,7},{72,8},{11,9},... | collective-permute-start | bytes 1327112 | tf_op jit(solution)/shard_map/ppermute | solution.py:41
  96.8 39.2 %collective-permute-start.19 = (bf16[256,1152]{1,0:T(8,128)(2,1)S(1)}, bf16[256,1152]{1,0:T(8,128)(2,1)S(1)}, u32[]{:S(2)}, u32[]{:S(2)}) collective-permute-start(bf16[256,1152]{1,0:T(8,128)(2,1)S(1)} %collective-permute-done.18.p2), channel_id=1, source_target_pairs={{255,0},{0,1},{1,2},{2,3},{3,4},{4,5},{5,6},{6,7},{7,8},{8,9},{9,1... | collective-permute-start | bytes 1769480 | tf_op jit(solution)/shard_map/ppermute | solution.py:41
  115.1 8.9 %collective-permute-start.24 = (bf16[48,1152]{1,0:T(8,128)(2,1)S(1)}, bf16[48,1152]{1,0:T(8,128)(2,1)S(1)}, u32[]{:S(2)}, u32[]{:S(2)}) collective-permute-start(bf16[48,1152]{1,0:T(8,128)(2,1)S(1)} %get-tuple-element.44), channel_id=1, source_target_pairs={{6,0},{193,1},{0,2},{195,3},{2,4},{197,5},{4,6},{199,7},{14,8},{20... | collective-permute-start | bytes 331784 | tf_op jit(solution)/shard_map/ppermute | solution.py:41
  118.8 5.2 %collective-permute-start.25 = (bf16[48,1152]{1,0:T(8,128)(2,1)S(1)}, bf16[48,1152]{1,0:T(8,128)(2,1)S(1)}, u32[]{:S(2)}, u32[]{:S(2)}) collective-permute-start(bf16[48,1152]{1,0:T(8,128)(2,1)S(1)} %get-tuple-element.45), channel_id=1, source_target_pairs={{4,0},{129,1},{6,2},{131,3},{0,4},{133,5},{2,6},{135,7},{12,8},{13... | collective-permute-start | bytes 331784 | tf_op jit(solution)/shard_map/ppermute | solution.py:41
  118.8 5.2 %collective-permute-start.26 = (bf16[48,1152]{1,0:T(8,128)(2,1)S(1)}, bf16[48,1152]{1,0:T(8,128)(2,1)S(1)}, u32[]{:S(2)}, u32[]{:S(2)}) collective-permute-start(bf16[48,1152]{1,0:T(8,128)(2,1)S(1)} %get-tuple-element.46), channel_id=1, source_target_pairs={{2,0},{65,1},{4,2},{67,3},{6,4},{69,5},{0,6},{71,7},{10,8},{73,9},... | collective-permute-start | bytes 331784 | tf_op jit(solution)/shard_map/ppermute | solution.py:41
  124.0 10.4 %collective-permute-start.28 = (bf16[18,1152]{1,0:T(8,128)(2,1)S(1)}, bf16[18,1152]{1,0:T(8,128)(2,1)S(1)}, u32[]{:S(2)}, u32[]{:S(2)}) collective-permute-start(bf16[18,1152]{1,0:T(8,128)(2,1)S(1)} %get-tuple-element.49), channel_id=1, source_target_pairs={{40,0},{41,1},{42,2},{43,3},{44,4},{45,5},{46,6},{47,7},{48,8},{49... | collective-permute-start | bytes 124424 | tf_op jit(solution)/shard_map/ppermute | solution.py:41
  124.9 9.5 %collective-permute-start.27 = (bf16[12,1152]{1,0:T(8,128)(2,1)S(1)}, bf16[12,1152]{1,0:T(8,128)(2,1)S(1)}, u32[]{:S(2)}, u32[]{:S(2)}) collective-permute-start(bf16[12,1152]{1,0:T(8,128)(2,1)S(1)} %get-tuple-element.48), channel_id=1, source_target_pairs={{16,0},{17,1},{18,2},{19,3},{20,4},{21,5},{22,6},{23,7},{24,8},{25... | collective-permute-start | bytes 82952 | tf_op jit(solution)/shard_map/ppermute | solution.py:41
  133.5 2.5 %copy-start.1 = (bf16[256,1152]{1,0:T(8,128)(2,1)S(1)}, bf16[256,1152]{1,0:T(8,128)(2,1)}, u32[]{:S(2)}) copy-start(bf16[256,1152]{1,0:T(8,128)(2,1)} %raw_ref.3) | copy-start | bytes 1769476
  134.5 4.8 %collective-permute-start.29 = (bf16[6,1152]{1,0:T(8,128)(2,1)S(1)}, bf16[6,1152]{1,0:T(8,128)(2,1)S(1)}, u32[]{:S(2)}, u32[]{:S(2)}) collective-permute-start(bf16[6,1152]{1,0:T(8,128)(2,1)S(1)} %get-tuple-element.51), channel_id=1, source_target_pairs={{8,0},{9,1},{10,2},{11,3},{12,4},{13,5},{14,6},{15,7},{16,8},{17,9... | collective-permute-start | bytes 41480 | tf_op jit(solution)/shard_map/ppermute | solution.py:41
  134.6 4.7 %collective-permute-start.30 = (bf16[6,1152]{1,0:T(8,128)(2,1)S(1)}, bf16[6,1152]{1,0:T(8,128)(2,1)S(1)}, u32[]{:S(2)}, u32[]{:S(2)}) collective-permute-start(bf16[6,1152]{1,0:T(8,128)(2,1)S(1)} %get-tuple-element.52), channel_id=1, source_target_pairs={{56,0},{57,1},{58,2},{59,3},{60,4},{61,5},{62,6},{63,7},{0,8},{1,9... | collective-permute-start | bytes 41480 | tf_op jit(solution)/shard_map/ppermute | solution.py:41
where the time goes:
time: 140 us
  starting transfers between devices  68.1 us (49%)
  waiting for transfers between devices  43 us (31%)
  Pallas kernels  20.1 us (14%)
  local copies, waits for them, and re-layouts  5.08 us (4%)
  between operations  2.17 us (2%)
  other arithmetic  1.53 us (1%)
    ppermute x31, starting transfers between devices, fetch(): lax.ppermute(value, AXES, [(index(*where(*coords(i))), i) for i in range(...  68.1 us
    ppermute x31, waiting for transfers between devices, fetch(): lax.ppermute(value, AXES, [(index(*where(*coords(i))), i) for i in range(...  43 us
    pallas_call x10, Pallas kernels, call(): pl.pallas_call(body, out_shape=[pltpu.VMEM(s, d) for s, d in outs], in_sp...  20.1 us
  transfers between devices with their start and end apart: 31, of which 10 were waited for; matrix products, arithmetic and copies ran while one was open for 4% of the time, Pallas kernels for 11%

commit v1 on v0

--- a/solution.py
+++ b/solution.py
@@ -61,29 +61,35 @@
     return lambda y, z, x, c: coords((index(y, z, x, c) + d) % NDEV)
 
 
-def call(body, outs, *args, flops=0, scratch=(), smem=(), limit=16):
+def call(body, outs, *args, flops=0, scratch=(), smem=(), hbm=(), limit=16, final=False):
     def spec(i):
-        return pl.BlockSpec(memory_space=pltpu.SMEM if i in smem else pltpu.VMEM)
+        return pl.BlockSpec(memory_space=pltpu.SMEM if i in smem else pltpu.HBM if i in hbm else pltpu.VMEM)
 
     return pl.pallas_call(
         body,
-        out_shape=[pltpu.VMEM(s, d) for s, d in outs],
+        out_shape=[jax.ShapeDtypeStruct(s, d) if final else pltpu.VMEM(s, d) for s, d in outs],
         in_specs=[spec(i) for i in range(len(args))],
         out_specs=[pl.BlockSpec(memory_space=pltpu.VMEM) for _ in outs],
         scratch_shapes=list(scratch),
         compiler_params=pltpu.CompilerParams(vmem_limit_bytes=limit << 20),
         cost_estimate=pl.CostEstimate(flops=flops, bytes_accessed=0, transcendentals=0),
-    )(*(a if i in smem else pltpu.with_memory_space_constraint(a, pltpu.VMEM) for i, a in enumerate(args)))
-
-
-def text_body(raw_ref, low_ref, length_ref):
+    )(*(
+        a if i in smem else pltpu.with_memory_space_constraint(a, pltpu.HBM if i in hbm else pltpu.VMEM)
+        for i, a in enumerate(args)
+    ))
+
+
+def text_body(raw_ref, w_ref, low_ref, length_ref, kept_ref):
+    kept_ref[...] = w_ref[...]
     raw = raw_ref[...].astype(F32)
     length = jnp.sqrt(jnp.sum(raw * raw, axis=1, keepdims=True) + EPS)
     length_ref[...] = length
     low_ref[...] = (raw / length).astype(BF16)
 
 
-def order_body(coord_ref, x_ref, pick_ref, xp_ref, xpt_ref):
+def order_body(coord_ref, source_ref, pick_ref, xp_ref, xpt_ref, x_ref, done):
+    copy = pltpu.make_async_copy(source_ref, x_ref, done)
+    copy.start()
     y, z, x, c = (coord_ref[i] for i in range(4))
     row = lax.broadcasted_iota(jnp.int32, (SUB, 1), 0)
     within = (z + row // OWN + (NZ - 3)) % NZ * (NX * NC * OWN) + row % OWN
@@ -100,6 +106,11 @@
             base = (at_y * (NZ * NX * NC) + at_x * NC + core) * OWN
             chosen = jnp.where(lanes == within + base, 1.0, 0.0).astype(BF16)
             pick_ref[pl.ds(pl.multiple_of(i * COLS + j * SUB, 16), SUB), :] = chosen
+
+    copy.wait()
+
+    @pl.loop(0, D // COLS)
+    def _(i):
         rows = pl.ds(pl.multiple_of(i * COLS, COLS), COLS)
         xpt_ref[rows, :] = mm(pick_ref[rows, :], x_ref[...], NT).astype(BF16)
         xp_ref[:, rows] = mm(x_ref[...], pick_ref[rows, :], NT).astype(BF16)
@@ -133,7 +144,7 @@
     return (-scale * polarity * jax.nn.sigmoid(-polarity * logits)).astype(BF16)
 
 
-def image_body(scalar_ref, low_ref, unit_ref, length_ref, t0, t1, t2, t3, xpt_ref, eg_ref, gw_ref, grad, pair):
+def image_body(scalar_ref, low_ref, unit_ref, length_ref, t0, t1, t2, t3, xpt_ref, eg_ref, s0, s1, s2, s3, grad, pair):
     scale, bias = scalar_ref[0], scalar_ref[1]
     texts = (t0, t1, t2, t3)
     for k, text in enumerate(texts):
@@ -147,18 +158,23 @@
         grad[:, cols] = part
         inner = inner + jnp.sum(part * unit_ref[:, cols], axis=1, keepdims=True)
     eg_ref[...] = ((grad[...] - unit_ref[...] * inner) / length_ref[...]).astype(BF16)
-
-    @pl.loop(0, HALF // PIECE)
-    def _(i):
-        at = pl.multiple_of(i * PIECE, PIECE)
-        part = mm(xpt_ref[pl.ds(HALF + at, PIECE), :], eg_ref[...])
-        gw_ref[pl.ds(at, PIECE), :] = part.astype(BF16)
-
-
-def weight_body(xpt_ref, eg_ref, came_ref, *outs):
-    for i, out in enumerate(outs):
-        rows = pl.ds(i * PIECE, PIECE)
-        out[...] = (mm(xpt_ref[rows, :], eg_ref[...]) + came_ref[rows, :].astype(F32)).astype(BF16)
+    for i, out in enumerate((s0, s1, s2, s3)):
+        out[...] = mm(xpt_ref[pl.ds(HALF + i * PIECE, PIECE), :], eg_ref[...]).astype(BF16)
+
+
+def weight_body(xpt_ref, eg_ref, came_ref, out, *, piece):
+    rows = pl.ds(piece * PIECE, PIECE)
+    out[...] = (mm(xpt_ref[rows, :], eg_ref[...]) + came_ref[...].astype(F32)).astype(BF16)
+
+
+def join_body(*refs, rows):
+    parts = [ref[...].astype(F32)[:n] for ref, n in zip(refs[:-1], rows, strict=True)]
+    refs[-1][...] = jnp.concatenate(parts, 0).astype(BF16)
+
+
+def stack_body(*refs):
+    for i, ref in enumerate(refs[:-1]):
+        refs[-1][pl.ds(i * SUB, SUB), :] = ref[...]
 
 
 def features_body(eg_ref, w_ref, pick_ref, out_ref, mixed):
@@ -206,13 +222,17 @@
     outs[2][...] = (mid[2 * OWN :] + high[2 * OWN :]).astype(BF16)
 
 
-def gather_weight(w):
-    before, after = fetch(w, along_z(-1)), fetch(w, along_z(1))
-    near = jnp.concatenate([before, w, after], 0)
+def join(rows, *parts):
+    (out,) = call(functools.partial(join_body, rows=rows), [((sum(rows), E), BF16)], *parts, flops=10**6)
+    return out
+
+
+def gather_weight(kept, before, after):
+    near = join((OWN,) * 3, before, kept, after)
     high, low = fetch(near, along_z(3)), fetch(near, along_z(-2))
-    ring = jnp.concatenate([low[: 2 * OWN], near, high], 0)
+    ring = join((2 * OWN, 3 * OWN, 3 * OWN), low, near, high)
     plane = [fetch(ring, along_first(d)) for d in (1, 2, 3)]
-    plane = jnp.concatenate([ring] + plane, 0)
+    (plane,) = call(stack_body, [((PIECE, E), BF16)], ring, *plane, flops=10**6)
     half = [plane] + [fetch(plane, along_second(d)) for d in (1, 2, 3)]
     return half + [fetch(piece, sibling) for piece in half]
 
@@ -237,16 +257,20 @@
 def on_device(image_features, head_weight, text_embeds, natural_exponent_factor, logit_bias):
     scalars = jnp.concatenate([jnp.exp(natural_exponent_factor), logit_bias])
     place = jnp.stack([lax.axis_index(a) for a in AXES]).astype(jnp.int32)
-    weight = gather_weight(head_weight)
-    text_low, text_length = call(
-        text_body, [((R, E), BF16), ((R, 1), F32)], text_embeds, flops=10**8
-    )
-    texts = [text_low]
-    for _ in range(1, S):
-        texts.append(fetch(texts[-1], along_blocks(1)))
+    before = fetch(head_weight, along_z(-1))
+    behind = fetch(head_weight, along_z(1))
+    text_low, text_length, kept = call(
+        text_body, [((R, E), BF16), ((R, 1), F32), ((OWN, E), BF16)], text_embeds, head_weight, flops=10**8
+    )
+    weight = gather_weight(kept, before, behind)
+    text1 = fetch(text_low, along_blocks(1))
+    text2 = fetch(text_low, along_blocks(2))
+    text3 = fetch(text2, along_blocks(1))
+    texts = [text_low, text1, text2, text3]
     pick, xp, xpt = call(
         order_body, [((D, D), BF16), ((R, D), BF16), ((D, R), BF16)], place, image_features,
-        flops=4 * D * D * R, smem=(0,),
+        flops=4 * D * D * R, smem=(0,), hbm=(1,),
+        scratch=[pltpu.VMEM((R, D), BF16), pltpu.SemaphoreType.DMA(())],
     )
     full, unit, low, length = call(
         embed_body, [((D, E), BF16), ((R, E), F32), ((R, E), BF16), ((R, 1), F32)], xp, *weight,
@@ -256,20 +280,24 @@
     for _ in range(1, S):
         images.append(fetch(images[-1], along_blocks(-1)))
     work = [pltpu.VMEM((R, E), F32), pltpu.VMEM((S, R, R), BF16)]
-    eg, sent = call(
-        image_body, [((R, E), BF16), ((HALF, E), BF16)], scalars, low, unit, length, *texts, xpt,
+    eg, *sent = call(
+        image_body, [((R, E), BF16)] + [((PIECE, E), BF16)] * 4, scalars, low, unit, length, *texts, xpt,
         flops=16 * R * R * E + 2 * R * HALF * E, scratch=work, smem=(0,),
     )
-    came = fetch(sent, sibling)
+    came = [fetch(piece, sibling) for piece in sent]
     (grad_features,) = call(
         features_body, [((R, D), BF16)], eg, full, pick, flops=2 * R * D * E + 2 * R * D * D,
-        scratch=[pltpu.VMEM((R, D), BF16)],
-    )
-    pieces = call(weight_body, [((PIECE, E), BF16)] * 4, xpt, eg, came, flops=2 * R * HALF * E)
+        scratch=[pltpu.VMEM((R, D), BF16)], final=True,
+    )
+    pieces = []
+    for i in range(4):
+        pieces += call(
+            functools.partial(weight_body, piece=i), [((PIECE, E), BF16)], xpt, eg, came[i], flops=2 * R * PIECE * E
+        )
     grad_weight = scatter_weight(pieces)
     (grad_text,) = call(
         text_grad_body, [((R, E), BF16)], scalars, text_embeds, text_low, text_length, *images,
-        flops=16 * R * R * E, scratch=work, smem=(0,),
+        flops=16 * R * R * E, scratch=work, smem=(0,), final=True,
     )
     return grad_features, grad_text, grad_weight
 

time: 140 us -> 134 us (0.957)
  the two profiles are of different devices: /device:TPU:1 before, /device:TPU:0 now
where the time goes in v1:
time: 134 us
  starting transfers between devices  57.8 us (43%)
  waiting for transfers between devices  49.3 us (37%)
  Pallas kernels  21.9 us (16%)
  between operations  2.2 us (2%)
  local copies, waits for them, and re-layouts  1.79 us (1%)
    ppermute x34, starting transfers between devices, fetch(): lax.ppermute(value, AXES, [(index(*where(*coords(i))), i) for i in range(...  57.8 us
    ppermute x34, waiting for transfers between devices, fetch(): lax.ppermute(value, AXES, [(index(*where(*coords(i))), i) for i in range(...  49.3 us
    pallas_call x16, Pallas kernels, call(): pl.pallas_call(body, out_shape=[jax.ShapeDtypeStruct(s, d) if final else...  21.9 us
  transfers between devices with their start and end apart: 34, of which 9 were waited for; matrix products, arithmetic and copies ran while one was open for 1% of the time, Pallas kernels for 14%

profile of v1, /device:TPU:0, one launch (start us, length us, event | category | flops | bytes accessed | tf_op | source)
XLA Modules:
  0.0 133.8 jit_solution(1067994353697512721)
XLA Ops:
  0.6 0.3 collective-permute-start
  0.9 4.0 %collective-permute-start.1 = (bf16[6,1152]{1,0:T(8,128)(2,1)}, bf16[6,1152]{1,0:T(8,128)(2,1)S(1)}, u32[]{:S(2)}, u32[]{:S(2)}) collective-permute-start(bf16[6,1152]{1,0:T(8,128)(2,1)} %w_ref.1), channel_id=1, source_target_pairs={{8,0},{9,1},{10,2},{11,3},{12,4},{13,5},{14,6},{15,7},{16,8},{17,9... | collective-permute-start | bytes 41480 | tf_op jit(solution)/shard_map/ppermute | solution.py:41
  4.9 1.1 copy-done
  6.0 0.7 copy-done.2
  6.7 0.2 shard_map.77
  7.0 2.4 %collective-permute-start.2 = (bf16[18,1152]{1,0:T(8,128)(2,1)S(1)}, bf16[18,1152]{1,0:T(8,128)(2,1)S(1)}, u32[]{:S(2)}, u32[]{:S(2)}) collective-permute-start(bf16[18,1152]{1,0:T(8,128)(2,1)S(1)} %shard_map.78.refs_1_), channel_id=1, source_target_pairs={{48,0},{49,1},{50,2},{51,3},{52,4},{53,5},{54,6},{55,7},{56,8},{57... | collective-permute-start | bytes 124424 | tf_op jit(solution)/shard_map/ppermute | solution.py:41
  9.4 3.2 %collective-permute-start.3 = (bf16[18,1152]{1,0:T(8,128)(2,1)S(1)}, bf16[18,1152]{1,0:T(8,128)(2,1)S(1)}, u32[]{:S(2)}, u32[]{:S(2)}) collective-permute-start(bf16[18,1152]{1,0:T(8,128)(2,1)S(1)} %shard_map.78.refs_1_), channel_id=1, source_target_pairs={{24,0},{25,1},{26,2},{27,3},{28,4},{29,5},{30,6},{31,7},{32,8},{33... | collective-permute-start | bytes 124424 | tf_op jit(solution)/shard_map/ppermute | solution.py:41
  12.6 5.4 %collective-permute-start.15 = (bf16[256,1152]{1,0:T(8,128)(2,1)S(1)}, bf16[256,1152]{1,0:T(8,128)(2,1)S(1)}, u32[]{:S(2)}, u32[]{:S(2)}) collective-permute-start(bf16[256,1152]{1,0:T(8,128)(2,1)S(1)} %get-tuple-element.33.t0.low_ref), channel_id=1, source_target_pairs={{2,0},{3,1},{4,2},{5,3},{6,4},{7,5},{8,6},{9,7},{10,8},{11,9},{12,... | collective-permute-start | bytes 1769480 | tf_op jit(solution)/shard_map/ppermute | solution.py:41
  18.0 0.4 collective-permute-start.4
  18.4 0.8 collective-permute-start.5
  19.2 0.9 collective-permute-start.6
  20.1 10.8 %collective-permute-done.4.refs_1_ = bf16[48,1152]{1,0:T(8,128)(2,1)S(1)} collective-permute-done((bf16[48,1152]{1,0:T(8,128)(2,1)S(1)}, bf16[48,1152]{1,0:T(8,128)(2,1)S(1)}, u32[]{:S(2)}, u32[]{:S(2)}) %collective-permute-start.4) | collective-permute-done | bytes 110624 | tf_op jit(solution)/shard_map/ppermute | solution.py:41
  31.0 3.0 %collective-permute-start.7 = (bf16[192,1152]{1,0:T(8,128)(2,1)S(1)}, bf16[192,1152]{1,0:T(8,128)(2,1)S(1)}, u32[]{:S(2)}, u32[]{:S(2)}) collective-permute-start(bf16[192,1152]{1,0:T(8,128)(2,1)S(1)} %shard_map.80.refs_0_), channel_id=1, source_target_pairs={{64,0},{3,1},{66,2},{5,3},{68,4},{7,5},{70,6},{1,7},{72,8},{11,9},... | collective-permute-start | bytes 1327112 | tf_op jit(solution)/shard_map/ppermute | solution.py:41
  34.0 0.6 collective-permute-start.8
  34.6 1.3 collective-permute-start.9
  35.9 10.8 %collective-permute-start.14 = (bf16[256,1152]{1,0:T(8,128)(2,1)S(1)}, bf16[256,1152]{1,0:T(8,128)(2,1)}, u32[]{:S(2)}, u32[]{:S(2)}) collective-permute-start(bf16[256,1152]{1,0:T(8,128)(2,1)S(1)} %get-tuple-element.33.t0.low_ref), channel_id=1, source_target_pairs={{1,0},{2,1},{3,2},{4,3},{5,4},{6,5},{7,6},{8,7},{9,8},{10,9},{11,1... | collective-permute-start | bytes 1769480 | tf_op jit(solution)/shard_map/ppermute | solution.py:41
  46.7 4.9 %collective-permute-start.16 = (bf16[256,1152]{1,0:T(8,128)(2,1)S(1)}, bf16[256,1152]{1,0:T(8,128)(2,1)}, u32[]{:S(2)}, u32[]{:S(2)}) collective-permute-start(bf16[256,1152]{1,0:T(8,128)(2,1)S(1)} %collective-permute-done.15.t2), channel_id=1, source_target_pairs={{1,0},{2,1},{3,2},{4,3},{5,4},{6,5},{7,6},{8,7},{9,8},{10,9},{11,1... | collective-permute-start | bytes 1769480 | tf_op jit(solution)/shard_map/ppermute | solution.py:41
  53.0 0.5 collective-permute-start.12
  53.5 0.3 collective-permute-start.13
  53.9 6.2 %shard_map.76 = (bf16[1536,1536]{1,0:T(8,128)(2,1)S(1)}, bf16[256,1536]{1,0:T(8,128)(2,1)S(1)}, bf16[1536,256]{1,0:T(8,128)(2,1)S(1)}) custom-call(s32[4]{0:T(128)S(1)} %pad_add_fusion.coord_ref, bf16[256,1536]{1,0:T(8,128)(2,1)} %source_ref.1), custom_call_target="tpu_custom_call" | custom-call | flops 2415919104 | tf_op jit(solution)/shard_map/pallas_call | solution.py:68
  60.2 1.6 %shard_map.81 = (bf16[1536,1152]{1,0:T(8,128)(2,1)S(1)}, f32[256,1152]{1,0:T(8,128)S(1)}, bf16[256,1152]{1,0:T(8,128)(2,1)S(1)}, f32[256,1]{1,0:T(8,128)S(1)}) custom-call(bf16[256,1536]{1,0:T(8,128)(2,1)S(1)} %get-tuple-element.28.xp_ref, bf16[192,1152]{1,0:T(8,128)(2,1)S(1)} %shard_map.80.refs_0_, bf16[192,1152]{1,0:T(8,128)(2,1)S(1)} %collective-permute-done.7.refs_1_, ...), custom_call_target="tpu_custom_call" | custom-call | flops 905969664 | tf_op jit(solution)/shard_map/pallas_call | solution.py:68
  61.8 0.3 collective-permute-start.17
  62.2 3.8 %shard_map.82 = (bf16[256,1152]{1,0:T(8,128)(2,1)S(1)}, bf16[192,1152]{1,0:T(8,128)(2,1)S(1)}, bf16[192,1152]{1,0:T(8,128)(2,1)S(1)}, bf16[192,1152]{1,0:T(8,128)(2,1)S(1)}, bf16[192,1152]{1,0:T(8,128)(2,1)S(1)}) custom-call(f32[2]{0:T(128)S(1)} %pad_maximum_fusion.scalar_ref, bf16[256,1152]{1,0:T(8,128)(2,1)S(1)} %get-tuple-element.30.low_ref.p0, ...), custom_call_target="tpu_custom_call" | custom-call | flops 1660944384 | tf_op jit(solution)/shard_map/pallas_call | solution.py:68
  66.0 0.3 collective-permute-start.25
  66.3 0.3 collective-permute-start.23
  66.6 0.2 collective-permute-start.21
  66.8 0.3 collective-permute-start.20
  67.1 0.8 collective-permute-done.25.came_ref
  67.8 0.3 shard_map.88
  68.1 1.6 %collective-permute-start.26 = (bf16[192,1152]{1,0:T(8,128)(2,1)S(1)}, bf16[192,1152]{1,0:T(8,128)(2,1)S(1)}, u32[]{:S(2)}, u32[]{:S(2)}) collective-permute-start(bf16[192,1152]{1,0:T(8,128)(2,1)S(1)} %shard_map.88), channel_id=1, source_target_pairs={{64,0},{3,1},{66,2},{5,3},{68,4},{7,5},{70,6},{1,7},{72,8},{11,9},... | collective-permute-start | bytes 1327112 | tf_op jit(solution)/shard_map/ppermute | solution.py:41
  69.8 0.3 shard_map.87
  70.2 0.3 shard_map.86
  70.5 1.2 collective-permute-start.22
  71.6 16.1 %collective-permute-done.17.p1 = bf16[256,1152]{1,0:T(8,128)(2,1)S(1)} collective-permute-done((bf16[256,1152]{1,0:T(8,128)(2,1)S(1)}, bf16[256,1152]{1,0:T(8,128)(2,1)S(1)}, u32[]{:S(2)}, u32[]{:S(2)}) %collective-permute-start.17) | collective-permute-done | bytes 589856 | tf_op jit(solution)/shard_map/ppermute | solution.py:41
  87.8 0.3 shard_map.85.refs_0_
  88.1 2.9 %collective-permute-done.22.refs_1_ = bf16[192,1152]{1,0:T(8,128)(2,1)S(1)} collective-permute-done((bf16[192,1152]{1,0:T(8,128)(2,1)S(1)}, bf16[192,1152]{1,0:T(8,128)(2,1)S(1)}, u32[]{:S(2)}, u32[]{:S(2)}) %collective-permute-start.22) | collective-permute-done | bytes 442400 | tf_op jit(solution)/shard_map/ppermute | solution.py:41
  91.2 0.3 collective-permute-start.27
  91.6 3.1 %collective-permute-start.29 = (bf16[48,1152]{1,0:T(8,128)(2,1)S(1)}, bf16[48,1152]{1,0:T(8,128)(2,1)S(1)}, u32[]{:S(2)}, u32[]{:S(2)}) collective-permute-start(bf16[48,1152]{1,0:T(8,128)(2,1)S(1)} %get-tuple-element.46), channel_id=1, source_target_pairs={{2,0},{65,1},{4,2},{67,3},{6,4},{69,5},{0,6},{71,7},{10,8},{73,9},... | collective-permute-start | bytes 331784 | tf_op jit(solution)/shard_map/ppermute | solution.py:41
  94.8 3.9 %collective-permute-done.27.refs_1_ = bf16[48,1152]{1,0:T(8,128)(2,1)S(1)} collective-permute-done((bf16[48,1152]{1,0:T(8,128)(2,1)S(1)}, bf16[48,1152]{1,0:T(8,128)(2,1)S(1)}, u32[]{:S(2)}, u32[]{:S(2)}) %collective-permute-start.27) | collective-permute-done | bytes 110624 | tf_op jit(solution)/shard_map/ppermute | solution.py:41
  98.7 0.9 collective-permute-done.29.refs_3_
  99.8 2.2 %collective-permute-start.30 = (bf16[12,1152]{1,0:T(8,128)(2,1)S(1)}, bf16[12,1152]{1,0:T(8,128)(2,1)S(1)}, u32[]{:S(2)}, u32[]{:S(2)}) collective-permute-start(bf16[12,1152]{1,0:T(8,128)(2,1)S(1)} %get-tuple-element.48), channel_id=1, source_target_pairs={{16,0},{17,1},{18,2},{19,3},{20,4},{21,5},{22,6},{23,7},{24,8},{25... | collective-permute-start | bytes 82952 | tf_op jit(solution)/shard_map/ppermute | solution.py:41
  101.9 2.7 %collective-permute-done.30.low_ref = bf16[12,1152]{1,0:T(8,128)(2,1)S(1)} collective-permute-done((bf16[12,1152]{1,0:T(8,128)(2,1)S(1)}, bf16[12,1152]{1,0:T(8,128)(2,1)S(1)}, u32[]{:S(2)}, u32[]{:S(2)}) %collective-permute-start.30) | collective-permute-done | bytes 27680 | tf_op jit(solution)/shard_map/ppermute | solution.py:41
  104.7 2.2 %collective-permute-done.31.high_ref = bf16[18,1152]{1,0:T(8,128)(2,1)S(1)} collective-permute-done((bf16[18,1152]{1,0:T(8,128)(2,1)S(1)}, bf16[18,1152]{1,0:T(8,128)(2,1)S(1)}, u32[]{:S(2)}, u32[]{:S(2)}) %collective-permute-start.31) | collective-permute-done | bytes 41504 | tf_op jit(solution)/shard_map/ppermute | solution.py:41
  106.9 8.9 %collective-permute-start.32 = (bf16[6,1152]{1,0:T(8,128)(2,1)S(1)}, bf16[6,1152]{1,0:T(8,128)(2,1)S(1)}, u32[]{:S(2)}, u32[]{:S(2)}) collective-permute-start(bf16[6,1152]{1,0:T(8,128)(2,1)S(1)} %get-tuple-element.51), channel_id=1, source_target_pairs={{8,0},{9,1},{10,2},{11,3},{12,4},{13,5},{14,6},{15,7},{16,8},{17,9... | collective-permute-start | bytes 41480 | tf_op jit(solution)/shard_map/ppermute | solution.py:41
  115.8 5.2 %shard_map.83 = bf16[256,1536]{1,0:T(8,128)(2,1)} custom-call(bf16[256,1152]{1,0:T(8,128)(2,1)S(1)} %get-tuple-element.35.eg_ref, bf16[1536,1152]{1,0:T(8,128)(2,1)S(1)} %get-tuple-element.36.w_ref, bf16[1536,1536]{1,0:T(8,128)(2,1)S(1)} %get-tuple-element.37.pick_ref), custom_call_target="tpu_custom_call" | custom-call | flops 2113929216 | tf_op jit(solution)/shard_map/pallas_call | solution.py:68
  121.0 0.6 convert_add_fusion
  121.7 8.9 %collective-permute-done.19.p3 = bf16[256,1152]{1,0:T(8,128)(2,1)S(1)} collective-permute-done((bf16[256,1152]{1,0:T(8,128)(2,1)S(1)}, bf16[256,1152]{1,0:T(8,128)(2,1)S(1)}, u32[]{:S(2)}, u32[]{:S(2)}) %collective-permute-start.19) | collective-permute-done | bytes 589856 | tf_op jit(solution)/shard_map/ppermute | solution.py:41
  130.6 3.2 %shard_map.84 = bf16[256,1152]{1,0:T(8,128)(2,1)} custom-call(f32[2]{0:T(128)S(1)} %pad_maximum_fusion.scalar_ref, bf16[256,1152]{1,0:T(8,128)(2,1)S(1)} %copy-done.1, bf16[256,1152]{1,0:T(8,128)(2,1)S(1)} %get-tuple-element.33.t0.low_ref, f32[256,1]{1,0:T(8,128)S(1)} %get-tuple-element.38.length_ref, bf16[256,1152]{1,0:T(8,128)(2,1)S(1)} %get-tuple-element.30.low_ref.p0, ...), custom_call_target="tpu_custom_call" | custom-call | flops 1207959552 | tf_op jit(solution)/shard_map/pallas_call | solution.py:68
  (45 shorter events, 1.0 us)
Async XLA Ops:
  0.6 6.3 %collective-permute-start = (bf16[6,1152]{1,0:T(8,128)(2,1)}, bf16[6,1152]{1,0:T(8,128)(2,1)S(1)}, u32[]{:S(2)}, u32[]{:S(2)}) collective-permute-start(bf16[6,1152]{1,0:T(8,128)(2,1)} %w_ref.1), channel_id=1, source_target_pairs={{56,0},{57,1},{58,2},{59,3},{60,4},{61,5},{62,6},{63,7},{0,8},{1,9... | collective-permute-start | bytes 41480 | tf_op jit(solution)/shard_map/ppermute | solution.py:41
  0.9 6.1 %collective-permute-start.1 = (bf16[6,1152]{1,0:T(8,128)(2,1)}, bf16[6,1152]{1,0:T(8,128)(2,1)S(1)}, u32[]{:S(2)}, u32[]{:S(2)}) collective-permute-start(bf16[6,1152]{1,0:T(8,128)(2,1)} %w_ref.1), channel_id=1, source_target_pairs={{8,0},{9,1},{10,2},{11,3},{12,4},{13,5},{14,6},{15,7},{16,8},{17,9... | collective-permute-start | bytes 41480 | tf_op jit(solution)/shard_map/ppermute | solution.py:41
  4.9 1.1 copy-start
  6.0 0.7 copy-start.2
  7.0 10.9 %collective-permute-start.2 = (bf16[18,1152]{1,0:T(8,128)(2,1)S(1)}, bf16[18,1152]{1,0:T(8,128)(2,1)S(1)}, u32[]{:S(2)}, u32[]{:S(2)}) collective-permute-start(bf16[18,1152]{1,0:T(8,128)(2,1)S(1)} %shard_map.78.refs_1_), channel_id=1, source_target_pairs={{48,0},{49,1},{50,2},{51,3},{52,4},{53,5},{54,6},{55,7},{56,8},{57... | collective-permute-start | bytes 124424 | tf_op jit(solution)/shard_map/ppermute | solution.py:41
  9.4 8.6 %collective-permute-start.3 = (bf16[18,1152]{1,0:T(8,128)(2,1)S(1)}, bf16[18,1152]{1,0:T(8,128)(2,1)S(1)}, u32[]{:S(2)}, u32[]{:S(2)}) collective-permute-start(bf16[18,1152]{1,0:T(8,128)(2,1)S(1)} %shard_map.78.refs_1_), channel_id=1, source_target_pairs={{24,0},{25,1},{26,2},{27,3},{28,4},{29,5},{30,6},{31,7},{32,8},{33... | collective-permute-start | bytes 124424 | tf_op jit(solution)/shard_map/ppermute | solution.py:41
  12.6 23.3 %collective-permute-start.15 = (bf16[256,1152]{1,0:T(8,128)(2,1)S(1)}, bf16[256,1152]{1,0:T(8,128)(2,1)S(1)}, u32[]{:S(2)}, u32[]{:S(2)}) collective-permute-start(bf16[256,1152]{1,0:T(8,128)(2,1)S(1)} %get-tuple-element.33.t0.low_ref), channel_id=1, source_target_pairs={{2,0},{3,1},{4,2},{5,3},{6,4},{7,5},{8,6},{9,7},{10,8},{11,9},{12,... | collective-permute-start | bytes 1769480 | tf_op jit(solution)/shard_map/ppermute | solution.py:41
  18.0 12.9 %collective-permute-start.4 = (bf16[48,1152]{1,0:T(8,128)(2,1)S(1)}, bf16[48,1152]{1,0:T(8,128)(2,1)S(1)}, u32[]{:S(2)}, u32[]{:S(2)}) collective-permute-start(bf16[48,1152]{1,0:T(8,128)(2,1)S(1)} %shard_map.79.refs_0_), channel_id=1, source_target_pairs={{2,0},{65,1},{4,2},{67,3},{6,4},{69,5},{0,6},{71,7},{10,8},{73,9},... | collective-permute-start | bytes 331784 | tf_op jit(solution)/shard_map/ppermute | solution.py:41
  18.4 12.6 %collective-permute-start.5 = (bf16[48,1152]{1,0:T(8,128)(2,1)S(1)}, bf16[48,1152]{1,0:T(8,128)(2,1)S(1)}, u32[]{:S(2)}, u32[]{:S(2)}) collective-permute-start(bf16[48,1152]{1,0:T(8,128)(2,1)S(1)} %shard_map.79.refs_0_), channel_id=1, source_target_pairs={{4,0},{129,1},{6,2},{131,3},{0,4},{133,5},{2,6},{135,7},{12,8},{13... | collective-permute-start | bytes 331784 | tf_op jit(solution)/shard_map/ppermute | solution.py:41
  19.2 11.8 %collective-permute-start.6 = (bf16[48,1152]{1,0:T(8,128)(2,1)S(1)}, bf16[48,1152]{1,0:T(8,128)(2,1)S(1)}, u32[]{:S(2)}, u32[]{:S(2)}) collective-permute-start(bf16[48,1152]{1,0:T(8,128)(2,1)S(1)} %shard_map.79.refs_0_), channel_id=1, source_target_pairs={{6,0},{193,1},{0,2},{195,3},{2,4},{197,5},{4,6},{199,7},{14,8},{20... | collective-permute-start | bytes 331784 | tf_op jit(solution)/shard_map/ppermute | solution.py:41
  31.0 15.7 %collective-permute-start.7 = (bf16[192,1152]{1,0:T(8,128)(2,1)S(1)}, bf16[192,1152]{1,0:T(8,128)(2,1)S(1)}, u32[]{:S(2)}, u32[]{:S(2)}) collective-permute-start(bf16[192,1152]{1,0:T(8,128)(2,1)S(1)} %shard_map.80.refs_0_), channel_id=1, source_target_pairs={{64,0},{3,1},{66,2},{5,3},{68,4},{7,5},{70,6},{1,7},{72,8},{11,9},... | collective-permute-start | bytes 1327112 | tf_op jit(solution)/shard_map/ppermute | solution.py:41
  34.0 18.9 %collective-permute-start.8 = (bf16[192,1152]{1,0:T(8,128)(2,1)S(1)}, bf16[192,1152]{1,0:T(8,128)(2,1)S(1)}, u32[]{:S(2)}, u32[]{:S(2)}) collective-permute-start(bf16[192,1152]{1,0:T(8,128)(2,1)S(1)} %shard_map.80.refs_0_), channel_id=1, source_target_pairs={{128,0},{5,1},{130,2},{7,3},{132,4},{1,5},{134,6},{3,7},{136,8},{1... | collective-permute-start | bytes 1327112 | tf_op jit(solution)/shard_map/ppermute | solution.py:41
  34.6 18.4 %collective-permute-start.9 = (bf16[192,1152]{1,0:T(8,128)(2,1)S(1)}, bf16[192,1152]{1,0:T(8,128)(2,1)S(1)}, u32[]{:S(2)}, u32[]{:S(2)}) collective-permute-start(bf16[192,1152]{1,0:T(8,128)(2,1)S(1)} %shard_map.80.refs_0_), channel_id=1, source_target_pairs={{192,0},{7,1},{194,2},{1,3},{196,4},{3,5},{198,6},{5,7},{200,8},{1... | collective-permute-start | bytes 1327112 | tf_op jit(solution)/shard_map/ppermute | solution.py:41
  35.9 17.6 %collective-permute-start.10 = (bf16[192,1152]{1,0:T(8,128)(2,1)S(1)}, bf16[192,1152]{1,0:T(8,128)(2,1)S(1)}, u32[]{:S(2)}, u32[]{:S(2)}) collective-permute-start(bf16[192,1152]{1,0:T(8,128)(2,1)S(1)} %shard_map.80.refs_0_), channel_id=1, source_target_pairs={{1,0},{0,1},{3,2},{2,3},{5,4},{4,5},{7,6},{6,7},{9,8},{8,9},{11,10... | collective-permute-start | bytes 1327112 | tf_op jit(solution)/shard_map/ppermute | solution.py:41
  35.9 26.2 %collective-permute-start.14 = (bf16[256,1152]{1,0:T(8,128)(2,1)S(1)}, bf16[256,1152]{1,0:T(8,128)(2,1)}, u32[]{:S(2)}, u32[]{:S(2)}) collective-permute-start(bf16[256,1152]{1,0:T(8,128)(2,1)S(1)} %get-tuple-element.33.t0.low_ref), channel_id=1, source_target_pairs={{1,0},{2,1},{3,2},{4,3},{5,4},{6,5},{7,6},{8,7},{9,8},{10,9},{11,1... | collective-permute-start | bytes 1769480 | tf_op jit(solution)/shard_map/ppermute | solution.py:41
  46.7 15.5 %collective-permute-start.16 = (bf16[256,1152]{1,0:T(8,128)(2,1)S(1)}, bf16[256,1152]{1,0:T(8,128)(2,1)}, u32[]{:S(2)}, u32[]{:S(2)}) collective-permute-start(bf16[256,1152]{1,0:T(8,128)(2,1)S(1)} %collective-permute-done.15.t2), channel_id=1, source_target_pairs={{1,0},{2,1},{3,2},{4,3},{5,4},{6,5},{7,6},{8,7},{9,8},{10,9},{11,1... | collective-permute-start | bytes 1769480 | tf_op jit(solution)/shard_map/ppermute | solution.py:41
  52.9 7.3 %collective-permute-start.11 = (bf16[192,1152]{1,0:T(8,128)(2,1)S(1)}, bf16[192,1152]{1,0:T(8,128)(2,1)S(1)}, u32[]{:S(2)}, u32[]{:S(2)}) collective-permute-start(bf16[192,1152]{1,0:T(8,128)(2,1)S(1)} %collective-permute-done.7.refs_1_), channel_id=1, source_target_pairs={{1,0},{0,1},{3,2},{2,3},{5,4},{4,5},{7,6},{6,7},{9,8},{8,9},{11,10... | collective-permute-start | bytes 1327112 | tf_op jit(solution)/shard_map/ppermute | solution.py:41
  53.0 7.2 %collective-permute-start.12 = (bf16[192,1152]{1,0:T(8,128)(2,1)S(1)}, bf16[192,1152]{1,0:T(8,128)(2,1)S(1)}, u32[]{:S(2)}, u32[]{:S(2)}) collective-permute-start(bf16[192,1152]{1,0:T(8,128)(2,1)S(1)} %collective-permute-done.8.refs_2_), channel_id=1, source_target_pairs={{1,0},{0,1},{3,2},{2,3},{5,4},{4,5},{7,6},{6,7},{9,8},{8,9},{11,10... | collective-permute-start | bytes 1327112 | tf_op jit(solution)/shard_map/ppermute | solution.py:41
  53.5 6.7 %collective-permute-start.13 = (bf16[192,1152]{1,0:T(8,128)(2,1)S(1)}, bf16[192,1152]{1,0:T(8,128)(2,1)S(1)}, u32[]{:S(2)}, u32[]{:S(2)}) collective-permute-start(bf16[192,1152]{1,0:T(8,128)(2,1)S(1)} %collective-permute-done.9.refs_3_), channel_id=1, source_target_pairs={{1,0},{0,1},{3,2},{2,3},{5,4},{4,5},{7,6},{6,7},{9,8},{8,9},{11,10... | collective-permute-start | bytes 1327112 | tf_op jit(solution)/shard_map/ppermute | solution.py:41
  61.8 25.9 %collective-permute-start.17 = (bf16[256,1152]{1,0:T(8,128)(2,1)S(1)}, bf16[256,1152]{1,0:T(8,128)(2,1)S(1)}, u32[]{:S(2)}, u32[]{:S(2)}) collective-permute-start(bf16[256,1152]{1,0:T(8,128)(2,1)S(1)} %get-tuple-element.30.low_ref.p0), channel_id=1, source_target_pairs={{255,0},{0,1},{1,2},{2,3},{3,4},{4,5},{5,6},{6,7},{7,8},{8,9},{9,1... | collective-permute-start | bytes 1769480 | tf_op jit(solution)/shard_map/ppermute | solution.py:41
  66.0 1.9 %collective-permute-start.25 = (bf16[192,1152]{1,0:T(8,128)(2,1)S(1)}, bf16[192,1152]{1,0:T(8,128)(2,1)S(1)}, u32[]{:S(2)}, u32[]{:S(2)}) collective-permute-start(bf16[192,1152]{1,0:T(8,128)(2,1)S(1)} %get-tuple-element.42), channel_id=1, source_target_pairs={{1,0},{0,1},{3,2},{2,3},{5,4},{4,5},{7,6},{6,7},{9,8},{8,9},{11,10... | collective-permute-start | bytes 1327112 | tf_op jit(solution)/shard_map/ppermute | solution.py:41
  66.3 3.5 %collective-permute-start.23 = (bf16[192,1152]{1,0:T(8,128)(2,1)S(1)}, bf16[192,1152]{1,0:T(8,128)(2,1)S(1)}, u32[]{:S(2)}, u32[]{:S(2)}) collective-permute-start(bf16[192,1152]{1,0:T(8,128)(2,1)S(1)} %get-tuple-element.41), channel_id=1, source_target_pairs={{1,0},{0,1},{3,2},{2,3},{5,4},{4,5},{7,6},{6,7},{9,8},{8,9},{11,10... | collective-permute-start | bytes 1327112 | tf_op jit(solution)/shard_map/ppermute | solution.py:41
  66.6 3.6 %collective-permute-start.21 = (bf16[192,1152]{1,0:T(8,128)(2,1)S(1)}, bf16[192,1152]{1,0:T(8,128)(2,1)S(1)}, u32[]{:S(2)}, u32[]{:S(2)}) collective-permute-start(bf16[192,1152]{1,0:T(8,128)(2,1)S(1)} %get-tuple-element.40), channel_id=1, source_target_pairs={{1,0},{0,1},{3,2},{2,3},{5,4},{4,5},{7,6},{6,7},{9,8},{8,9},{11,10... | collective-permute-start | bytes 1327112 | tf_op jit(solution)/shard_map/ppermute | solution.py:41
  66.8 21.0 %collective-permute-start.20 = (bf16[192,1152]{1,0:T(8,128)(2,1)S(1)}, bf16[192,1152]{1,0:T(8,128)(2,1)S(1)}, u32[]{:S(2)}, u32[]{:S(2)}) collective-permute-start(bf16[192,1152]{1,0:T(8,128)(2,1)S(1)} %get-tuple-element.39), channel_id=1, source_target_pairs={{1,0},{0,1},{3,2},{2,3},{5,4},{4,5},{7,6},{6,7},{9,8},{8,9},{11,10... | collective-permute-start | bytes 1327112 | tf_op jit(solution)/shard_map/ppermute | solution.py:41
  68.1 19.9 %collective-permute-start.26 = (bf16[192,1152]{1,0:T(8,128)(2,1)S(1)}, bf16[192,1152]{1,0:T(8,128)(2,1)S(1)}, u32[]{:S(2)}, u32[]{:S(2)}) collective-permute-start(bf16[192,1152]{1,0:T(8,128)(2,1)S(1)} %shard_map.88), channel_id=1, source_target_pairs={{64,0},{3,1},{66,2},{5,3},{68,4},{7,5},{70,6},{1,7},{72,8},{11,9},... | collective-permute-start | bytes 1327112 | tf_op jit(solution)/shard_map/ppermute | solution.py:41
  70.1 18.0 %collective-permute-start.24 = (bf16[192,1152]{1,0:T(8,128)(2,1)S(1)}, bf16[192,1152]{1,0:T(8,128)(2,1)S(1)}, u32[]{:S(2)}, u32[]{:S(2)}) collective-permute-start(bf16[192,1152]{1,0:T(8,128)(2,1)S(1)} %shard_map.87), channel_id=1, source_target_pairs={{128,0},{5,1},{130,2},{7,3},{132,4},{1,5},{134,6},{3,7},{136,8},{1... | collective-permute-start | bytes 1327112 | tf_op jit(solution)/shard_map/ppermute | solution.py:41
  70.5 20.5 %collective-permute-start.22 = (bf16[192,1152]{1,0:T(8,128)(2,1)S(1)}, bf16[192,1152]{1,0:T(8,128)(2,1)S(1)}, u32[]{:S(2)}, u32[]{:S(2)}) collective-permute-start(bf16[192,1152]{1,0:T(8,128)(2,1)S(1)} %shard_map.86), channel_id=1, source_target_pairs={{192,0},{7,1},{194,2},{1,3},{196,4},{3,5},{198,6},{5,7},{200,8},{1... | collective-permute-start | bytes 1327112 | tf_op jit(solution)/shard_map/ppermute | solution.py:41
  87.8 28.1 %collective-permute-start.18 = (bf16[256,1152]{1,0:T(8,128)(2,1)S(1)}, bf16[256,1152]{1,0:T(8,128)(2,1)S(1)}, u32[]{:S(2)}, u32[]{:S(2)}) collective-permute-start(bf16[256,1152]{1,0:T(8,128)(2,1)S(1)} %collective-permute-done.17.p1), channel_id=1, source_target_pairs={{255,0},{0,1},{1,2},{2,3},{3,4},{4,5},{5,6},{6,7},{7,8},{8,9},{9,1... | collective-permute-start | bytes 1769480 | tf_op jit(solution)/shard_map/ppermute | solution.py:41
  91.2 7.4 %collective-permute-start.27 = (bf16[48,1152]{1,0:T(8,128)(2,1)S(1)}, bf16[48,1152]{1,0:T(8,128)(2,1)S(1)}, u32[]{:S(2)}, u32[]{:S(2)}) collective-permute-start(bf16[48,1152]{1,0:T(8,128)(2,1)S(1)} %get-tuple-element.44), channel_id=1, source_target_pairs={{6,0},{193,1},{0,2},{195,3},{2,4},{197,5},{4,6},{199,7},{14,8},{20... | collective-permute-start | bytes 331784 | tf_op jit(solution)/shard_map/ppermute | solution.py:41
  91.5 7.1 %collective-permute-start.28 = (bf16[48,1152]{1,0:T(8,128)(2,1)S(1)}, bf16[48,1152]{1,0:T(8,128)(2,1)S(1)}, u32[]{:S(2)}, u32[]{:S(2)}) collective-permute-start(bf16[48,1152]{1,0:T(8,128)(2,1)S(1)} %get-tuple-element.45), channel_id=1, source_target_pairs={{4,0},{129,1},{6,2},{131,3},{0,4},{133,5},{2,6},{135,7},{12,8},{13... | collective-permute-start | bytes 331784 | tf_op jit(solution)/shard_map/ppermute | solution.py:41
  91.6 7.9 %collective-permute-start.29 = (bf16[48,1152]{1,0:T(8,128)(2,1)S(1)}, bf16[48,1152]{1,0:T(8,128)(2,1)S(1)}, u32[]{:S(2)}, u32[]{:S(2)}) collective-permute-start(bf16[48,1152]{1,0:T(8,128)(2,1)S(1)} %get-tuple-element.46), channel_id=1, source_target_pairs={{2,0},{65,1},{4,2},{67,3},{6,4},{69,5},{0,6},{71,7},{10,8},{73,9},... | collective-permute-start | bytes 331784 | tf_op jit(solution)/shard_map/ppermute | solution.py:41
  99.6 7.2 %collective-permute-start.31 = (bf16[18,1152]{1,0:T(8,128)(2,1)S(1)}, bf16[18,1152]{1,0:T(8,128)(2,1)S(1)}, u32[]{:S(2)}, u32[]{:S(2)}) collective-permute-start(bf16[18,1152]{1,0:T(8,128)(2,1)S(1)} %get-tuple-element.49), channel_id=1, source_target_pairs={{40,0},{41,1},{42,2},{43,3},{44,4},{45,5},{46,6},{47,7},{48,8},{49... | collective-permute-start | bytes 124424 | tf_op jit(solution)/shard_map/ppermute | solution.py:41
  99.8 4.9 %collective-permute-start.30 = (bf16[12,1152]{1,0:T(8,128)(2,1)S(1)}, bf16[12,1152]{1,0:T(8,128)(2,1)S(1)}, u32[]{:S(2)}, u32[]{:S(2)}) collective-permute-start(bf16[12,1152]{1,0:T(8,128)(2,1)S(1)} %get-tuple-element.48), channel_id=1, source_target_pairs={{16,0},{17,1},{18,2},{19,3},{20,4},{21,5},{22,6},{23,7},{24,8},{25... | collective-permute-start | bytes 82952 | tf_op jit(solution)/shard_map/ppermute | solution.py:41
  106.9 14.1 %collective-permute-start.32 = (bf16[6,1152]{1,0:T(8,128)(2,1)S(1)}, bf16[6,1152]{1,0:T(8,128)(2,1)S(1)}, u32[]{:S(2)}, u32[]{:S(2)}) collective-permute-start(bf16[6,1152]{1,0:T(8,128)(2,1)S(1)} %get-tuple-element.51), channel_id=1, source_target_pairs={{8,0},{9,1},{10,2},{11,3},{12,4},{13,5},{14,6},{15,7},{16,8},{17,9... | collective-permute-start | bytes 41480 | tf_op jit(solution)/shard_map/ppermute | solution.py:41
  115.8 5.2 %collective-permute-start.33 = (bf16[6,1152]{1,0:T(8,128)(2,1)S(1)}, bf16[6,1152]{1,0:T(8,128)(2,1)S(1)}, u32[]{:S(2)}, u32[]{:S(2)}) collective-permute-start(bf16[6,1152]{1,0:T(8,128)(2,1)S(1)} %get-tuple-element.52), channel_id=1, source_target_pairs={{56,0},{57,1},{58,2},{59,3},{60,4},{61,5},{62,6},{63,7},{0,8},{1,9... | collective-permute-start | bytes 41480 | tf_op jit(solution)/shard_map/ppermute | solution.py:41
  115.8 14.7 %collective-permute-start.19 = (bf16[256,1152]{1,0:T(8,128)(2,1)S(1)}, bf16[256,1152]{1,0:T(8,128)(2,1)S(1)}, u32[]{:S(2)}, u32[]{:S(2)}) collective-permute-start(bf16[256,1152]{1,0:T(8,128)(2,1)S(1)} %collective-permute-done.18.p2), channel_id=1, source_target_pairs={{255,0},{0,1},{1,2},{2,3},{3,4},{4,5},{5,6},{6,7},{7,8},{8,9},{9,1... | collective-permute-start | bytes 1769480 | tf_op jit(solution)/shard_map/ppermute | solution.py:41
  115.8 14.7 %copy-start.1 = (bf16[256,1152]{1,0:T(8,128)(2,1)S(1)}, bf16[256,1152]{1,0:T(8,128)(2,1)}, u32[]{:S(2)}) copy-start(bf16[256,1152]{1,0:T(8,128)(2,1)} %raw_ref.3) | copy-start | bytes 1769476

commit v2 on v1

--- a/solution.py
+++ b/solution.py
@@ -57,8 +57,23 @@
     return y, z, x, 1 - c
 
 
-def along_blocks(d):
-    return lambda y, z, x, c: coords((index(y, z, x, c) + d) % NDEV)
+def send(value, step, parity):
+    return lax.ppermute(value, AXES, [(i, (i + step) % NDEV) for i in range(parity, NDEV, 2)])
+
+
+def window(own, step):
+    inner, outer = (1, 0) if step < 0 else (0, 1)
+
+    def near(value):
+        return send(value, step, inner)
+
+    def far(value):
+        return send(value, step, outer)
+
+    a1, b1 = near(own), far(own)
+    b2, a2 = far(a1), near(b1)
+    b3, a3 = far(a2), near(b2)
+    return a1, a2, a3, b1, b2, b3
 
 
 def call(body, outs, *args, flops=0, scratch=(), smem=(), hbm=(), limit=16, final=False):
@@ -144,17 +159,33 @@
     return (-scale * polarity * jax.nn.sigmoid(-polarity * logits)).astype(BF16)
 
 
-def image_body(scalar_ref, low_ref, unit_ref, length_ref, t0, t1, t2, t3, xpt_ref, eg_ref, s0, s1, s2, s3, grad, pair):
+def collect(all_ref, refs, near):
+    all_ref[pl.ds(0, R), :] = refs[0][...]
+
+    @pl.when(near)
+    def _():
+        for k in range(1, S):
+            all_ref[pl.ds(k * R, R), :] = refs[k][...]
+
+    @pl.when(jnp.logical_not(near))
+    def _():
+        for k in range(1, S):
+            all_ref[pl.ds(k * R, R), :] = refs[k + S - 1][...]
+
+
+def image_body(
+    scalar_ref, coord_ref, low_ref, unit_ref, length_ref, *refs
+):
+    text_refs, (xpt_ref, eg_ref, s0, s1, s2, s3, grad, pair, texts) = refs[:7], refs[7:]
     scale, bias = scalar_ref[0], scalar_ref[1]
-    texts = (t0, t1, t2, t3)
-    for k, text in enumerate(texts):
-        pair[k] = derivative(low_ref[...], text[...], scale, bias, k == 0)
+    collect(texts, text_refs, coord_ref[3] == 0)
+    for k in range(S):
+        rows = pl.ds(k * R, R)
+        pair[:, rows] = derivative(low_ref[...], texts[rows, :], scale, bias, k == 0)
     inner = jnp.zeros((R, 1), F32)
     for at in range(0, E, COLS):
         cols = pl.ds(at, COLS)
-        part = mm(pair[0], t0[:, cols])
-        for k in range(1, S):
-            part = part + mm(pair[k], texts[k][:, cols])
+        part = mm(pair[...], texts[:, cols])
         grad[:, cols] = part
         inner = inner + jnp.sum(part * unit_ref[:, cols], axis=1, keepdims=True)
     eg_ref[...] = ((grad[...] - unit_ref[...] * inner) / length_ref[...]).astype(BF16)
@@ -189,18 +220,18 @@
         out_ref[:, cols] = mm(mixed[...], pick_ref[:, cols]).astype(BF16)
 
 
-def text_grad_body(scalar_ref, raw_ref, low_ref, length_ref, p0, p1, p2, p3, out_ref, grad, pair):
+def text_grad_body(scalar_ref, coord_ref, raw_ref, low_ref, length_ref, *refs):
+    image_refs, (out_ref, grad, pair, images) = refs[:7], refs[7:]
     scale, bias = scalar_ref[0], scalar_ref[1]
-    images = (p0, p1, p2, p3)
-    for k, image in enumerate(images):
-        pair[k] = derivative(low_ref[...], image[...], scale, bias, k == 0)
+    collect(images, image_refs, coord_ref[3] == 1)
+    for k in range(S):
+        rows = pl.ds(k * R, R)
+        pair[:, rows] = derivative(low_ref[...], images[rows, :], scale, bias, k == 0)
     length = length_ref[...]
     inner = jnp.zeros((R, 1), F32)
     for at in range(0, E, COLS):
         cols = pl.ds(at, COLS)
-        part = mm(pair[0], p0[:, cols])
-        for k in range(1, S):
-            part = part + mm(pair[k], images[k][:, cols])
+        part = mm(pair[...], images[:, cols])
         grad[:, cols] = part
         inner = inner + jnp.sum(part * (raw_ref[:, cols].astype(F32) / length), axis=1, keepdims=True)
     out_ref[...] = ((grad[...] - raw_ref[...].astype(F32) / length * inner) / length).astype(BF16)
@@ -263,10 +294,7 @@
         text_body, [((R, E), BF16), ((R, 1), F32), ((OWN, E), BF16)], text_embeds, head_weight, flops=10**8
     )
     weight = gather_weight(kept, before, behind)
-    text1 = fetch(text_low, along_blocks(1))
-    text2 = fetch(text_low, along_blocks(2))
-    text3 = fetch(text2, along_blocks(1))
-    texts = [text_low, text1, text2, text3]
+    texts = (text_low, *window(text_low, -1))
     pick, xp, xpt = call(
         order_body, [((D, D), BF16), ((R, D), BF16), ((D, R), BF16)], place, image_features,
         flops=4 * D * D * R, smem=(0,), hbm=(1,),
@@ -276,13 +304,11 @@
         embed_body, [((D, E), BF16), ((R, E), F32), ((R, E), BF16), ((R, 1), F32)], xp, *weight,
         flops=2 * R * D * E,
     )
-    images = [low]
-    for _ in range(1, S):
-        images.append(fetch(images[-1], along_blocks(-1)))
-    work = [pltpu.VMEM((R, E), F32), pltpu.VMEM((S, R, R), BF16)]
+    images = (low, *window(low, 1))
+    work = [pltpu.VMEM((R, E), F32), pltpu.VMEM((R, S * R), BF16), pltpu.VMEM((S * R, E), BF16)]
     eg, *sent = call(
-        image_body, [((R, E), BF16)] + [((PIECE, E), BF16)] * 4, scalars, low, unit, length, *texts, xpt,
-        flops=16 * R * R * E + 2 * R * HALF * E, scratch=work, smem=(0,),
+        image_body, [((R, E), BF16)] + [((PIECE, E), BF16)] * 4, scalars, place, low, unit, length, *texts, xpt,
+        flops=16 * R * R * E + 2 * R * HALF * E, scratch=work, smem=(0, 1),
     )
     came = [fetch(piece, sibling) for piece in sent]
     (grad_features,) = call(
@@ -296,8 +322,8 @@
         )
     grad_weight = scatter_weight(pieces)
     (grad_text,) = call(
-        text_grad_body, [((R, E), BF16)], scalars, text_embeds, text_low, text_length, *images,
-        flops=16 * R * R * E, scratch=work, smem=(0,), final=True,
+        text_grad_body, [((R, E), BF16)], scalars, place, text_embeds, text_low, text_length, *images,
+        flops=16 * R * R * E, scratch=work, smem=(0, 1), final=True,
     )
     return grad_features, grad_text, grad_weight
 

time: 134 us -> 146 us (1.090)
  starting transfers between devices: 57.8 us -> 63.9 us
  waiting for transfers between devices: 49.3 us -> 52.8 us
  Pallas kernels: 21.9 us -> 23.4 us
    ppermute x0 -> x12, starting transfers between devices: none -> 40.7 us  [send(): lax.ppermute(value, AXES, [(i, (i + step) % NDEV) for i in range(parity,...]
    ppermute x34 -> x28, starting transfers between devices: 57.8 us -> 23.2 us  [fetch(): lax.ppermute(value, AXES, [(index(*where(*coords(i))), i) for i in range(...]
    ppermute x0 -> x12, waiting for transfers between devices: none -> 24 us  [send(): lax.ppermute(value, AXES, [(i, (i + step) % NDEV) for i in range(parity,...]
    ppermute x34 -> x28, waiting for transfers between devices: 49.3 us -> 28.8 us  [fetch(): lax.ppermute(value, AXES, [(index(*where(*coords(i))), i) for i in range(...]
    pallas_call x16, Pallas kernels: 21.9 us -> 23.4 us  [call(): pl.pallas_call(body, out_shape=[jax.ShapeDtypeStruct(s, d) if final else...]
  transfers between devices with their start and end apart: 34 -> 40, of which waited for: 9 -> 17; matrix products, arithmetic and copies ran while one was open for 1% -> 1% of each run, Pallas kernels for 14% -> 11%
where the time goes in v2:
time: 146 us; the launch traced here: 145 us
  starting transfers between devices  63.9 us (44%)
  waiting for transfers between devices  52.8 us (36%)
  Pallas kernels  23.4 us (16%)
  between operations  2.38 us (2%)
  local copies, waits for them, and re-layouts  1.79 us (1%)
    ppermute x12, starting transfers between devices, send(): lax.ppermute(value, AXES, [(i, (i + step) % NDEV) for i in range(parity,...  40.7 us
    ppermute x28, waiting for transfers between devices, fetch(): lax.ppermute(value, AXES, [(index(*where(*coords(i))), i) for i in range(...  28.8 us
    ppermute x12, waiting for transfers between devices, send(): lax.ppermute(value, AXES, [(i, (i + step) % NDEV) for i in range(parity,...  24 us
    pallas_call x16, Pallas kernels, call(): pl.pallas_call(body, out_shape=[jax.ShapeDtypeStruct(s, d) if final else...  23.4 us
    ppermute x28, starting transfers between devices, fetch(): lax.ppermute(value, AXES, [(index(*where(*coords(i))), i) for i in range(...  23.2 us
  transfers between devices with their start and end apart: 40, of which 17 were waited for; matrix products, arithmetic and copies ran while one was open for 1% of the time, Pallas kernels for 11%

profile of v2, /device:TPU:0, one launch (start us, length us, event | category | flops | bytes accessed | tf_op | source)
XLA Modules:
  0.0 145.1 jit_solution(13305388776592646830)
XLA Ops:
  0.6 1.1 copy-done
  1.7 0.7 copy-done.4
  2.7 1.3 collective-permute-start.14
  4.0 11.5 %collective-permute-start.15 = (bf16[256,1152]{1,0:T(8,128)(2,1)S(1)}, bf16[256,1152]{1,0:T(8,128)(2,1)S(1)}, u32[]{:S(2)}, u32[]{:S(2)}) collective-permute-start(bf16[256,1152]{1,0:T(8,128)(2,1)S(1)} %get-tuple-element.33.refs_0_.low_ref), channel_id=1, source_target_pairs={{0,255},{2,1},{4,3},{6,5},{8,7},{10,9},{12,11},{14,13},{16,15},{18... | collective-permute-start | bytes 1769480 | tf_op jit(solution)/shard_map/ppermute | solution.py:61
  15.6 3.2 %collective-permute-start.1 = (bf16[6,1152]{1,0:T(8,128)(2,1)S(1)}, bf16[6,1152]{1,0:T(8,128)(2,1)S(1)}, u32[]{:S(2)}, u32[]{:S(2)}) collective-permute-start(bf16[6,1152]{1,0:T(8,128)(2,1)S(1)} %copy-done.4), channel_id=1, source_target_pairs={{8,0},{9,1},{10,2},{11,3},{12,4},{13,5},{14,6},{15,7},{16,8},{17,9... | collective-permute-start | bytes 41480 | tf_op jit(solution)/shard_map/ppermute | solution.py:41
  18.8 1.7 %collective-permute-done.refs_0_ = bf16[6,1152]{1,0:T(8,128)(2,1)S(1)} collective-permute-done((bf16[6,1152]{1,0:T(8,128)(2,1)S(1)}, bf16[6,1152]{1,0:T(8,128)(2,1)S(1)}, u32[]{:S(2)}, u32[]{:S(2)}) %collective-permute-start) | collective-permute-done | bytes 13856 | tf_op jit(solution)/shard_map/ppermute | solution.py:41
  20.5 4.3 %collective-permute-done.1.refs_2_ = bf16[6,1152]{1,0:T(8,128)(2,1)S(1)} collective-permute-done((bf16[6,1152]{1,0:T(8,128)(2,1)S(1)}, bf16[6,1152]{1,0:T(8,128)(2,1)S(1)}, u32[]{:S(2)}, u32[]{:S(2)}) %collective-permute-start.1) | collective-permute-done | bytes 13856 | tf_op jit(solution)/shard_map/ppermute | solution.py:41
  24.9 6.0 %collective-permute-start.3 = (bf16[18,1152]{1,0:T(8,128)(2,1)S(1)}, bf16[18,1152]{1,0:T(8,128)(2,1)S(1)}, u32[]{:S(2)}, u32[]{:S(2)}) collective-permute-start(bf16[18,1152]{1,0:T(8,128)(2,1)S(1)} %shard_map.78.refs_1_), channel_id=1, source_target_pairs={{24,0},{25,1},{26,2},{27,3},{28,4},{29,5},{30,6},{31,7},{32,8},{33... | collective-permute-start | bytes 124424 | tf_op jit(solution)/shard_map/ppermute | solution.py:41
  31.2 1.6 %collective-permute-done.3.refs_2_ = bf16[18,1152]{1,0:T(8,128)(2,1)S(1)} collective-permute-done((bf16[18,1152]{1,0:T(8,128)(2,1)S(1)}, bf16[18,1152]{1,0:T(8,128)(2,1)S(1)}, u32[]{:S(2)}, u32[]{:S(2)}) %collective-permute-start.3) | collective-permute-done | bytes 41504 | tf_op jit(solution)/shard_map/ppermute | solution.py:41
  33.0 1.9 %collective-permute-start.6 = (bf16[48,1152]{1,0:T(8,128)(2,1)S(1)}, bf16[48,1152]{1,0:T(8,128)(2,1)S(1)}, u32[]{:S(2)}, u32[]{:S(2)}) collective-permute-start(bf16[48,1152]{1,0:T(8,128)(2,1)S(1)} %shard_map.79.refs_0_), channel_id=1, source_target_pairs={{6,0},{193,1},{0,2},{195,3},{2,4},{197,5},{4,6},{199,7},{14,8},{20... | collective-permute-start | bytes 331784 | tf_op jit(solution)/shard_map/ppermute | solution.py:41
  34.9 2.7 %collective-permute-done.4.refs_1_ = bf16[48,1152]{1,0:T(8,128)(2,1)S(1)} collective-permute-done((bf16[48,1152]{1,0:T(8,128)(2,1)S(1)}, bf16[48,1152]{1,0:T(8,128)(2,1)S(1)}, u32[]{:S(2)}, u32[]{:S(2)}) %collective-permute-start.4) | collective-permute-done | bytes 110624 | tf_op jit(solution)/shard_map/ppermute | solution.py:41
  37.7 1.6 %collective-permute-done.5.refs_2_ = bf16[48,1152]{1,0:T(8,128)(2,1)S(1)} collective-permute-done((bf16[48,1152]{1,0:T(8,128)(2,1)S(1)}, bf16[48,1152]{1,0:T(8,128)(2,1)S(1)}, u32[]{:S(2)}, u32[]{:S(2)}) %collective-permute-start.5) | collective-permute-done | bytes 110624 | tf_op jit(solution)/shard_map/ppermute | solution.py:41
  39.3 1.2 collective-permute-done.6.refs_3_
  40.5 0.8 collective-permute-start.7
  41.3 1.3 collective-permute-start.17
  42.7 1.3 collective-permute-start.16
  44.0 0.4 collective-permute-start.8
  44.4 1.0 collective-permute-start.9
  45.4 3.5 %collective-permute-done.7.refs_1_ = bf16[192,1152]{1,0:T(8,128)(2,1)S(1)} collective-permute-done((bf16[192,1152]{1,0:T(8,128)(2,1)S(1)}, bf16[192,1152]{1,0:T(8,128)(2,1)S(1)}, u32[]{:S(2)}, u32[]{:S(2)}) %collective-permute-start.7) | collective-permute-done | bytes 442400 | tf_op jit(solution)/shard_map/ppermute | solution.py:41
  48.9 1.1 collective-permute-done.17.refs_5_
  50.0 1.3 collective-permute-start.18
  51.3 15.3 %collective-permute-start.19 = (bf16[256,1152]{1,0:T(8,128)(2,1)S(1)}, bf16[256,1152]{1,0:T(8,128)(2,1)}, u32[]{:S(2)}, u32[]{:S(2)}) collective-permute-start(bf16[256,1152]{1,0:T(8,128)(2,1)S(1)} %collective-permute-done.16.refs_2_), channel_id=1, source_target_pairs={{0,255},{2,1},{4,3},{6,5},{8,7},{10,9},{12,11},{14,13},{16,15},{18... | collective-permute-start | bytes 1769480 | tf_op jit(solution)/shard_map/ppermute | solution.py:61
  68.1 0.5 collective-permute-start.12
  69.0 6.2 %shard_map.76 = (bf16[1536,1536]{1,0:T(8,128)(2,1)S(1)}, bf16[256,1536]{1,0:T(8,128)(2,1)S(1)}, bf16[1536,256]{1,0:T(8,128)(2,1)S(1)}) custom-call(s32[4]{0:T(128)S(1)} %pad_add_fusion.coord_ref, bf16[256,1536]{1,0:T(8,128)(2,1)} %source_ref.1), custom_call_target="tpu_custom_call" | custom-call | flops 2415919104 | tf_op jit(solution)/shard_map/pallas_call | solution.py:83
  75.3 2.8 %shard_map.81 = (bf16[1536,1152]{1,0:T(8,128)(2,1)S(1)}, f32[256,1152]{1,0:T(8,128)S(1)}, bf16[256,1152]{1,0:T(8,128)(2,1)S(1)}, f32[256,1]{1,0:T(8,128)S(1)}) custom-call(bf16[256,1536]{1,0:T(8,128)(2,1)S(1)} %get-tuple-element.28.xp_ref, bf16[192,1152]{1,0:T(8,128)(2,1)S(1)} %shard_map.80.refs_0_, bf16[192,1152]{1,0:T(8,128)(2,1)S(1)} %copy-done.3, ...), custom_call_target="tpu_custom_call" | custom-call | flops 905969664 | tf_op jit(solution)/shard_map/pallas_call | solution.py:83
  78.2 3.9 %shard_map.82 = (bf16[256,1152]{1,0:T(8,128)(2,1)S(1)}, bf16[192,1152]{1,0:T(8,128)(2,1)S(1)}, bf16[192,1152]{1,0:T(8,128)(2,1)S(1)}, bf16[192,1152]{1,0:T(8,128)(2,1)S(1)}, bf16[192,1152]{1,0:T(8,128)(2,1)S(1)}) custom-call(f32[2]{0:T(128)S(1)} %pad_maximum_fusion.scalar_ref, s32[4]{0:T(128)S(1)} %pad_add_fusion.coord_ref, ...), custom_call_target="tpu_custom_call" | custom-call | flops 1660944384 | tf_op jit(solution)/shard_map/pallas_call | solution.py:83
  82.4 2.2 %collective-permute-start.20 = (bf16[256,1152]{1,0:T(8,128)(2,1)S(1)}, bf16[256,1152]{1,0:T(8,128)(2,1)S(1)}, u32[]{:S(2)}, u32[]{:S(2)}) collective-permute-start(bf16[256,1152]{1,0:T(8,128)(2,1)S(1)} %get-tuple-element.30.low_ref.refs_0_), channel_id=1, source_target_pairs={{0,1},{2,3},{4,5},{6,7},{8,9},{10,11},{12,13},{14,15},{16,17},{18,... | collective-permute-start | bytes 1769480 | tf_op jit(solution)/shard_map/ppermute | solution.py:61
  84.6 1.3 collective-permute-start.21
  86.0 0.5 collective-permute-start.27
  86.9 0.9 collective-permute-done.29.came_ref
  88.1 0.3 collective-permute-done.27.came_ref
  88.5 1.9 %collective-permute-start.30 = (bf16[192,1152]{1,0:T(8,128)(2,1)S(1)}, bf16[192,1152]{1,0:T(8,128)(2,1)S(1)}, u32[]{:S(2)}, u32[]{:S(2)}) collective-permute-start(bf16[192,1152]{1,0:T(8,128)(2,1)S(1)} %shard_map.87), channel_id=1, source_target_pairs={{128,0},{5,1},{130,2},{7,3},{132,4},{1,5},{134,6},{3,7},{136,8},{1... | collective-permute-start | bytes 1327112 | tf_op jit(solution)/shard_map/ppermute | solution.py:41
  90.8 14.8 %collective-permute-done.21.refs_4_ = bf16[256,1152]{1,0:T(8,128)(2,1)S(1)} collective-permute-done((bf16[256,1152]{1,0:T(8,128)(2,1)S(1)}, bf16[256,1152]{1,0:T(8,128)(2,1)S(1)}, u32[]{:S(2)}, u32[]{:S(2)}) %collective-permute-start.21) | collective-permute-done | bytes 589856 | tf_op jit(solution)/shard_map/ppermute | solution.py:61
  105.6 1.3 collective-permute-start.23
  106.9 1.3 collective-permute-start.22
  108.6 1.5 %collective-permute-done.28.refs_1_ = bf16[192,1152]{1,0:T(8,128)(2,1)S(1)} collective-permute-done((bf16[192,1152]{1,0:T(8,128)(2,1)S(1)}, bf16[192,1152]{1,0:T(8,128)(2,1)S(1)}, u32[]{:S(2)}, u32[]{:S(2)}) %collective-permute-start.28) | collective-permute-done | bytes 442400 | tf_op jit(solution)/shard_map/ppermute | solution.py:41
  110.7 2.9 %collective-permute-start.35 = (bf16[48,1152]{1,0:T(8,128)(2,1)S(1)}, bf16[48,1152]{1,0:T(8,128)(2,1)S(1)}, u32[]{:S(2)}, u32[]{:S(2)}) collective-permute-start(bf16[48,1152]{1,0:T(8,128)(2,1)S(1)} %get-tuple-element.46), channel_id=1, source_target_pairs={{2,0},{65,1},{4,2},{67,3},{6,4},{69,5},{0,6},{71,7},{10,8},{73,9},... | collective-permute-start | bytes 331784 | tf_op jit(solution)/shard_map/ppermute | solution.py:41
  113.6 7.0 %collective-permute-done.33.refs_1_ = bf16[48,1152]{1,0:T(8,128)(2,1)S(1)} collective-permute-done((bf16[48,1152]{1,0:T(8,128)(2,1)S(1)}, bf16[48,1152]{1,0:T(8,128)(2,1)S(1)}, u32[]{:S(2)}, u32[]{:S(2)}) %collective-permute-start.33) | collective-permute-done | bytes 110624 | tf_op jit(solution)/shard_map/ppermute | solution.py:41
  120.8 2.7 %collective-permute-done.23.refs_5_ = bf16[256,1152]{1,0:T(8,128)(2,1)S(1)} collective-permute-done((bf16[256,1152]{1,0:T(8,128)(2,1)S(1)}, bf16[256,1152]{1,0:T(8,128)(2,1)S(1)}, u32[]{:S(2)}, u32[]{:S(2)}) %collective-permute-start.23) | collective-permute-done | bytes 589856 | tf_op jit(solution)/shard_map/ppermute | solution.py:61
  123.5 1.3 collective-permute-start.24
  124.8 1.3 collective-permute-start.25
  126.2 2.2 %collective-permute-done.37.high_ref = bf16[18,1152]{1,0:T(8,128)(2,1)S(1)} collective-permute-done((bf16[18,1152]{1,0:T(8,128)(2,1)S(1)}, bf16[18,1152]{1,0:T(8,128)(2,1)S(1)}, u32[]{:S(2)}, u32[]{:S(2)}) %collective-permute-start.37) | collective-permute-done | bytes 41504 | tf_op jit(solution)/shard_map/ppermute | solution.py:41
  128.4 1.3 collective-permute-start.38
  129.7 0.8 collective-permute-start.39
  130.5 5.2 %shard_map.83 = bf16[256,1536]{1,0:T(8,128)(2,1)} custom-call(bf16[256,1152]{1,0:T(8,128)(2,1)S(1)} %get-tuple-element.35.eg_ref, bf16[1536,1152]{1,0:T(8,128)(2,1)S(1)} %get-tuple-element.36.w_ref, bf16[1536,1536]{1,0:T(8,128)(2,1)S(1)} %get-tuple-element.37.pick_ref), custom_call_target="tpu_custom_call" | custom-call | flops 2113929216 | tf_op jit(solution)/shard_map/pallas_call | solution.py:83
  135.7 0.6 convert_add_fusion
  136.3 5.3 %collective-permute-done.25.refs_6_ = bf16[256,1152]{1,0:T(8,128)(2,1)S(1)} collective-permute-done((bf16[256,1152]{1,0:T(8,128)(2,1)S(1)}, bf16[256,1152]{1,0:T(8,128)(2,1)S(1)}, u32[]{:S(2)}, u32[]{:S(2)}) %collective-permute-start.25) | collective-permute-done | bytes 589856 | tf_op jit(solution)/shard_map/ppermute | solution.py:61
  141.7 3.4 %shard_map.84 = bf16[256,1152]{1,0:T(8,128)(2,1)} custom-call(f32[2]{0:T(128)S(1)} %pad_maximum_fusion.scalar_ref, s32[4]{0:T(128)S(1)} %pad_add_fusion.coord_ref, bf16[256,1152]{1,0:T(8,128)(2,1)S(1)} %copy-done.1, bf16[256,1152]{1,0:T(8,128)(2,1)S(1)} %get-tuple-element.33.refs_0_.low_ref, f32[256,1]{1,0:T(8,128)S(1)} %get-tuple-element.38.length_ref, ...), custom_call_target="tpu_custom_call" | custom-call | flops 1207959552 | tf_op jit(solution)/shard_map/pallas_call | solution.py:83
  (61 shorter events, 4.2 us)
Async XLA Ops:
  0.6 1.1 copy-start
  1.7 0.7 copy-start.4
  2.7 38.7 %collective-permute-start.14 = (bf16[256,1152]{1,0:T(8,128)(2,1)S(1)}, bf16[256,1152]{1,0:T(8,128)(2,1)S(1)}, u32[]{:S(2)}, u32[]{:S(2)}) collective-permute-start(bf16[256,1152]{1,0:T(8,128)(2,1)S(1)} %get-tuple-element.33.refs_0_.low_ref), channel_id=1, source_target_pairs={{1,0},{3,2},{5,4},{7,6},{9,8},{11,10},{13,12},{15,14},{17,16},{19,... | collective-permute-start | bytes 1769480 | tf_op jit(solution)/shard_map/ppermute | solution.py:61
  4.0 38.7 %collective-permute-start.15 = (bf16[256,1152]{1,0:T(8,128)(2,1)S(1)}, bf16[256,1152]{1,0:T(8,128)(2,1)S(1)}, u32[]{:S(2)}, u32[]{:S(2)}) collective-permute-start(bf16[256,1152]{1,0:T(8,128)(2,1)S(1)} %get-tuple-element.33.refs_0_.low_ref), channel_id=1, source_target_pairs={{0,255},{2,1},{4,3},{6,5},{8,7},{10,9},{12,11},{14,13},{16,15},{18... | collective-permute-start | bytes 1769480 | tf_op jit(solution)/shard_map/ppermute | solution.py:61
  15.5 5.0 %collective-permute-start = (bf16[6,1152]{1,0:T(8,128)(2,1)S(1)}, bf16[6,1152]{1,0:T(8,128)(2,1)S(1)}, u32[]{:S(2)}, u32[]{:S(2)}) collective-permute-start(bf16[6,1152]{1,0:T(8,128)(2,1)S(1)} %copy-done.4), channel_id=1, source_target_pairs={{56,0},{57,1},{58,2},{59,3},{60,4},{61,5},{62,6},{63,7},{0,8},{1,9... | collective-permute-start | bytes 41480 | tf_op jit(solution)/shard_map/ppermute | solution.py:41
  15.6 9.2 %collective-permute-start.1 = (bf16[6,1152]{1,0:T(8,128)(2,1)S(1)}, bf16[6,1152]{1,0:T(8,128)(2,1)S(1)}, u32[]{:S(2)}, u32[]{:S(2)}) collective-permute-start(bf16[6,1152]{1,0:T(8,128)(2,1)S(1)} %copy-done.4), channel_id=1, source_target_pairs={{8,0},{9,1},{10,2},{11,3},{12,4},{13,5},{14,6},{15,7},{16,8},{17,9... | collective-permute-start | bytes 41480 | tf_op jit(solution)/shard_map/ppermute | solution.py:41
  24.8 6.4 %collective-permute-start.2 = (bf16[18,1152]{1,0:T(8,128)(2,1)S(1)}, bf16[18,1152]{1,0:T(8,128)(2,1)S(1)}, u32[]{:S(2)}, u32[]{:S(2)}) collective-permute-start(bf16[18,1152]{1,0:T(8,128)(2,1)S(1)} %shard_map.78.refs_1_), channel_id=1, source_target_pairs={{48,0},{49,1},{50,2},{51,3},{52,4},{53,5},{54,6},{55,7},{56,8},{57... | collective-permute-start | bytes 124424 | tf_op jit(solution)/shard_map/ppermute | solution.py:41
  24.9 7.9 %collective-permute-start.3 = (bf16[18,1152]{1,0:T(8,128)(2,1)S(1)}, bf16[18,1152]{1,0:T(8,128)(2,1)S(1)}, u32[]{:S(2)}, u32[]{:S(2)}) collective-permute-start(bf16[18,1152]{1,0:T(8,128)(2,1)S(1)} %shard_map.78.refs_1_), channel_id=1, source_target_pairs={{24,0},{25,1},{26,2},{27,3},{28,4},{29,5},{30,6},{31,7},{32,8},{33... | collective-permute-start | bytes 124424 | tf_op jit(solution)/shard_map/ppermute | solution.py:41
  32.8 4.8 %collective-permute-start.4 = (bf16[48,1152]{1,0:T(8,128)(2,1)S(1)}, bf16[48,1152]{1,0:T(8,128)(2,1)S(1)}, u32[]{:S(2)}, u32[]{:S(2)}) collective-permute-start(bf16[48,1152]{1,0:T(8,128)(2,1)S(1)} %shard_map.79.refs_0_), channel_id=1, source_target_pairs={{2,0},{65,1},{4,2},{67,3},{6,4},{69,5},{0,6},{71,7},{10,8},{73,9},... | collective-permute-start | bytes 331784 | tf_op jit(solution)/shard_map/ppermute | solution.py:41
  32.9 6.4 %collective-permute-start.5 = (bf16[48,1152]{1,0:T(8,128)(2,1)S(1)}, bf16[48,1152]{1,0:T(8,128)(2,1)S(1)}, u32[]{:S(2)}, u32[]{:S(2)}) collective-permute-start(bf16[48,1152]{1,0:T(8,128)(2,1)S(1)} %shard_map.79.refs_0_), channel_id=1, source_target_pairs={{4,0},{129,1},{6,2},{131,3},{0,4},{133,5},{2,6},{135,7},{12,8},{13... | collective-permute-start | bytes 331784 | tf_op jit(solution)/shard_map/ppermute | solution.py:41
  33.0 7.4 %collective-permute-start.6 = (bf16[48,1152]{1,0:T(8,128)(2,1)S(1)}, bf16[48,1152]{1,0:T(8,128)(2,1)S(1)}, u32[]{:S(2)}, u32[]{:S(2)}) collective-permute-start(bf16[48,1152]{1,0:T(8,128)(2,1)S(1)} %shard_map.79.refs_0_), channel_id=1, source_target_pairs={{6,0},{193,1},{0,2},{195,3},{2,4},{197,5},{4,6},{199,7},{14,8},{20... | collective-permute-start | bytes 331784 | tf_op jit(solution)/shard_map/ppermute | solution.py:41
  40.5 8.4 %collective-permute-start.7 = (bf16[192,1152]{1,0:T(8,128)(2,1)S(1)}, bf16[192,1152]{1,0:T(8,128)(2,1)S(1)}, u32[]{:S(2)}, u32[]{:S(2)}) collective-permute-start(bf16[192,1152]{1,0:T(8,128)(2,1)S(1)} %shard_map.80.refs_0_), channel_id=1, source_target_pairs={{64,0},{3,1},{66,2},{5,3},{68,4},{7,5},{70,6},{1,7},{72,8},{11,9},... | collective-permute-start | bytes 1327112 | tf_op jit(solution)/shard_map/ppermute | solution.py:41
  41.3 8.7 %collective-permute-start.17 = (bf16[256,1152]{1,0:T(8,128)(2,1)S(1)}, bf16[256,1152]{1,0:T(8,128)(2,1)S(1)}, u32[]{:S(2)}, u32[]{:S(2)}) collective-permute-start(bf16[256,1152]{1,0:T(8,128)(2,1)S(1)} %collective-permute-done.14.refs_1_), channel_id=1, source_target_pairs={{0,255},{2,1},{4,3},{6,5},{8,7},{10,9},{12,11},{14,13},{16,15},{18... | collective-permute-start | bytes 1769480 | tf_op jit(solution)/shard_map/ppermute | solution.py:61
  42.7 8.6 %collective-permute-start.16 = (bf16[256,1152]{1,0:T(8,128)(2,1)S(1)}, bf16[256,1152]{1,0:T(8,128)(2,1)S(1)}, u32[]{:S(2)}, u32[]{:S(2)}) collective-permute-start(bf16[256,1152]{1,0:T(8,128)(2,1)S(1)} %collective-permute-done.15.refs_4_), channel_id=1, source_target_pairs={{1,0},{3,2},{5,4},{7,6},{9,8},{11,10},{13,12},{15,14},{17,16},{19,... | collective-permute-start | bytes 1769480 | tf_op jit(solution)/shard_map/ppermute | solution.py:61
  44.0 24.0 %collective-permute-start.8 = (bf16[192,1152]{1,0:T(8,128)(2,1)S(1)}, bf16[192,1152]{1,0:T(8,128)(2,1)}, u32[]{:S(2)}, u32[]{:S(2)}) collective-permute-start(bf16[192,1152]{1,0:T(8,128)(2,1)S(1)} %shard_map.80.refs_0_), channel_id=1, source_target_pairs={{128,0},{5,1},{130,2},{7,3},{132,4},{1,5},{134,6},{3,7},{136,8},{1... | collective-permute-start | bytes 1327112 | tf_op jit(solution)/shard_map/ppermute | solution.py:41
  44.4 23.7 %collective-permute-start.9 = (bf16[192,1152]{1,0:T(8,128)(2,1)S(1)}, bf16[192,1152]{1,0:T(8,128)(2,1)}, u32[]{:S(2)}, u32[]{:S(2)}) collective-permute-start(bf16[192,1152]{1,0:T(8,128)(2,1)S(1)} %shard_map.80.refs_0_), channel_id=1, source_target_pairs={{192,0},{7,1},{194,2},{1,3},{196,4},{3,5},{198,6},{5,7},{200,8},{1... | collective-permute-start | bytes 1327112 | tf_op jit(solution)/shard_map/ppermute | solution.py:41
  48.9 2.4 %copy-start.2 = (bf16[192,1152]{1,0:T(8,128)(2,1)}, bf16[192,1152]{1,0:T(8,128)(2,1)S(1)}, u32[]{:S(2)}) copy-start(bf16[192,1152]{1,0:T(8,128)(2,1)S(1)} %collective-permute-done.7.refs_1_) | copy-start | bytes 1327108
  48.9 19.7 %collective-permute-start.10 = (bf16[192,1152]{1,0:T(8,128)(2,1)S(1)}, bf16[192,1152]{1,0:T(8,128)(2,1)}, u32[]{:S(2)}, u32[]{:S(2)}) collective-permute-start(bf16[192,1152]{1,0:T(8,128)(2,1)S(1)} %shard_map.80.refs_0_), channel_id=1, source_target_pairs={{1,0},{0,1},{3,2},{2,3},{5,4},{4,5},{7,6},{6,7},{9,8},{8,9},{11,10... | collective-permute-start | bytes 1327112 | tf_op jit(solution)/shard_map/ppermute | solution.py:41
  50.0 28.1 %collective-permute-start.18 = (bf16[256,1152]{1,0:T(8,128)(2,1)S(1)}, bf16[256,1152]{1,0:T(8,128)(2,1)}, u32[]{:S(2)}, u32[]{:S(2)}) collective-permute-start(bf16[256,1152]{1,0:T(8,128)(2,1)S(1)} %collective-permute-done.17.refs_5_), channel_id=1, source_target_pairs={{1,0},{3,2},{5,4},{7,6},{9,8},{11,10},{13,12},{15,14},{17,16},{19,... | collective-permute-start | bytes 1769480 | tf_op jit(solution)/shard_map/ppermute | solution.py:61
  51.3 26.8 %collective-permute-start.19 = (bf16[256,1152]{1,0:T(8,128)(2,1)S(1)}, bf16[256,1152]{1,0:T(8,128)(2,1)}, u32[]{:S(2)}, u32[]{:S(2)}) collective-permute-start(bf16[256,1152]{1,0:T(8,128)(2,1)S(1)} %collective-permute-done.16.refs_2_), channel_id=1, source_target_pairs={{0,255},{2,1},{4,3},{6,5},{8,7},{10,9},{12,11},{14,13},{16,15},{18... | collective-permute-start | bytes 1769480 | tf_op jit(solution)/shard_map/ppermute | solution.py:61
  68.0 7.3 %collective-permute-start.11 = (bf16[192,1152]{1,0:T(8,128)(2,1)}, bf16[192,1152]{1,0:T(8,128)(2,1)S(1)}, u32[]{:S(2)}, u32[]{:S(2)}) collective-permute-start(bf16[192,1152]{1,0:T(8,128)(2,1)} %copy-done.2), channel_id=1, source_target_pairs={{1,0},{0,1},{3,2},{2,3},{5,4},{4,5},{7,6},{6,7},{9,8},{8,9},{11,10... | collective-permute-start | bytes 1327112 | tf_op jit(solution)/shard_map/ppermute | solution.py:41
  68.1 7.2 %collective-permute-start.12 = (bf16[192,1152]{1,0:T(8,128)(2,1)}, bf16[192,1152]{1,0:T(8,128)(2,1)S(1)}, u32[]{:S(2)}, u32[]{:S(2)}) collective-permute-start(bf16[192,1152]{1,0:T(8,128)(2,1)} %collective-permute-done.8.refs_2_), channel_id=1, source_target_pairs={{1,0},{0,1},{3,2},{2,3},{5,4},{4,5},{7,6},{6,7},{9,8},{8,9},{11,10... | collective-permute-start | bytes 1327112 | tf_op jit(solution)/shard_map/ppermute | solution.py:41
  68.6 6.7 %collective-permute-start.13 = (bf16[192,1152]{1,0:T(8,128)(2,1)}, bf16[192,1152]{1,0:T(8,128)(2,1)S(1)}, u32[]{:S(2)}, u32[]{:S(2)}) collective-permute-start(bf16[192,1152]{1,0:T(8,128)(2,1)} %collective-permute-done.9.refs_3_), channel_id=1, source_target_pairs={{1,0},{0,1},{3,2},{2,3},{5,4},{4,5},{7,6},{6,7},{9,8},{8,9},{11,10... | collective-permute-start | bytes 1327112 | tf_op jit(solution)/shard_map/ppermute | solution.py:41
  69.0 6.3 %copy-start.3 = (bf16[192,1152]{1,0:T(8,128)(2,1)S(1)}, bf16[192,1152]{1,0:T(8,128)(2,1)}, u32[]{:S(2)}) copy-start(bf16[192,1152]{1,0:T(8,128)(2,1)} %copy-done.2) | copy-start | bytes 1327108
  82.1 4.4 %collective-permute-start.31 = (bf16[192,1152]{1,0:T(8,128)(2,1)S(1)}, bf16[192,1152]{1,0:T(8,128)(2,1)S(1)}, u32[]{:S(2)}, u32[]{:S(2)}) collective-permute-start(bf16[192,1152]{1,0:T(8,128)(2,1)S(1)} %get-tuple-element.42), channel_id=1, source_target_pairs={{1,0},{0,1},{3,2},{2,3},{5,4},{4,5},{7,6},{6,7},{9,8},{8,9},{11,10... | collective-permute-start | bytes 1327112 | tf_op jit(solution)/shard_map/ppermute | solution.py:41
  82.4 8.2 %collective-permute-start.20 = (bf16[256,1152]{1,0:T(8,128)(2,1)S(1)}, bf16[256,1152]{1,0:T(8,128)(2,1)S(1)}, u32[]{:S(2)}, u32[]{:S(2)}) collective-permute-start(bf16[256,1152]{1,0:T(8,128)(2,1)S(1)} %get-tuple-element.30.low_ref.refs_0_), channel_id=1, source_target_pairs={{0,1},{2,3},{4,5},{6,7},{8,9},{10,11},{12,13},{14,15},{16,17},{18,... | collective-permute-start | bytes 1769480 | tf_op jit(solution)/shard_map/ppermute | solution.py:61
  84.6 21.0 %collective-permute-start.21 = (bf16[256,1152]{1,0:T(8,128)(2,1)S(1)}, bf16[256,1152]{1,0:T(8,128)(2,1)S(1)}, u32[]{:S(2)}, u32[]{:S(2)}) collective-permute-start(bf16[256,1152]{1,0:T(8,128)(2,1)S(1)} %get-tuple-element.30.low_ref.refs_0_), channel_id=1, source_target_pairs={{1,2},{3,4},{5,6},{7,8},{9,10},{11,12},{13,14},{15,16},{17,18},{19... | collective-permute-start | bytes 1769480 | tf_op jit(solution)/shard_map/ppermute | solution.py:61
  85.9 1.9 %collective-permute-start.29 = (bf16[192,1152]{1,0:T(8,128)(2,1)S(1)}, bf16[192,1152]{1,0:T(8,128)(2,1)S(1)}, u32[]{:S(2)}, u32[]{:S(2)}) collective-permute-start(bf16[192,1152]{1,0:T(8,128)(2,1)S(1)} %get-tuple-element.41), channel_id=1, source_target_pairs={{1,0},{0,1},{3,2},{2,3},{5,4},{4,5},{7,6},{6,7},{9,8},{8,9},{11,10... | collective-permute-start | bytes 1327112 | tf_op jit(solution)/shard_map/ppermute | solution.py:41
  86.0 2.4 %collective-permute-start.27 = (bf16[192,1152]{1,0:T(8,128)(2,1)S(1)}, bf16[192,1152]{1,0:T(8,128)(2,1)S(1)}, u32[]{:S(2)}, u32[]{:S(2)}) collective-permute-start(bf16[192,1152]{1,0:T(8,128)(2,1)S(1)} %get-tuple-element.40), channel_id=1, source_target_pairs={{1,0},{0,1},{3,2},{2,3},{5,4},{4,5},{7,6},{6,7},{9,8},{8,9},{11,10... | collective-permute-start | bytes 1327112 | tf_op jit(solution)/shard_map/ppermute | solution.py:41
  86.5 20.3 %collective-permute-start.26 = (bf16[192,1152]{1,0:T(8,128)(2,1)S(1)}, bf16[192,1152]{1,0:T(8,128)(2,1)S(1)}, u32[]{:S(2)}, u32[]{:S(2)}) collective-permute-start(bf16[192,1152]{1,0:T(8,128)(2,1)S(1)} %get-tuple-element.39), channel_id=1, source_target_pairs={{1,0},{0,1},{3,2},{2,3},{5,4},{4,5},{7,6},{6,7},{9,8},{8,9},{11,10... | collective-permute-start | bytes 1327112 | tf_op jit(solution)/shard_map/ppermute | solution.py:41
  87.8 20.7 %collective-permute-start.32 = (bf16[192,1152]{1,0:T(8,128)(2,1)S(1)}, bf16[192,1152]{1,0:T(8,128)(2,1)S(1)}, u32[]{:S(2)}, u32[]{:S(2)}) collective-permute-start(bf16[192,1152]{1,0:T(8,128)(2,1)S(1)} %shard_map.88), channel_id=1, source_target_pairs={{64,0},{3,1},{66,2},{5,3},{68,4},{7,5},{70,6},{1,7},{72,8},{11,9},... | collective-permute-start | bytes 1327112 | tf_op jit(solution)/shard_map/ppermute | solution.py:41
  88.5 20.1 %collective-permute-start.30 = (bf16[192,1152]{1,0:T(8,128)(2,1)S(1)}, bf16[192,1152]{1,0:T(8,128)(2,1)S(1)}, u32[]{:S(2)}, u32[]{:S(2)}) collective-permute-start(bf16[192,1152]{1,0:T(8,128)(2,1)S(1)} %shard_map.87), channel_id=1, source_target_pairs={{128,0},{5,1},{130,2},{7,3},{132,4},{1,5},{134,6},{3,7},{136,8},{1... | collective-permute-start | bytes 1327112 | tf_op jit(solution)/shard_map/ppermute | solution.py:41
  90.7 19.4 %collective-permute-start.28 = (bf16[192,1152]{1,0:T(8,128)(2,1)S(1)}, bf16[192,1152]{1,0:T(8,128)(2,1)S(1)}, u32[]{:S(2)}, u32[]{:S(2)}) collective-permute-start(bf16[192,1152]{1,0:T(8,128)(2,1)S(1)} %shard_map.86), channel_id=1, source_target_pairs={{192,0},{7,1},{194,2},{1,3},{196,4},{3,5},{198,6},{5,7},{200,8},{1... | collective-permute-start | bytes 1327112 | tf_op jit(solution)/shard_map/ppermute | solution.py:41
  105.6 17.9 %collective-permute-start.23 = (bf16[256,1152]{1,0:T(8,128)(2,1)S(1)}, bf16[256,1152]{1,0:T(8,128)(2,1)S(1)}, u32[]{:S(2)}, u32[]{:S(2)}) collective-permute-start(bf16[256,1152]{1,0:T(8,128)(2,1)S(1)} %collective-permute-done.20.refs_1_), channel_id=1, source_target_pairs={{1,2},{3,4},{5,6},{7,8},{9,10},{11,12},{13,14},{15,16},{17,18},{19... | collective-permute-start | bytes 1769480 | tf_op jit(solution)/shard_map/ppermute | solution.py:61
  106.9 17.9 %collective-permute-start.22 = (bf16[256,1152]{1,0:T(8,128)(2,1)S(1)}, bf16[256,1152]{1,0:T(8,128)(2,1)S(1)}, u32[]{:S(2)}, u32[]{:S(2)}) collective-permute-start(bf16[256,1152]{1,0:T(8,128)(2,1)S(1)} %collective-permute-done.21.refs_4_), channel_id=1, source_target_pairs={{0,1},{2,3},{4,5},{6,7},{8,9},{10,11},{12,13},{14,15},{16,17},{18,... | collective-permute-start | bytes 1769480 | tf_op jit(solution)/shard_map/ppermute | solution.py:61
  110.3 10.3 %collective-permute-start.33 = (bf16[48,1152]{1,0:T(8,128)(2,1)S(1)}, bf16[48,1152]{1,0:T(8,128)(2,1)S(1)}, u32[]{:S(2)}, u32[]{:S(2)}) collective-permute-start(bf16[48,1152]{1,0:T(8,128)(2,1)S(1)} %get-tuple-element.44), channel_id=1, source_target_pairs={{6,0},{193,1},{0,2},{195,3},{2,4},{197,5},{4,6},{199,7},{14,8},{20... | collective-permute-start | bytes 331784 | tf_op jit(solution)/shard_map/ppermute | solution.py:41
  110.4 10.2 %collective-permute-start.34 = (bf16[48,1152]{1,0:T(8,128)(2,1)S(1)}, bf16[48,1152]{1,0:T(8,128)(2,1)S(1)}, u32[]{:S(2)}, u32[]{:S(2)}) collective-permute-start(bf16[48,1152]{1,0:T(8,128)(2,1)S(1)} %get-tuple-element.45), channel_id=1, source_target_pairs={{4,0},{129,1},{6,2},{131,3},{0,4},{133,5},{2,6},{135,7},{12,8},{13... | collective-permute-start | bytes 331784 | tf_op jit(solution)/shard_map/ppermute | solution.py:41
  110.7 9.9 %collective-permute-start.35 = (bf16[48,1152]{1,0:T(8,128)(2,1)S(1)}, bf16[48,1152]{1,0:T(8,128)(2,1)S(1)}, u32[]{:S(2)}, u32[]{:S(2)}) collective-permute-start(bf16[48,1152]{1,0:T(8,128)(2,1)S(1)} %get-tuple-element.46), channel_id=1, source_target_pairs={{2,0},{65,1},{4,2},{67,3},{6,4},{69,5},{0,6},{71,7},{10,8},{73,9},... | collective-permute-start | bytes 331784 | tf_op jit(solution)/shard_map/ppermute | solution.py:41
  120.7 7.7 %collective-permute-start.37 = (bf16[18,1152]{1,0:T(8,128)(2,1)S(1)}, bf16[18,1152]{1,0:T(8,128)(2,1)S(1)}, u32[]{:S(2)}, u32[]{:S(2)}) collective-permute-start(bf16[18,1152]{1,0:T(8,128)(2,1)S(1)} %get-tuple-element.49), channel_id=1, source_target_pairs={{40,0},{41,1},{42,2},{43,3},{44,4},{45,5},{46,6},{47,7},{48,8},{49... | collective-permute-start | bytes 124424 | tf_op jit(solution)/shard_map/ppermute | solution.py:41
  120.8 5.4 %collective-permute-start.36 = (bf16[12,1152]{1,0:T(8,128)(2,1)S(1)}, bf16[12,1152]{1,0:T(8,128)(2,1)S(1)}, u32[]{:S(2)}, u32[]{:S(2)}) collective-permute-start(bf16[12,1152]{1,0:T(8,128)(2,1)S(1)} %get-tuple-element.48), channel_id=1, source_target_pairs={{16,0},{17,1},{18,2},{19,3},{20,4},{21,5},{22,6},{23,7},{24,8},{25... | collective-permute-start | bytes 82952 | tf_op jit(solution)/shard_map/ppermute | solution.py:41
  123.5 12.8 %collective-permute-start.24 = (bf16[256,1152]{1,0:T(8,128)(2,1)S(1)}, bf16[256,1152]{1,0:T(8,128)(2,1)S(1)}, u32[]{:S(2)}, u32[]{:S(2)}) collective-permute-start(bf16[256,1152]{1,0:T(8,128)(2,1)S(1)} %collective-permute-done.23.refs_5_), channel_id=1, source_target_pairs={{0,1},{2,3},{4,5},{6,7},{8,9},{10,11},{12,13},{14,15},{16,17},{18,... | collective-permute-start | bytes 1769480 | tf_op jit(solution)/shard_map/ppermute | solution.py:61
  124.8 16.8 %collective-permute-start.25 = (bf16[256,1152]{1,0:T(8,128)(2,1)S(1)}, bf16[256,1152]{1,0:T(8,128)(2,1)S(1)}, u32[]{:S(2)}, u32[]{:S(2)}) collective-permute-start(bf16[256,1152]{1,0:T(8,128)(2,1)S(1)} %collective-permute-done.22.refs_2_), channel_id=1, source_target_pairs={{1,2},{3,4},{5,6},{7,8},{9,10},{11,12},{13,14},{15,16},{17,18},{19... | collective-permute-start | bytes 1769480 | tf_op jit(solution)/shard_map/ppermute | solution.py:61
  128.4 7.3 %collective-permute-start.38 = (bf16[6,1152]{1,0:T(8,128)(2,1)S(1)}, bf16[6,1152]{1,0:T(8,128)(2,1)S(1)}, u32[]{:S(2)}, u32[]{:S(2)}) collective-permute-start(bf16[6,1152]{1,0:T(8,128)(2,1)S(1)} %get-tuple-element.51), channel_id=1, source_target_pairs={{8,0},{9,1},{10,2},{11,3},{12,4},{13,5},{14,6},{15,7},{16,8},{17,9... | collective-permute-start | bytes 41480 | tf_op jit(solution)/shard_map/ppermute | solution.py:41
  129.7 6.0 %collective-permute-start.39 = (bf16[6,1152]{1,0:T(8,128)(2,1)S(1)}, bf16[6,1152]{1,0:T(8,128)(2,1)S(1)}, u32[]{:S(2)}, u32[]{:S(2)}) collective-permute-start(bf16[6,1152]{1,0:T(8,128)(2,1)S(1)} %get-tuple-element.52), channel_id=1, source_target_pairs={{56,0},{57,1},{58,2},{59,3},{60,4},{61,5},{62,6},{63,7},{0,8},{1,9... | collective-permute-start | bytes 41480 | tf_op jit(solution)/shard_map/ppermute | solution.py:41
  130.5 11.2 %copy-start.1 = (bf16[256,1152]{1,0:T(8,128)(2,1)S(1)}, bf16[256,1152]{1,0:T(8,128)(2,1)}, u32[]{:S(2)}) copy-start(bf16[256,1152]{1,0:T(8,128)(2,1)} %raw_ref.3) | copy-start | bytes 1769476

commit v3 on v1

--- a/solution.py
+++ b/solution.py
@@ -46,11 +46,11 @@
 
 
 def along_first(d):
-    return lambda y, z, x, c: (y, z, x + d, c) if c == 0 else (y + d, z, x, c)
+    return lambda y, z, x, c: (y, z, x + d, c) if c == 1 else (y + d, z, x, c)
 
 
 def along_second(d):
-    return lambda y, z, x, c: (y + d, z, x, c) if c == 0 else (y, z, x + d, c)
+    return lambda y, z, x, c: (y + d, z, x, c) if c == 1 else (y, z, x + d, c)
 
 
 def sibling(y, z, x, c):
@@ -79,12 +79,24 @@
     ))
 
 
-def text_body(raw_ref, w_ref, low_ref, length_ref, kept_ref):
-    kept_ref[...] = w_ref[...]
-    raw = raw_ref[...].astype(F32)
-    length = jnp.sqrt(jnp.sum(raw * raw, axis=1, keepdims=True) + EPS)
-    length_ref[...] = length
-    low_ref[...] = (raw / length).astype(BF16)
+def length_of(rows):
+    return jnp.sqrt(jnp.sum(rows * rows, axis=1, keepdims=True) + EPS)
+
+
+def text_body(raw_source, w_source, low_ref, raw_ref, w_ref, done):
+    half = R // 2
+    copies = [pltpu.make_async_copy(w_source, w_ref, done.at[2])]
+    for i in range(2):
+        rows = pl.ds(i * half, half)
+        copies.append(pltpu.make_async_copy(raw_source.at[rows, :], raw_ref.at[rows, :], done.at[i]))
+    for copy in copies:
+        copy.start()
+    for i in range(2):
+        rows = pl.ds(i * half, half)
+        copies[i + 1].wait()
+        raw = raw_ref[rows, :].astype(F32)
+        low_ref[rows, :] = (raw / length_of(raw)).astype(BF16)
+    copies[0].wait()
 
 
 def order_body(coord_ref, source_ref, pick_ref, xp_ref, xpt_ref, x_ref, done):
@@ -101,8 +113,8 @@
             group = i * (COLS // SUB) + j
             core = (c + group // 16) % NC
             second, first = group // 4 % 4, group % 4
-            at_y = (y + jnp.where(core == 0, second, first)) % NY
-            at_x = (x + jnp.where(core == 0, first, second)) % NX
+            at_y = (y + jnp.where(core == 1, second, first)) % NY
+            at_x = (x + jnp.where(core == 1, first, second)) % NX
             base = (at_y * (NZ * NX * NC) + at_x * NC + core) * OWN
             chosen = jnp.where(lanes == within + base, 1.0, 0.0).astype(BF16)
             pick_ref[pl.ds(pl.multiple_of(i * COLS + j * SUB, 16), SUB), :] = chosen
@@ -189,12 +201,12 @@
         out_ref[:, cols] = mm(mixed[...], pick_ref[:, cols]).astype(BF16)
 
 
-def text_grad_body(scalar_ref, raw_ref, low_ref, length_ref, p0, p1, p2, p3, out_ref, grad, pair):
+def text_grad_body(scalar_ref, raw_ref, low_ref, p0, p1, p2, p3, out_ref, grad, pair):
     scale, bias = scalar_ref[0], scalar_ref[1]
     images = (p0, p1, p2, p3)
     for k, image in enumerate(images):
         pair[k] = derivative(low_ref[...], image[...], scale, bias, k == 0)
-    length = length_ref[...]
+    length = length_of(raw_ref[...].astype(F32))
     inner = jnp.zeros((R, 1), F32)
     for at in range(0, E, COLS):
         cols = pl.ds(at, COLS)
@@ -259,14 +271,14 @@
     place = jnp.stack([lax.axis_index(a) for a in AXES]).astype(jnp.int32)
     before = fetch(head_weight, along_z(-1))
     behind = fetch(head_weight, along_z(1))
-    text_low, text_length, kept = call(
-        text_body, [((R, E), BF16), ((R, 1), F32), ((OWN, E), BF16)], text_embeds, head_weight, flops=10**8
+    text_low, text_raw, kept = call(
+        text_body, [((R, E), BF16), ((R, E), BF16), ((OWN, E), BF16)], text_embeds, head_weight,
+        flops=10**8, hbm=(0, 1), scratch=[pltpu.SemaphoreType.DMA((3,))],
     )
     weight = gather_weight(kept, before, behind)
-    text1 = fetch(text_low, along_blocks(1))
-    text2 = fetch(text_low, along_blocks(2))
-    text3 = fetch(text2, along_blocks(1))
-    texts = [text_low, text1, text2, text3]
+    texts = [text_low]
+    for _ in range(1, S):
+        texts.append(fetch(texts[-1], along_blocks(1)))
     pick, xp, xpt = call(
         order_body, [((D, D), BF16), ((R, D), BF16), ((D, R), BF16)], place, image_features,
         flops=4 * D * D * R, smem=(0,), hbm=(1,),
@@ -296,7 +308,7 @@
         )
     grad_weight = scatter_weight(pieces)
     (grad_text,) = call(
-        text_grad_body, [((R, E), BF16)], scalars, text_embeds, text_low, text_length, *images,
+        text_grad_body, [((R, E), BF16)], scalars, text_raw, text_low, *images,
         flops=16 * R * R * E, scratch=work, smem=(0,), final=True,
     )
     return grad_features, grad_text, grad_weight

time: 134 us -> 140 us (1.045)
  the two profiles are of different devices: /device:TPU:0 before, /device:TPU:96 now
where the time goes in v3:
time: 140 us
  waiting for transfers between devices  69.4 us (50%)
  starting transfers between devices  43.6 us (31%)
  Pallas kernels  23 us (16%)
  between operations  2.18 us (2%)
    ppermute x34, waiting for transfers between devices, fetch(): lax.ppermute(value, AXES, [(index(*where(*coords(i))), i) for i in range(...  69.4 us
    ppermute x34, starting transfers between devices, fetch(): lax.ppermute(value, AXES, [(index(*where(*coords(i))), i) for i in range(...  43.6 us
    pallas_call x16, Pallas kernels, call(): pl.pallas_call(body, out_shape=[jax.ShapeDtypeStruct(s, d) if final else...  23 us
  transfers between devices with their start and end apart: 34, of which 15 were waited for; matrix products, arithmetic and copies ran while one was open for 0% of the time, Pallas kernels for 16%

profile of v3, /device:TPU:96, one launch (start us, length us, event | category | flops | bytes accessed | tf_op | source)
XLA Modules:
  0.0 139.8 jit_solution(13424634771153240326)
XLA Ops:
  0.6 1.3 shard_map.77
  2.0 0.8 copy-done.2
  2.8 1.7 %collective-permute-start.14 = (bf16[256,1152]{1,0:T(8,128)(2,1)S(1)}, bf16[256,1152]{1,0:T(8,128)(2,1)}, u32[]{:S(2)}, u32[]{:S(2)}) collective-permute-start(bf16[256,1152]{1,0:T(8,128)(2,1)S(1)} %get-tuple-element.33.t0.low_ref), channel_id=1, source_target_pairs={{1,0},{2,1},{3,2},{4,3},{5,4},{6,5},{7,6},{8,7},{9,8},{10,9},{11,1... | collective-permute-start | bytes 1769480 | tf_op jit(solution)/shard_map/ppermute | solution.py:41
  4.5 3.1 %collective-permute-start = (bf16[6,1152]{1,0:T(8,128)(2,1)}, bf16[6,1152]{1,0:T(8,128)(2,1)S(1)}, u32[]{:S(2)}, u32[]{:S(2)}) collective-permute-start(bf16[6,1152]{1,0:T(8,128)(2,1)} %w_source.1), channel_id=1, source_target_pairs={{56,0},{57,1},{58,2},{59,3},{60,4},{61,5},{62,6},{63,7},{0,8},{1,9... | collective-permute-start | bytes 41480 | tf_op jit(solution)/shard_map/ppermute | solution.py:41
  7.7 1.7 %collective-permute-done.refs_0_ = bf16[6,1152]{1,0:T(8,128)(2,1)S(1)} collective-permute-done((bf16[6,1152]{1,0:T(8,128)(2,1)}, bf16[6,1152]{1,0:T(8,128)(2,1)S(1)}, u32[]{:S(2)}, u32[]{:S(2)}) %collective-permute-start) | collective-permute-done | bytes 13856 | tf_op jit(solution)/shard_map/ppermute | solution.py:41
  9.3 6.6 %collective-permute-done.1.refs_2_ = bf16[6,1152]{1,0:T(8,128)(2,1)S(1)} collective-permute-done((bf16[6,1152]{1,0:T(8,128)(2,1)}, bf16[6,1152]{1,0:T(8,128)(2,1)S(1)}, u32[]{:S(2)}, u32[]{:S(2)}) %collective-permute-start.1) | collective-permute-done | bytes 13856 | tf_op jit(solution)/shard_map/ppermute | solution.py:41
  15.9 3.9 %collective-permute-start.2 = (bf16[18,1152]{1,0:T(8,128)(2,1)S(1)}, bf16[18,1152]{1,0:T(8,128)(2,1)S(1)}, u32[]{:S(2)}, u32[]{:S(2)}) collective-permute-start(bf16[18,1152]{1,0:T(8,128)(2,1)S(1)} %shard_map.78.refs_1_), channel_id=1, source_target_pairs={{48,0},{49,1},{50,2},{51,3},{52,4},{53,5},{54,6},{55,7},{56,8},{57... | collective-permute-start | bytes 124424 | tf_op jit(solution)/shard_map/ppermute | solution.py:41
  19.8 1.7 %collective-permute-start.3 = (bf16[18,1152]{1,0:T(8,128)(2,1)S(1)}, bf16[18,1152]{1,0:T(8,128)(2,1)S(1)}, u32[]{:S(2)}, u32[]{:S(2)}) collective-permute-start(bf16[18,1152]{1,0:T(8,128)(2,1)S(1)} %shard_map.78.refs_1_), channel_id=1, source_target_pairs={{24,0},{25,1},{26,2},{27,3},{28,4},{29,5},{30,6},{31,7},{32,8},{33... | collective-permute-start | bytes 124424 | tf_op jit(solution)/shard_map/ppermute | solution.py:41
  21.5 0.1 collective-permute-done.2.refs_0_
  21.6 5.8 %collective-permute-done.3.refs_2_ = bf16[18,1152]{1,0:T(8,128)(2,1)S(1)} collective-permute-done((bf16[18,1152]{1,0:T(8,128)(2,1)S(1)}, bf16[18,1152]{1,0:T(8,128)(2,1)S(1)}, u32[]{:S(2)}, u32[]{:S(2)}) %collective-permute-start.3) | collective-permute-done | bytes 41504 | tf_op jit(solution)/shard_map/ppermute | solution.py:41
  27.5 2.7 %collective-permute-start.4 = (bf16[48,1152]{1,0:T(8,128)(2,1)S(1)}, bf16[48,1152]{1,0:T(8,128)(2,1)S(1)}, u32[]{:S(2)}, u32[]{:S(2)}) collective-permute-start(bf16[48,1152]{1,0:T(8,128)(2,1)S(1)} %shard_map.79.refs_0_), channel_id=1, source_target_pairs={{64,0},{3,1},{66,2},{5,3},{68,4},{7,5},{70,6},{1,7},{72,8},{11,9},... | collective-permute-start | bytes 331784 | tf_op jit(solution)/shard_map/ppermute | solution.py:41
  30.2 0.6 collective-permute-start.5
  30.8 1.0 collective-permute-start.6
  31.8 7.6 %collective-permute-done.4.refs_1_ = bf16[48,1152]{1,0:T(8,128)(2,1)S(1)} collective-permute-done((bf16[48,1152]{1,0:T(8,128)(2,1)S(1)}, bf16[48,1152]{1,0:T(8,128)(2,1)S(1)}, u32[]{:S(2)}, u32[]{:S(2)}) %collective-permute-start.4) | collective-permute-done | bytes 110624 | tf_op jit(solution)/shard_map/ppermute | solution.py:41
  39.4 1.4 %collective-permute-done.6.refs_3_ = bf16[48,1152]{1,0:T(8,128)(2,1)S(1)} collective-permute-done((bf16[48,1152]{1,0:T(8,128)(2,1)S(1)}, bf16[48,1152]{1,0:T(8,128)(2,1)S(1)}, u32[]{:S(2)}, u32[]{:S(2)}) %collective-permute-start.6) | collective-permute-done | bytes 110624 | tf_op jit(solution)/shard_map/ppermute | solution.py:41
  41.1 1.9 %collective-permute-start.9 = (bf16[192,1152]{1,0:T(8,128)(2,1)S(1)}, bf16[192,1152]{1,0:T(8,128)(2,1)S(1)}, u32[]{:S(2)}, u32[]{:S(2)}) collective-permute-start(bf16[192,1152]{1,0:T(8,128)(2,1)S(1)} %shard_map.80.refs_0_), channel_id=1, source_target_pairs={{6,0},{193,1},{0,2},{195,3},{2,4},{197,5},{4,6},{199,7},{14,8},{20... | collective-permute-start | bytes 1327112 | tf_op jit(solution)/shard_map/ppermute | solution.py:41
  43.0 0.5 collective-permute-start.10
  43.5 14.3 %collective-permute-done.7.refs_1_ = bf16[192,1152]{1,0:T(8,128)(2,1)S(1)} collective-permute-done((bf16[192,1152]{1,0:T(8,128)(2,1)S(1)}, bf16[192,1152]{1,0:T(8,128)(2,1)S(1)}, u32[]{:S(2)}, u32[]{:S(2)}) %collective-permute-start.7) | collective-permute-done | bytes 442400 | tf_op jit(solution)/shard_map/ppermute | solution.py:41
  57.8 0.5 collective-permute-start.12
  58.5 5.6 %collective-permute-start.16 = (bf16[256,1152]{1,0:T(8,128)(2,1)}, bf16[256,1152]{1,0:T(8,128)(2,1)S(1)}, u32[]{:S(2)}, u32[]{:S(2)}) collective-permute-start(bf16[256,1152]{1,0:T(8,128)(2,1)} %collective-permute-done.15.t2), channel_id=1, source_target_pairs={{1,0},{2,1},{3,2},{4,3},{5,4},{6,5},{7,6},{8,7},{9,8},{10,9},{11,1... | collective-permute-start | bytes 1769480 | tf_op jit(solution)/shard_map/ppermute | solution.py:41
  64.1 6.2 %shard_map.76 = (bf16[1536,1536]{1,0:T(8,128)(2,1)S(1)}, bf16[256,1536]{1,0:T(8,128)(2,1)S(1)}, bf16[1536,256]{1,0:T(8,128)(2,1)S(1)}) custom-call(s32[4]{0:T(128)S(1)} %pad_add_fusion.coord_ref, bf16[256,1536]{1,0:T(8,128)(2,1)} %source_ref.1), custom_call_target="tpu_custom_call" | custom-call | flops 2415919104 | tf_op jit(solution)/shard_map/pallas_call | solution.py:68
  70.4 1.6 %shard_map.81 = (bf16[1536,1152]{1,0:T(8,128)(2,1)S(1)}, f32[256,1152]{1,0:T(8,128)S(1)}, bf16[256,1152]{1,0:T(8,128)(2,1)S(1)}, f32[256,1]{1,0:T(8,128)S(1)}) custom-call(bf16[256,1536]{1,0:T(8,128)(2,1)S(1)} %get-tuple-element.28.xp_ref, bf16[192,1152]{1,0:T(8,128)(2,1)S(1)} %shard_map.80.refs_0_, bf16[192,1152]{1,0:T(8,128)(2,1)S(1)} %collective-permute-done.7.refs_1_, ...), custom_call_target="tpu_custom_call" | custom-call | flops 905969664 | tf_op jit(solution)/shard_map/pallas_call | solution.py:68
  73.5 3.8 %shard_map.82 = (bf16[256,1152]{1,0:T(8,128)(2,1)S(1)}, bf16[192,1152]{1,0:T(8,128)(2,1)S(1)}, bf16[192,1152]{1,0:T(8,128)(2,1)S(1)}, bf16[192,1152]{1,0:T(8,128)(2,1)S(1)}, bf16[192,1152]{1,0:T(8,128)(2,1)S(1)}) custom-call(f32[2]{0:T(128)S(1)} %pad_maximum_fusion.scalar_ref, bf16[256,1152]{1,0:T(8,128)(2,1)S(1)} %get-tuple-element.30.low_ref.p0, ...), custom_call_target="tpu_custom_call" | custom-call | flops 1660944384 | tf_op jit(solution)/shard_map/pallas_call | solution.py:68
  77.3 0.9 collective-permute-start.25
  78.2 0.1 collective-permute-start.23
  78.3 0.4 collective-permute-start.21
  78.8 4.8 %collective-permute-done.17.p1 = bf16[256,1152]{1,0:T(8,128)(2,1)S(1)} collective-permute-done((bf16[256,1152]{1,0:T(8,128)(2,1)S(1)}, bf16[256,1152]{1,0:T(8,128)(2,1)S(1)}, u32[]{:S(2)}, u32[]{:S(2)}) %collective-permute-start.17) | collective-permute-done | bytes 589856 | tf_op jit(solution)/shard_map/ppermute | solution.py:41
  83.5 0.3 shard_map.88
  83.8 5.1 %collective-permute-start.26 = (bf16[192,1152]{1,0:T(8,128)(2,1)S(1)}, bf16[192,1152]{1,0:T(8,128)(2,1)S(1)}, u32[]{:S(2)}, u32[]{:S(2)}) collective-permute-start(bf16[192,1152]{1,0:T(8,128)(2,1)S(1)} %shard_map.88), channel_id=1, source_target_pairs={{2,0},{65,1},{4,2},{67,3},{6,4},{69,5},{0,6},{71,7},{10,8},{73,9},... | collective-permute-start | bytes 1327112 | tf_op jit(solution)/shard_map/ppermute | solution.py:41
  88.9 0.3 shard_map.87
  89.3 0.3 shard_map.86
  89.6 0.9 collective-permute-start.22
  90.6 5.0 %collective-permute-done.18.p2 = bf16[256,1152]{1,0:T(8,128)(2,1)S(1)} collective-permute-done((bf16[256,1152]{1,0:T(8,128)(2,1)S(1)}, bf16[256,1152]{1,0:T(8,128)(2,1)S(1)}, u32[]{:S(2)}, u32[]{:S(2)}) %collective-permute-start.18) | collective-permute-done | bytes 589856 | tf_op jit(solution)/shard_map/ppermute | solution.py:41
  95.6 0.3 shard_map.85.refs_0_
  95.9 3.6 %collective-permute-done.26.refs_3_ = bf16[192,1152]{1,0:T(8,128)(2,1)S(1)} collective-permute-done((bf16[192,1152]{1,0:T(8,128)(2,1)S(1)}, bf16[192,1152]{1,0:T(8,128)(2,1)S(1)}, u32[]{:S(2)}, u32[]{:S(2)}) %collective-permute-start.26) | collective-permute-done | bytes 442400 | tf_op jit(solution)/shard_map/ppermute | solution.py:41
  99.5 4.2 %collective-permute-done.24.refs_2_ = bf16[192,1152]{1,0:T(8,128)(2,1)S(1)} collective-permute-done((bf16[192,1152]{1,0:T(8,128)(2,1)S(1)}, bf16[192,1152]{1,0:T(8,128)(2,1)S(1)}, u32[]{:S(2)}, u32[]{:S(2)}) %collective-permute-start.24) | collective-permute-done | bytes 442400 | tf_op jit(solution)/shard_map/ppermute | solution.py:41
  103.7 9.4 %collective-permute-done.22.refs_1_ = bf16[192,1152]{1,0:T(8,128)(2,1)S(1)} collective-permute-done((bf16[192,1152]{1,0:T(8,128)(2,1)S(1)}, bf16[192,1152]{1,0:T(8,128)(2,1)S(1)}, u32[]{:S(2)}, u32[]{:S(2)}) %collective-permute-start.22) | collective-permute-done | bytes 442400 | tf_op jit(solution)/shard_map/ppermute | solution.py:41
  113.1 0.2 shard_map.89
  113.4 3.6 %collective-permute-start.28 = (bf16[48,1152]{1,0:T(8,128)(2,1)S(1)}, bf16[48,1152]{1,0:T(8,128)(2,1)S(1)}, u32[]{:S(2)}, u32[]{:S(2)}) collective-permute-start(bf16[48,1152]{1,0:T(8,128)(2,1)S(1)} %get-tuple-element.45), channel_id=1, source_target_pairs={{128,0},{5,1},{130,2},{7,3},{132,4},{1,5},{134,6},{3,7},{136,8},{1... | collective-permute-start | bytes 331784 | tf_op jit(solution)/shard_map/ppermute | solution.py:41
  117.0 2.3 %collective-permute-done.27.refs_1_ = bf16[48,1152]{1,0:T(8,128)(2,1)S(1)} collective-permute-done((bf16[48,1152]{1,0:T(8,128)(2,1)S(1)}, bf16[48,1152]{1,0:T(8,128)(2,1)S(1)}, u32[]{:S(2)}, u32[]{:S(2)}) %collective-permute-start.27) | collective-permute-done | bytes 110624 | tf_op jit(solution)/shard_map/ppermute | solution.py:41
  119.4 1.6 %collective-permute-done.28.refs_2_ = bf16[48,1152]{1,0:T(8,128)(2,1)S(1)} collective-permute-done((bf16[48,1152]{1,0:T(8,128)(2,1)S(1)}, bf16[48,1152]{1,0:T(8,128)(2,1)S(1)}, u32[]{:S(2)}, u32[]{:S(2)}) %collective-permute-start.28) | collective-permute-done | bytes 110624 | tf_op jit(solution)/shard_map/ppermute | solution.py:41
  120.9 0.8 collective-permute-done.29.refs_3_
  121.9 2.4 %collective-permute-start.31 = (bf16[18,1152]{1,0:T(8,128)(2,1)S(1)}, bf16[18,1152]{1,0:T(8,128)(2,1)S(1)}, u32[]{:S(2)}, u32[]{:S(2)}) collective-permute-start(bf16[18,1152]{1,0:T(8,128)(2,1)S(1)} %get-tuple-element.49), channel_id=1, source_target_pairs={{40,0},{41,1},{42,2},{43,3},{44,4},{45,5},{46,6},{47,7},{48,8},{49... | collective-permute-start | bytes 124424 | tf_op jit(solution)/shard_map/ppermute | solution.py:41
  124.2 3.1 %collective-permute-start.30 = (bf16[12,1152]{1,0:T(8,128)(2,1)S(1)}, bf16[12,1152]{1,0:T(8,128)(2,1)S(1)}, u32[]{:S(2)}, u32[]{:S(2)}) collective-permute-start(bf16[12,1152]{1,0:T(8,128)(2,1)S(1)} %get-tuple-element.48), channel_id=1, source_target_pairs={{16,0},{17,1},{18,2},{19,3},{20,4},{21,5},{22,6},{23,7},{24,8},{25... | collective-permute-start | bytes 82952 | tf_op jit(solution)/shard_map/ppermute | solution.py:41
  127.4 5.2 %shard_map.83 = bf16[256,1536]{1,0:T(8,128)(2,1)} custom-call(bf16[256,1152]{1,0:T(8,128)(2,1)S(1)} %get-tuple-element.35.eg_ref, bf16[1536,1152]{1,0:T(8,128)(2,1)S(1)} %get-tuple-element.36.w_ref, bf16[1536,1536]{1,0:T(8,128)(2,1)S(1)} %get-tuple-element.37.pick_ref), custom_call_target="tpu_custom_call" | custom-call | flops 2113929216 | tf_op jit(solution)/shard_map/pallas_call | solution.py:68
  132.7 3.2 %collective-permute-start.33 = (bf16[6,1152]{1,0:T(8,128)(2,1)S(1)}, bf16[6,1152]{1,0:T(8,128)(2,1)S(1)}, u32[]{:S(2)}, u32[]{:S(2)}) collective-permute-start(bf16[6,1152]{1,0:T(8,128)(2,1)S(1)} %get-tuple-element.52), channel_id=1, source_target_pairs={{56,0},{57,1},{58,2},{59,3},{60,4},{61,5},{62,6},{63,7},{0,8},{1,9... | collective-permute-start | bytes 41480 | tf_op jit(solution)/shard_map/ppermute | solution.py:41
  135.9 3.3 %shard_map.84 = bf16[256,1152]{1,0:T(8,128)(2,1)} custom-call(f32[2]{0:T(128)S(1)} %pad_maximum_fusion.scalar_ref, bf16[256,1152]{1,0:T(8,128)(2,1)S(1)} %copy-done.3, bf16[256,1152]{1,0:T(8,128)(2,1)S(1)} %copy-done.1, bf16[256,1152]{1,0:T(8,128)(2,1)S(1)} %get-tuple-element.30.low_ref.p0, bf16[256,1152]{1,0:T(8,128)(2,1)S(1)} %collective-permute-done.17.p1, ...), custom_call_target="tpu_custom_call" | custom-call | flops 1207959552 | tf_op jit(solution)/shard_map/pallas_call | solution.py:68
  139.2 0.6 convert_add_fusion
  (47 shorter events, 1.0 us)
Async XLA Ops:
  2.0 0.8 copy-start.2
  2.8 55.6 %copy-start = (bf16[256,1152]{1,0:T(8,128)(2,1)}, bf16[256,1152]{1,0:T(8,128)(2,1)S(1)}, u32[]{:S(2)}) copy-start(bf16[256,1152]{1,0:T(8,128)(2,1)S(1)} %get-tuple-element.33.t0.low_ref) | copy-start | bytes 1769476
  2.8 40.2 %collective-permute-start.14 = (bf16[256,1152]{1,0:T(8,128)(2,1)S(1)}, bf16[256,1152]{1,0:T(8,128)(2,1)}, u32[]{:S(2)}, u32[]{:S(2)}) collective-permute-start(bf16[256,1152]{1,0:T(8,128)(2,1)S(1)} %get-tuple-element.33.t0.low_ref), channel_id=1, source_target_pairs={{1,0},{2,1},{3,2},{4,3},{5,4},{6,5},{7,6},{8,7},{9,8},{10,9},{11,1... | collective-permute-start | bytes 1769480 | tf_op jit(solution)/shard_map/ppermute | solution.py:41
  4.5 4.8 %collective-permute-start = (bf16[6,1152]{1,0:T(8,128)(2,1)}, bf16[6,1152]{1,0:T(8,128)(2,1)S(1)}, u32[]{:S(2)}, u32[]{:S(2)}) collective-permute-start(bf16[6,1152]{1,0:T(8,128)(2,1)} %w_source.1), channel_id=1, source_target_pairs={{56,0},{57,1},{58,2},{59,3},{60,4},{61,5},{62,6},{63,7},{0,8},{1,9... | collective-permute-start | bytes 41480 | tf_op jit(solution)/shard_map/ppermute | solution.py:41
  7.7 8.3 %collective-permute-start.1 = (bf16[6,1152]{1,0:T(8,128)(2,1)}, bf16[6,1152]{1,0:T(8,128)(2,1)S(1)}, u32[]{:S(2)}, u32[]{:S(2)}) collective-permute-start(bf16[6,1152]{1,0:T(8,128)(2,1)} %w_source.1), channel_id=1, source_target_pairs={{8,0},{9,1},{10,2},{11,3},{12,4},{13,5},{14,6},{15,7},{16,8},{17,9... | collective-permute-start | bytes 41480 | tf_op jit(solution)/shard_map/ppermute | solution.py:41
  15.9 5.7 %collective-permute-start.2 = (bf16[18,1152]{1,0:T(8,128)(2,1)S(1)}, bf16[18,1152]{1,0:T(8,128)(2,1)S(1)}, u32[]{:S(2)}, u32[]{:S(2)}) collective-permute-start(bf16[18,1152]{1,0:T(8,128)(2,1)S(1)} %shard_map.78.refs_1_), channel_id=1, source_target_pairs={{48,0},{49,1},{50,2},{51,3},{52,4},{53,5},{54,6},{55,7},{56,8},{57... | collective-permute-start | bytes 124424 | tf_op jit(solution)/shard_map/ppermute | solution.py:41
  19.8 7.6 %collective-permute-start.3 = (bf16[18,1152]{1,0:T(8,128)(2,1)S(1)}, bf16[18,1152]{1,0:T(8,128)(2,1)S(1)}, u32[]{:S(2)}, u32[]{:S(2)}) collective-permute-start(bf16[18,1152]{1,0:T(8,128)(2,1)S(1)} %shard_map.78.refs_1_), channel_id=1, source_target_pairs={{24,0},{25,1},{26,2},{27,3},{28,4},{29,5},{30,6},{31,7},{32,8},{33... | collective-permute-start | bytes 124424 | tf_op jit(solution)/shard_map/ppermute | solution.py:41
  27.5 12.0 %collective-permute-start.4 = (bf16[48,1152]{1,0:T(8,128)(2,1)S(1)}, bf16[48,1152]{1,0:T(8,128)(2,1)S(1)}, u32[]{:S(2)}, u32[]{:S(2)}) collective-permute-start(bf16[48,1152]{1,0:T(8,128)(2,1)S(1)} %shard_map.79.refs_0_), channel_id=1, source_target_pairs={{64,0},{3,1},{66,2},{5,3},{68,4},{7,5},{70,6},{1,7},{72,8},{11,9},... | collective-permute-start | bytes 331784 | tf_op jit(solution)/shard_map/ppermute | solution.py:41
  30.2 9.2 %collective-permute-start.5 = (bf16[48,1152]{1,0:T(8,128)(2,1)S(1)}, bf16[48,1152]{1,0:T(8,128)(2,1)S(1)}, u32[]{:S(2)}, u32[]{:S(2)}) collective-permute-start(bf16[48,1152]{1,0:T(8,128)(2,1)S(1)} %shard_map.79.refs_0_), channel_id=1, source_target_pairs={{128,0},{5,1},{130,2},{7,3},{132,4},{1,5},{134,6},{3,7},{136,8},{1... | collective-permute-start | bytes 331784 | tf_op jit(solution)/shard_map/ppermute | solution.py:41
  30.8 10.0 %collective-permute-start.6 = (bf16[48,1152]{1,0:T(8,128)(2,1)S(1)}, bf16[48,1152]{1,0:T(8,128)(2,1)S(1)}, u32[]{:S(2)}, u32[]{:S(2)}) collective-permute-start(bf16[48,1152]{1,0:T(8,128)(2,1)S(1)} %shard_map.79.refs_0_), channel_id=1, source_target_pairs={{192,0},{7,1},{194,2},{1,3},{196,4},{3,5},{198,6},{5,7},{200,8},{1... | collective-permute-start | bytes 331784 | tf_op jit(solution)/shard_map/ppermute | solution.py:41
  40.9 17.0 %collective-permute-start.7 = (bf16[192,1152]{1,0:T(8,128)(2,1)S(1)}, bf16[192,1152]{1,0:T(8,128)(2,1)S(1)}, u32[]{:S(2)}, u32[]{:S(2)}) collective-permute-start(bf16[192,1152]{1,0:T(8,128)(2,1)S(1)} %shard_map.80.refs_0_), channel_id=1, source_target_pairs={{2,0},{65,1},{4,2},{67,3},{6,4},{69,5},{0,6},{71,7},{10,8},{73,9},... | collective-permute-start | bytes 1327112 | tf_op jit(solution)/shard_map/ppermute | solution.py:41
  41.0 16.9 %collective-permute-start.8 = (bf16[192,1152]{1,0:T(8,128)(2,1)S(1)}, bf16[192,1152]{1,0:T(8,128)(2,1)S(1)}, u32[]{:S(2)}, u32[]{:S(2)}) collective-permute-start(bf16[192,1152]{1,0:T(8,128)(2,1)S(1)} %shard_map.80.refs_0_), channel_id=1, source_target_pairs={{4,0},{129,1},{6,2},{131,3},{0,4},{133,5},{2,6},{135,7},{12,8},{13... | collective-permute-start | bytes 1327112 | tf_op jit(solution)/shard_map/ppermute | solution.py:41
  41.1 17.3 %collective-permute-start.9 = (bf16[192,1152]{1,0:T(8,128)(2,1)S(1)}, bf16[192,1152]{1,0:T(8,128)(2,1)S(1)}, u32[]{:S(2)}, u32[]{:S(2)}) collective-permute-start(bf16[192,1152]{1,0:T(8,128)(2,1)S(1)} %shard_map.80.refs_0_), channel_id=1, source_target_pairs={{6,0},{193,1},{0,2},{195,3},{2,4},{197,5},{4,6},{199,7},{14,8},{20... | collective-permute-start | bytes 1327112 | tf_op jit(solution)/shard_map/ppermute | solution.py:41
  43.0 15.6 %collective-permute-start.15 = (bf16[256,1152]{1,0:T(8,128)(2,1)}, bf16[256,1152]{1,0:T(8,128)(2,1)}, u32[]{:S(2)}, u32[]{:S(2)}) collective-permute-start(bf16[256,1152]{1,0:T(8,128)(2,1)} %collective-permute-done.14.t1), channel_id=1, source_target_pairs={{1,0},{2,1},{3,2},{4,3},{5,4},{6,5},{7,6},{8,7},{9,8},{10,9},{11,1... | collective-permute-start | bytes 1769480 | tf_op jit(solution)/shard_map/ppermute | solution.py:41
  43.0 27.4 %collective-permute-start.10 = (bf16[192,1152]{1,0:T(8,128)(2,1)S(1)}, bf16[192,1152]{1,0:T(8,128)(2,1)S(1)}, u32[]{:S(2)}, u32[]{:S(2)}) collective-permute-start(bf16[192,1152]{1,0:T(8,128)(2,1)S(1)} %shard_map.80.refs_0_), channel_id=1, source_target_pairs={{1,0},{0,1},{3,2},{2,3},{5,4},{4,5},{7,6},{6,7},{9,8},{8,9},{11,10... | collective-permute-start | bytes 1327112 | tf_op jit(solution)/shard_map/ppermute | solution.py:41
  57.8 12.5 %collective-permute-start.11 = (bf16[192,1152]{1,0:T(8,128)(2,1)S(1)}, bf16[192,1152]{1,0:T(8,128)(2,1)S(1)}, u32[]{:S(2)}, u32[]{:S(2)}) collective-permute-start(bf16[192,1152]{1,0:T(8,128)(2,1)S(1)} %collective-permute-done.7.refs_1_), channel_id=1, source_target_pairs={{1,0},{0,1},{3,2},{2,3},{5,4},{4,5},{7,6},{6,7},{9,8},{8,9},{11,10... | collective-permute-start | bytes 1327112 | tf_op jit(solution)/shard_map/ppermute | solution.py:41
  57.8 12.5 %collective-permute-start.12 = (bf16[192,1152]{1,0:T(8,128)(2,1)S(1)}, bf16[192,1152]{1,0:T(8,128)(2,1)S(1)}, u32[]{:S(2)}, u32[]{:S(2)}) collective-permute-start(bf16[192,1152]{1,0:T(8,128)(2,1)S(1)} %collective-permute-done.8.refs_2_), channel_id=1, source_target_pairs={{1,0},{0,1},{3,2},{2,3},{5,4},{4,5},{7,6},{6,7},{9,8},{8,9},{11,10... | collective-permute-start | bytes 1327112 | tf_op jit(solution)/shard_map/ppermute | solution.py:41
  58.4 12.0 %collective-permute-start.13 = (bf16[192,1152]{1,0:T(8,128)(2,1)S(1)}, bf16[192,1152]{1,0:T(8,128)(2,1)S(1)}, u32[]{:S(2)}, u32[]{:S(2)}) collective-permute-start(bf16[192,1152]{1,0:T(8,128)(2,1)S(1)} %collective-permute-done.9.refs_3_), channel_id=1, source_target_pairs={{1,0},{0,1},{3,2},{2,3},{5,4},{4,5},{7,6},{6,7},{9,8},{8,9},{11,10... | collective-permute-start | bytes 1327112 | tf_op jit(solution)/shard_map/ppermute | solution.py:41
  58.5 15.0 %collective-permute-start.16 = (bf16[256,1152]{1,0:T(8,128)(2,1)}, bf16[256,1152]{1,0:T(8,128)(2,1)S(1)}, u32[]{:S(2)}, u32[]{:S(2)}) collective-permute-start(bf16[256,1152]{1,0:T(8,128)(2,1)} %collective-permute-done.15.t2), channel_id=1, source_target_pairs={{1,0},{2,1},{3,2},{4,3},{5,4},{6,5},{7,6},{8,7},{9,8},{10,9},{11,1... | collective-permute-start | bytes 1769480 | tf_op jit(solution)/shard_map/ppermute | solution.py:41
  70.3 3.2 %copy-start.1 = (bf16[256,1152]{1,0:T(8,128)(2,1)S(1)}, bf16[256,1152]{1,0:T(8,128)(2,1)}, u32[]{:S(2)}) copy-start(bf16[256,1152]{1,0:T(8,128)(2,1)} %copy-done) | copy-start | bytes 1769476
  72.0 11.5 %collective-permute-start.17 = (bf16[256,1152]{1,0:T(8,128)(2,1)S(1)}, bf16[256,1152]{1,0:T(8,128)(2,1)S(1)}, u32[]{:S(2)}, u32[]{:S(2)}) collective-permute-start(bf16[256,1152]{1,0:T(8,128)(2,1)S(1)} %get-tuple-element.30.low_ref.p0), channel_id=1, source_target_pairs={{255,0},{0,1},{1,2},{2,3},{3,4},{4,5},{5,6},{6,7},{7,8},{8,9},{9,1... | collective-permute-start | bytes 1769480 | tf_op jit(solution)/shard_map/ppermute | solution.py:41
  77.3 6.2 %collective-permute-start.25 = (bf16[192,1152]{1,0:T(8,128)(2,1)S(1)}, bf16[192,1152]{1,0:T(8,128)(2,1)S(1)}, u32[]{:S(2)}, u32[]{:S(2)}) collective-permute-start(bf16[192,1152]{1,0:T(8,128)(2,1)S(1)} %get-tuple-element.42), channel_id=1, source_target_pairs={{1,0},{0,1},{3,2},{2,3},{5,4},{4,5},{7,6},{6,7},{9,8},{8,9},{11,10... | collective-permute-start | bytes 1327112 | tf_op jit(solution)/shard_map/ppermute | solution.py:41
  78.2 10.7 %collective-permute-start.23 = (bf16[192,1152]{1,0:T(8,128)(2,1)S(1)}, bf16[192,1152]{1,0:T(8,128)(2,1)S(1)}, u32[]{:S(2)}, u32[]{:S(2)}) collective-permute-start(bf16[192,1152]{1,0:T(8,128)(2,1)S(1)} %get-tuple-element.41), channel_id=1, source_target_pairs={{1,0},{0,1},{3,2},{2,3},{5,4},{4,5},{7,6},{6,7},{9,8},{8,9},{11,10... | collective-permute-start | bytes 1327112 | tf_op jit(solution)/shard_map/ppermute | solution.py:41
  78.3 11.0 %collective-permute-start.21 = (bf16[192,1152]{1,0:T(8,128)(2,1)S(1)}, bf16[192,1152]{1,0:T(8,128)(2,1)S(1)}, u32[]{:S(2)}, u32[]{:S(2)}) collective-permute-start(bf16[192,1152]{1,0:T(8,128)(2,1)S(1)} %get-tuple-element.40), channel_id=1, source_target_pairs={{1,0},{0,1},{3,2},{2,3},{5,4},{4,5},{7,6},{6,7},{9,8},{8,9},{11,10... | collective-permute-start | bytes 1327112 | tf_op jit(solution)/shard_map/ppermute | solution.py:41
  83.5 12.1 %collective-permute-start.18 = (bf16[256,1152]{1,0:T(8,128)(2,1)S(1)}, bf16[256,1152]{1,0:T(8,128)(2,1)S(1)}, u32[]{:S(2)}, u32[]{:S(2)}) collective-permute-start(bf16[256,1152]{1,0:T(8,128)(2,1)S(1)} %collective-permute-done.17.p1), channel_id=1, source_target_pairs={{255,0},{0,1},{1,2},{2,3},{3,4},{4,5},{5,6},{6,7},{7,8},{8,9},{9,1... | collective-permute-start | bytes 1769480 | tf_op jit(solution)/shard_map/ppermute | solution.py:41
  83.5 12.1 %collective-permute-start.20 = (bf16[192,1152]{1,0:T(8,128)(2,1)S(1)}, bf16[192,1152]{1,0:T(8,128)(2,1)S(1)}, u32[]{:S(2)}, u32[]{:S(2)}) collective-permute-start(bf16[192,1152]{1,0:T(8,128)(2,1)S(1)} %get-tuple-element.39), channel_id=1, source_target_pairs={{1,0},{0,1},{3,2},{2,3},{5,4},{4,5},{7,6},{6,7},{9,8},{8,9},{11,10... | collective-permute-start | bytes 1327112 | tf_op jit(solution)/shard_map/ppermute | solution.py:41
  83.8 15.6 %collective-permute-start.26 = (bf16[192,1152]{1,0:T(8,128)(2,1)S(1)}, bf16[192,1152]{1,0:T(8,128)(2,1)S(1)}, u32[]{:S(2)}, u32[]{:S(2)}) collective-permute-start(bf16[192,1152]{1,0:T(8,128)(2,1)S(1)} %shard_map.88), channel_id=1, source_target_pairs={{2,0},{65,1},{4,2},{67,3},{6,4},{69,5},{0,6},{71,7},{10,8},{73,9},... | collective-permute-start | bytes 1327112 | tf_op jit(solution)/shard_map/ppermute | solution.py:41
  89.2 14.5 %collective-permute-start.24 = (bf16[192,1152]{1,0:T(8,128)(2,1)S(1)}, bf16[192,1152]{1,0:T(8,128)(2,1)S(1)}, u32[]{:S(2)}, u32[]{:S(2)}) collective-permute-start(bf16[192,1152]{1,0:T(8,128)(2,1)S(1)} %shard_map.87), channel_id=1, source_target_pairs={{4,0},{129,1},{6,2},{131,3},{0,4},{133,5},{2,6},{135,7},{12,8},{13... | collective-permute-start | bytes 1327112 | tf_op jit(solution)/shard_map/ppermute | solution.py:41
  89.6 23.5 %collective-permute-start.22 = (bf16[192,1152]{1,0:T(8,128)(2,1)S(1)}, bf16[192,1152]{1,0:T(8,128)(2,1)S(1)}, u32[]{:S(2)}, u32[]{:S(2)}) collective-permute-start(bf16[192,1152]{1,0:T(8,128)(2,1)S(1)} %shard_map.86), channel_id=1, source_target_pairs={{6,0},{193,1},{0,2},{195,3},{2,4},{197,5},{4,6},{199,7},{14,8},{20... | collective-permute-start | bytes 1327112 | tf_op jit(solution)/shard_map/ppermute | solution.py:41
  95.6 40.3 %collective-permute-start.19 = (bf16[256,1152]{1,0:T(8,128)(2,1)S(1)}, bf16[256,1152]{1,0:T(8,128)(2,1)S(1)}, u32[]{:S(2)}, u32[]{:S(2)}) collective-permute-start(bf16[256,1152]{1,0:T(8,128)(2,1)S(1)} %collective-permute-done.18.p2), channel_id=1, source_target_pairs={{255,0},{0,1},{1,2},{2,3},{3,4},{4,5},{5,6},{6,7},{7,8},{8,9},{9,1... | collective-permute-start | bytes 1769480 | tf_op jit(solution)/shard_map/ppermute | solution.py:41
  113.3 6.0 %collective-permute-start.27 = (bf16[48,1152]{1,0:T(8,128)(2,1)S(1)}, bf16[48,1152]{1,0:T(8,128)(2,1)S(1)}, u32[]{:S(2)}, u32[]{:S(2)}) collective-permute-start(bf16[48,1152]{1,0:T(8,128)(2,1)S(1)} %get-tuple-element.44), channel_id=1, source_target_pairs={{192,0},{7,1},{194,2},{1,3},{196,4},{3,5},{198,6},{5,7},{200,8},{1... | collective-permute-start | bytes 331784 | tf_op jit(solution)/shard_map/ppermute | solution.py:41
  113.4 7.5 %collective-permute-start.28 = (bf16[48,1152]{1,0:T(8,128)(2,1)S(1)}, bf16[48,1152]{1,0:T(8,128)(2,1)S(1)}, u32[]{:S(2)}, u32[]{:S(2)}) collective-permute-start(bf16[48,1152]{1,0:T(8,128)(2,1)S(1)} %get-tuple-element.45), channel_id=1, source_target_pairs={{128,0},{5,1},{130,2},{7,3},{132,4},{1,5},{134,6},{3,7},{136,8},{1... | collective-permute-start | bytes 331784 | tf_op jit(solution)/shard_map/ppermute | solution.py:41
  117.0 4.7 %collective-permute-start.29 = (bf16[48,1152]{1,0:T(8,128)(2,1)S(1)}, bf16[48,1152]{1,0:T(8,128)(2,1)S(1)}, u32[]{:S(2)}, u32[]{:S(2)}) collective-permute-start(bf16[48,1152]{1,0:T(8,128)(2,1)S(1)} %get-tuple-element.46), channel_id=1, source_target_pairs={{64,0},{3,1},{66,2},{5,3},{68,4},{7,5},{70,6},{1,7},{72,8},{11,9},... | collective-permute-start | bytes 331784 | tf_op jit(solution)/shard_map/ppermute | solution.py:41
  121.9 10.7 %collective-permute-start.31 = (bf16[18,1152]{1,0:T(8,128)(2,1)S(1)}, bf16[18,1152]{1,0:T(8,128)(2,1)S(1)}, u32[]{:S(2)}, u32[]{:S(2)}) collective-permute-start(bf16[18,1152]{1,0:T(8,128)(2,1)S(1)} %get-tuple-element.49), channel_id=1, source_target_pairs={{40,0},{41,1},{42,2},{43,3},{44,4},{45,5},{46,6},{47,7},{48,8},{49... | collective-permute-start | bytes 124424 | tf_op jit(solution)/shard_map/ppermute | solution.py:41
  124.2 8.3 %collective-permute-start.30 = (bf16[12,1152]{1,0:T(8,128)(2,1)S(1)}, bf16[12,1152]{1,0:T(8,128)(2,1)S(1)}, u32[]{:S(2)}, u32[]{:S(2)}) collective-permute-start(bf16[12,1152]{1,0:T(8,128)(2,1)S(1)} %get-tuple-element.48), channel_id=1, source_target_pairs={{16,0},{17,1},{18,2},{19,3},{20,4},{21,5},{22,6},{23,7},{24,8},{25... | collective-permute-start | bytes 82952 | tf_op jit(solution)/shard_map/ppermute | solution.py:41
  127.4 8.5 %copy-start.3 = (bf16[256,1152]{1,0:T(8,128)(2,1)S(1)}, bf16[256,1152]{1,0:T(8,128)(2,1)}, u32[]{:S(2)}) copy-start(bf16[256,1152]{1,0:T(8,128)(2,1)} %copy-done.2) | copy-start | bytes 1769476
  132.6 6.6 %collective-permute-start.32 = (bf16[6,1152]{1,0:T(8,128)(2,1)S(1)}, bf16[6,1152]{1,0:T(8,128)(2,1)S(1)}, u32[]{:S(2)}, u32[]{:S(2)}) collective-permute-start(bf16[6,1152]{1,0:T(8,128)(2,1)S(1)} %get-tuple-element.51), channel_id=1, source_target_pairs={{8,0},{9,1},{10,2},{11,3},{12,4},{13,5},{14,6},{15,7},{16,8},{17,9... | collective-permute-start | bytes 41480 | tf_op jit(solution)/shard_map/ppermute | solution.py:41
  132.7 6.5 %collective-permute-start.33 = (bf16[6,1152]{1,0:T(8,128)(2,1)S(1)}, bf16[6,1152]{1,0:T(8,128)(2,1)S(1)}, u32[]{:S(2)}, u32[]{:S(2)}) collective-permute-start(bf16[6,1152]{1,0:T(8,128)(2,1)S(1)} %get-tuple-element.52), channel_id=1, source_target_pairs={{56,0},{57,1},{58,2},{59,3},{60,4},{61,5},{62,6},{63,7},{0,8},{1,9... | collective-permute-start | bytes 41480 | tf_op jit(solution)/shard_map/ppermute | solution.py:41

commit v4 on v3

--- a/solution.py
+++ b/solution.py
@@ -46,11 +46,11 @@
 
 
 def along_first(d):
-    return lambda y, z, x, c: (y, z, x + d, c) if c == 1 else (y + d, z, x, c)
+    return lambda y, z, x, c: (y, z, x + d, c) if c == 0 else (y + d, z, x, c)
 
 
 def along_second(d):
-    return lambda y, z, x, c: (y + d, z, x, c) if c == 1 else (y, z, x + d, c)
+    return lambda y, z, x, c: (y + d, z, x, c) if c == 0 else (y, z, x + d, c)
 
 
 def sibling(y, z, x, c):
@@ -61,7 +61,7 @@
     return lambda y, z, x, c: coords((index(y, z, x, c) + d) % NDEV)
 
 
-def call(body, outs, *args, flops=0, scratch=(), smem=(), hbm=(), limit=16, final=False):
+def call(body, outs, *args, flops=0, scratch=(), smem=(), hbm=(), limit=8, final=False):
     def spec(i):
         return pl.BlockSpec(memory_space=pltpu.SMEM if i in smem else pltpu.HBM if i in hbm else pltpu.VMEM)
 
@@ -113,8 +113,8 @@
             group = i * (COLS // SUB) + j
             core = (c + group // 16) % NC
             second, first = group // 4 % 4, group % 4
-            at_y = (y + jnp.where(core == 1, second, first)) % NY
-            at_x = (x + jnp.where(core == 1, first, second)) % NX
+            at_y = (y + jnp.where(core == 0, second, first)) % NY
+            at_x = (x + jnp.where(core == 0, first, second)) % NX
             base = (at_y * (NZ * NX * NC) + at_x * NC + core) * OWN
             chosen = jnp.where(lanes == within + base, 1.0, 0.0).astype(BF16)
             pick_ref[pl.ds(pl.multiple_of(i * COLS + j * SUB, 16), SUB), :] = chosen

time: 140 us -> 142 us (1.014)
  the two profiles are of different devices: /device:TPU:96 before, /device:TPU:24 now
where the time goes in v4:
time: 142 us
  waiting for transfers between devices  65.6 us (46%)
  starting transfers between devices  49.8 us (35%)
  Pallas kernels  23 us (16%)
  between operations  2.22 us (2%)
    ppermute x34, waiting for transfers between devices, fetch(): lax.ppermute(value, AXES, [(index(*where(*coords(i))), i) for i in range(...  65.6 us
    ppermute x34, starting transfers between devices, fetch(): lax.ppermute(value, AXES, [(index(*where(*coords(i))), i) for i in range(...  49.8 us
    pallas_call x16, Pallas kernels, call(): pl.pallas_call(body, out_shape=[jax.ShapeDtypeStruct(s, d) if final else...  23 us
  transfers between devices with their start and end apart: 34, of which 18 were waited for; matrix products, arithmetic and copies ran while one was open for 0% of the time, Pallas kernels for 15%

profile of v4, /device:TPU:24, one launch (start us, length us, event | category | flops | bytes accessed | tf_op | source)
XLA Modules:
  0.0 142.3 jit_solution(14031414178880833314)
XLA Ops:
  0.6 1.3 shard_map.77
  2.0 0.8 copy-done.2
  2.8 7.7 %collective-permute-start.14 = (bf16[256,1152]{1,0:T(8,128)(2,1)S(1)}, bf16[256,1152]{1,0:T(8,128)(2,1)}, u32[]{:S(2)}, u32[]{:S(2)}) collective-permute-start(bf16[256,1152]{1,0:T(8,128)(2,1)S(1)} %get-tuple-element.33.t0.low_ref), channel_id=1, source_target_pairs={{1,0},{2,1},{3,2},{4,3},{5,4},{6,5},{7,6},{8,7},{9,8},{10,9},{11,1... | collective-permute-start | bytes 1769480 | tf_op jit(solution)/shard_map/ppermute | solution.py:41
  10.5 3.2 %collective-permute-start.1 = (bf16[6,1152]{1,0:T(8,128)(2,1)}, bf16[6,1152]{1,0:T(8,128)(2,1)S(1)}, u32[]{:S(2)}, u32[]{:S(2)}) collective-permute-start(bf16[6,1152]{1,0:T(8,128)(2,1)} %w_source.1), channel_id=1, source_target_pairs={{8,0},{9,1},{10,2},{11,3},{12,4},{13,5},{14,6},{15,7},{16,8},{17,9... | collective-permute-start | bytes 41480 | tf_op jit(solution)/shard_map/ppermute | solution.py:41
  13.7 2.1 %collective-permute-done.refs_0_ = bf16[6,1152]{1,0:T(8,128)(2,1)S(1)} collective-permute-done((bf16[6,1152]{1,0:T(8,128)(2,1)}, bf16[6,1152]{1,0:T(8,128)(2,1)S(1)}, u32[]{:S(2)}, u32[]{:S(2)}) %collective-permute-start) | collective-permute-done | bytes 13856 | tf_op jit(solution)/shard_map/ppermute | solution.py:41
  15.8 4.0 %collective-permute-done.1.refs_2_ = bf16[6,1152]{1,0:T(8,128)(2,1)S(1)} collective-permute-done((bf16[6,1152]{1,0:T(8,128)(2,1)}, bf16[6,1152]{1,0:T(8,128)(2,1)S(1)}, u32[]{:S(2)}, u32[]{:S(2)}) %collective-permute-start.1) | collective-permute-done | bytes 13856 | tf_op jit(solution)/shard_map/ppermute | solution.py:41
  19.9 6.0 %collective-permute-start.3 = (bf16[18,1152]{1,0:T(8,128)(2,1)S(1)}, bf16[18,1152]{1,0:T(8,128)(2,1)S(1)}, u32[]{:S(2)}, u32[]{:S(2)}) collective-permute-start(bf16[18,1152]{1,0:T(8,128)(2,1)S(1)} %shard_map.78.refs_1_), channel_id=1, source_target_pairs={{24,0},{25,1},{26,2},{27,3},{28,4},{29,5},{30,6},{31,7},{32,8},{33... | collective-permute-start | bytes 124424 | tf_op jit(solution)/shard_map/ppermute | solution.py:41
  26.0 0.3 collective-permute-done.2.refs_0_
  26.3 1.7 %collective-permute-done.3.refs_2_ = bf16[18,1152]{1,0:T(8,128)(2,1)S(1)} collective-permute-done((bf16[18,1152]{1,0:T(8,128)(2,1)S(1)}, bf16[18,1152]{1,0:T(8,128)(2,1)S(1)}, u32[]{:S(2)}, u32[]{:S(2)}) %collective-permute-start.3) | collective-permute-done | bytes 41504 | tf_op jit(solution)/shard_map/ppermute | solution.py:41
  28.1 0.1 collective-permute-start.5
  28.2 1.9 %collective-permute-start.6 = (bf16[48,1152]{1,0:T(8,128)(2,1)S(1)}, bf16[48,1152]{1,0:T(8,128)(2,1)S(1)}, u32[]{:S(2)}, u32[]{:S(2)}) collective-permute-start(bf16[48,1152]{1,0:T(8,128)(2,1)S(1)} %shard_map.79.refs_0_), channel_id=1, source_target_pairs={{6,0},{193,1},{0,2},{195,3},{2,4},{197,5},{4,6},{199,7},{14,8},{20... | collective-permute-start | bytes 331784 | tf_op jit(solution)/shard_map/ppermute | solution.py:41
  30.1 3.9 %collective-permute-done.4.refs_1_ = bf16[48,1152]{1,0:T(8,128)(2,1)S(1)} collective-permute-done((bf16[48,1152]{1,0:T(8,128)(2,1)S(1)}, bf16[48,1152]{1,0:T(8,128)(2,1)S(1)}, u32[]{:S(2)}, u32[]{:S(2)}) %collective-permute-start.4) | collective-permute-done | bytes 110624 | tf_op jit(solution)/shard_map/ppermute | solution.py:41
  34.0 1.7 %collective-permute-done.5.refs_2_ = bf16[48,1152]{1,0:T(8,128)(2,1)S(1)} collective-permute-done((bf16[48,1152]{1,0:T(8,128)(2,1)S(1)}, bf16[48,1152]{1,0:T(8,128)(2,1)S(1)}, u32[]{:S(2)}, u32[]{:S(2)}) %collective-permute-start.5) | collective-permute-done | bytes 110624 | tf_op jit(solution)/shard_map/ppermute | solution.py:41
  35.7 3.4 %collective-permute-done.6.refs_3_ = bf16[48,1152]{1,0:T(8,128)(2,1)S(1)} collective-permute-done((bf16[48,1152]{1,0:T(8,128)(2,1)S(1)}, bf16[48,1152]{1,0:T(8,128)(2,1)S(1)}, u32[]{:S(2)}, u32[]{:S(2)}) %collective-permute-start.6) | collective-permute-done | bytes 110624 | tf_op jit(solution)/shard_map/ppermute | solution.py:41
  39.2 0.7 collective-permute-start.7
  39.9 3.5 %collective-permute-start.8 = (bf16[192,1152]{1,0:T(8,128)(2,1)S(1)}, bf16[192,1152]{1,0:T(8,128)(2,1)S(1)}, u32[]{:S(2)}, u32[]{:S(2)}) collective-permute-start(bf16[192,1152]{1,0:T(8,128)(2,1)S(1)} %shard_map.80.refs_0_), channel_id=1, source_target_pairs={{128,0},{5,1},{130,2},{7,3},{132,4},{1,5},{134,6},{3,7},{136,8},{1... | collective-permute-start | bytes 1327112 | tf_op jit(solution)/shard_map/ppermute | solution.py:41
  43.4 0.5 collective-permute-start.10
  43.9 4.9 %collective-permute-done.7.refs_1_ = bf16[192,1152]{1,0:T(8,128)(2,1)S(1)} collective-permute-done((bf16[192,1152]{1,0:T(8,128)(2,1)S(1)}, bf16[192,1152]{1,0:T(8,128)(2,1)S(1)}, u32[]{:S(2)}, u32[]{:S(2)}) %collective-permute-start.7) | collective-permute-done | bytes 442400 | tf_op jit(solution)/shard_map/ppermute | solution.py:41
  48.7 5.6 %collective-permute-done.8.refs_2_ = bf16[192,1152]{1,0:T(8,128)(2,1)S(1)} collective-permute-done((bf16[192,1152]{1,0:T(8,128)(2,1)S(1)}, bf16[192,1152]{1,0:T(8,128)(2,1)S(1)}, u32[]{:S(2)}, u32[]{:S(2)}) %collective-permute-start.8) | collective-permute-done | bytes 442400 | tf_op jit(solution)/shard_map/ppermute | solution.py:41
  54.4 0.5 collective-permute-start.13
  55.0 4.7 %collective-permute-start.16 = (bf16[256,1152]{1,0:T(8,128)(2,1)}, bf16[256,1152]{1,0:T(8,128)(2,1)S(1)}, u32[]{:S(2)}, u32[]{:S(2)}) collective-permute-start(bf16[256,1152]{1,0:T(8,128)(2,1)} %collective-permute-done.15.t2), channel_id=1, source_target_pairs={{1,0},{2,1},{3,2},{4,3},{5,4},{6,5},{7,6},{8,7},{9,8},{10,9},{11,1... | collective-permute-start | bytes 1769480 | tf_op jit(solution)/shard_map/ppermute | solution.py:41
  59.6 6.2 %shard_map.76 = (bf16[1536,1536]{1,0:T(8,128)(2,1)S(1)}, bf16[256,1536]{1,0:T(8,128)(2,1)S(1)}, bf16[1536,256]{1,0:T(8,128)(2,1)S(1)}) custom-call(s32[4]{0:T(128)S(1)} %pad_add_fusion.coord_ref, bf16[256,1536]{1,0:T(8,128)(2,1)} %source_ref.1), custom_call_target="tpu_custom_call" | custom-call | flops 2415919104 | tf_op jit(solution)/shard_map/pallas_call | solution.py:68
  65.9 1.6 %shard_map.81 = (bf16[1536,1152]{1,0:T(8,128)(2,1)S(1)}, f32[256,1152]{1,0:T(8,128)S(1)}, bf16[256,1152]{1,0:T(8,128)(2,1)S(1)}, f32[256,1]{1,0:T(8,128)S(1)}) custom-call(bf16[256,1536]{1,0:T(8,128)(2,1)S(1)} %get-tuple-element.28.xp_ref, bf16[192,1152]{1,0:T(8,128)(2,1)S(1)} %shard_map.80.refs_0_, bf16[192,1152]{1,0:T(8,128)(2,1)S(1)} %collective-permute-done.7.refs_1_, ...), custom_call_target="tpu_custom_call" | custom-call | flops 905969664 | tf_op jit(solution)/shard_map/pallas_call | solution.py:68
  69.1 3.8 %shard_map.82 = (bf16[256,1152]{1,0:T(8,128)(2,1)S(1)}, bf16[192,1152]{1,0:T(8,128)(2,1)S(1)}, bf16[192,1152]{1,0:T(8,128)(2,1)S(1)}, bf16[192,1152]{1,0:T(8,128)(2,1)S(1)}, bf16[192,1152]{1,0:T(8,128)(2,1)S(1)}) custom-call(f32[2]{0:T(128)S(1)} %pad_maximum_fusion.scalar_ref, bf16[256,1152]{1,0:T(8,128)(2,1)S(1)} %get-tuple-element.30.low_ref.p0, ...), custom_call_target="tpu_custom_call" | custom-call | flops 1660944384 | tf_op jit(solution)/shard_map/pallas_call | solution.py:68
  72.9 0.1 collective-permute-start.25
  73.0 0.5 collective-permute-start.23
  73.5 0.1 collective-permute-start.21
  73.6 7.6 %collective-permute-done.17.p1 = bf16[256,1152]{1,0:T(8,128)(2,1)S(1)} collective-permute-done((bf16[256,1152]{1,0:T(8,128)(2,1)S(1)}, bf16[256,1152]{1,0:T(8,128)(2,1)S(1)}, u32[]{:S(2)}, u32[]{:S(2)}) %collective-permute-start.17) | collective-permute-done | bytes 589856 | tf_op jit(solution)/shard_map/ppermute | solution.py:41
  81.2 0.3 shard_map.88
  81.5 5.9 %collective-permute-start.26 = (bf16[192,1152]{1,0:T(8,128)(2,1)S(1)}, bf16[192,1152]{1,0:T(8,128)(2,1)S(1)}, u32[]{:S(2)}, u32[]{:S(2)}) collective-permute-start(bf16[192,1152]{1,0:T(8,128)(2,1)S(1)} %shard_map.88), channel_id=1, source_target_pairs={{64,0},{3,1},{66,2},{5,3},{68,4},{7,5},{70,6},{1,7},{72,8},{11,9},... | collective-permute-start | bytes 1327112 | tf_op jit(solution)/shard_map/ppermute | solution.py:41
  87.3 0.3 shard_map.87
  87.7 6.9 %collective-permute-start.24 = (bf16[192,1152]{1,0:T(8,128)(2,1)S(1)}, bf16[192,1152]{1,0:T(8,128)(2,1)S(1)}, u32[]{:S(2)}, u32[]{:S(2)}) collective-permute-start(bf16[192,1152]{1,0:T(8,128)(2,1)S(1)} %shard_map.87), channel_id=1, source_target_pairs={{128,0},{5,1},{130,2},{7,3},{132,4},{1,5},{134,6},{3,7},{136,8},{1... | collective-permute-start | bytes 1327112 | tf_op jit(solution)/shard_map/ppermute | solution.py:41
  94.6 0.3 shard_map.86
  95.0 2.0 %collective-permute-done.18.p2 = bf16[256,1152]{1,0:T(8,128)(2,1)S(1)} collective-permute-done((bf16[256,1152]{1,0:T(8,128)(2,1)S(1)}, bf16[256,1152]{1,0:T(8,128)(2,1)S(1)}, u32[]{:S(2)}, u32[]{:S(2)}) %collective-permute-start.18) | collective-permute-done | bytes 589856 | tf_op jit(solution)/shard_map/ppermute | solution.py:41
  97.0 0.3 shard_map.85.refs_0_
  97.3 1.7 %collective-permute-done.26.refs_3_ = bf16[192,1152]{1,0:T(8,128)(2,1)S(1)} collective-permute-done((bf16[192,1152]{1,0:T(8,128)(2,1)S(1)}, bf16[192,1152]{1,0:T(8,128)(2,1)S(1)}, u32[]{:S(2)}, u32[]{:S(2)}) %collective-permute-start.26) | collective-permute-done | bytes 442400 | tf_op jit(solution)/shard_map/ppermute | solution.py:41
  99.0 6.2 %collective-permute-done.24.refs_2_ = bf16[192,1152]{1,0:T(8,128)(2,1)S(1)} collective-permute-done((bf16[192,1152]{1,0:T(8,128)(2,1)S(1)}, bf16[192,1152]{1,0:T(8,128)(2,1)S(1)}, u32[]{:S(2)}, u32[]{:S(2)}) %collective-permute-start.24) | collective-permute-done | bytes 442400 | tf_op jit(solution)/shard_map/ppermute | solution.py:41
  105.2 12.1 %collective-permute-done.22.refs_1_ = bf16[192,1152]{1,0:T(8,128)(2,1)S(1)} collective-permute-done((bf16[192,1152]{1,0:T(8,128)(2,1)S(1)}, bf16[192,1152]{1,0:T(8,128)(2,1)S(1)}, u32[]{:S(2)}, u32[]{:S(2)}) %collective-permute-start.22) | collective-permute-done | bytes 442400 | tf_op jit(solution)/shard_map/ppermute | solution.py:41
  117.3 0.2 shard_map.89
  117.6 0.1 collective-permute-start.28
  117.7 3.1 %collective-permute-start.29 = (bf16[48,1152]{1,0:T(8,128)(2,1)S(1)}, bf16[48,1152]{1,0:T(8,128)(2,1)S(1)}, u32[]{:S(2)}, u32[]{:S(2)}) collective-permute-start(bf16[48,1152]{1,0:T(8,128)(2,1)S(1)} %get-tuple-element.46), channel_id=1, source_target_pairs={{2,0},{65,1},{4,2},{67,3},{6,4},{69,5},{0,6},{71,7},{10,8},{73,9},... | collective-permute-start | bytes 331784 | tf_op jit(solution)/shard_map/ppermute | solution.py:41
  120.9 4.7 %collective-permute-done.27.refs_1_ = bf16[48,1152]{1,0:T(8,128)(2,1)S(1)} collective-permute-done((bf16[48,1152]{1,0:T(8,128)(2,1)S(1)}, bf16[48,1152]{1,0:T(8,128)(2,1)S(1)}, u32[]{:S(2)}, u32[]{:S(2)}) %collective-permute-start.27) | collective-permute-done | bytes 110624 | tf_op jit(solution)/shard_map/ppermute | solution.py:41
  125.9 5.2 %shard_map.83 = bf16[256,1536]{1,0:T(8,128)(2,1)} custom-call(bf16[256,1152]{1,0:T(8,128)(2,1)S(1)} %get-tuple-element.35.eg_ref, bf16[1536,1152]{1,0:T(8,128)(2,1)S(1)} %get-tuple-element.36.w_ref, bf16[1536,1536]{1,0:T(8,128)(2,1)S(1)} %get-tuple-element.37.pick_ref), custom_call_target="tpu_custom_call" | custom-call | flops 2113929216 | tf_op jit(solution)/shard_map/pallas_call | solution.py:68
  131.1 1.9 %collective-permute-done.31.high_ref = bf16[18,1152]{1,0:T(8,128)(2,1)S(1)} collective-permute-done((bf16[18,1152]{1,0:T(8,128)(2,1)S(1)}, bf16[18,1152]{1,0:T(8,128)(2,1)S(1)}, u32[]{:S(2)}, u32[]{:S(2)}) %collective-permute-start.31) | collective-permute-done | bytes 41504 | tf_op jit(solution)/shard_map/ppermute | solution.py:41
  133.0 3.7 %collective-permute-start.32 = (bf16[6,1152]{1,0:T(8,128)(2,1)S(1)}, bf16[6,1152]{1,0:T(8,128)(2,1)S(1)}, u32[]{:S(2)}, u32[]{:S(2)}) collective-permute-start(bf16[6,1152]{1,0:T(8,128)(2,1)S(1)} %get-tuple-element.51), channel_id=1, source_target_pairs={{8,0},{9,1},{10,2},{11,3},{12,4},{13,5},{14,6},{15,7},{16,8},{17,9... | collective-permute-start | bytes 41480 | tf_op jit(solution)/shard_map/ppermute | solution.py:41
  136.7 3.3 %shard_map.84 = bf16[256,1152]{1,0:T(8,128)(2,1)} custom-call(f32[2]{0:T(128)S(1)} %pad_maximum_fusion.scalar_ref, bf16[256,1152]{1,0:T(8,128)(2,1)S(1)} %copy-done.3, bf16[256,1152]{1,0:T(8,128)(2,1)S(1)} %copy-done.1, bf16[256,1152]{1,0:T(8,128)(2,1)S(1)} %get-tuple-element.30.low_ref.p0, bf16[256,1152]{1,0:T(8,128)(2,1)S(1)} %collective-permute-done.17.p1, ...), custom_call_target="tpu_custom_call" | custom-call | flops 1207959552 | tf_op jit(solution)/shard_map/pallas_call | solution.py:68
  140.0 1.7 %collective-permute-done.33 = bf16[6,1152]{1,0:T(8,128)(2,1)S(1)} collective-permute-done((bf16[6,1152]{1,0:T(8,128)(2,1)S(1)}, bf16[6,1152]{1,0:T(8,128)(2,1)S(1)}, u32[]{:S(2)}, u32[]{:S(2)}) %collective-permute-start.33) | collective-permute-done | bytes 13856 | tf_op jit(solution)/shard_map/ppermute | solution.py:41
  141.7 0.6 convert_add_fusion
  (47 shorter events, 1.1 us)
Async XLA Ops:
  2.0 0.8 copy-start.2
  2.8 51.6 %copy-start = (bf16[256,1152]{1,0:T(8,128)(2,1)}, bf16[256,1152]{1,0:T(8,128)(2,1)S(1)}, u32[]{:S(2)}) copy-start(bf16[256,1152]{1,0:T(8,128)(2,1)S(1)} %get-tuple-element.33.t0.low_ref) | copy-start | bytes 1769476
  2.8 40.6 %collective-permute-start.14 = (bf16[256,1152]{1,0:T(8,128)(2,1)S(1)}, bf16[256,1152]{1,0:T(8,128)(2,1)}, u32[]{:S(2)}, u32[]{:S(2)}) collective-permute-start(bf16[256,1152]{1,0:T(8,128)(2,1)S(1)} %get-tuple-element.33.t0.low_ref), channel_id=1, source_target_pairs={{1,0},{2,1},{3,2},{4,3},{5,4},{6,5},{7,6},{8,7},{9,8},{10,9},{11,1... | collective-permute-start | bytes 1769480 | tf_op jit(solution)/shard_map/ppermute | solution.py:41
  10.5 5.4 %collective-permute-start = (bf16[6,1152]{1,0:T(8,128)(2,1)}, bf16[6,1152]{1,0:T(8,128)(2,1)S(1)}, u32[]{:S(2)}, u32[]{:S(2)}) collective-permute-start(bf16[6,1152]{1,0:T(8,128)(2,1)} %w_source.1), channel_id=1, source_target_pairs={{56,0},{57,1},{58,2},{59,3},{60,4},{61,5},{62,6},{63,7},{0,8},{1,9... | collective-permute-start | bytes 41480 | tf_op jit(solution)/shard_map/ppermute | solution.py:41
  10.5 9.4 %collective-permute-start.1 = (bf16[6,1152]{1,0:T(8,128)(2,1)}, bf16[6,1152]{1,0:T(8,128)(2,1)S(1)}, u32[]{:S(2)}, u32[]{:S(2)}) collective-permute-start(bf16[6,1152]{1,0:T(8,128)(2,1)} %w_source.1), channel_id=1, source_target_pairs={{8,0},{9,1},{10,2},{11,3},{12,4},{13,5},{14,6},{15,7},{16,8},{17,9... | collective-permute-start | bytes 41480 | tf_op jit(solution)/shard_map/ppermute | solution.py:41
  19.9 6.4 %collective-permute-start.2 = (bf16[18,1152]{1,0:T(8,128)(2,1)S(1)}, bf16[18,1152]{1,0:T(8,128)(2,1)S(1)}, u32[]{:S(2)}, u32[]{:S(2)}) collective-permute-start(bf16[18,1152]{1,0:T(8,128)(2,1)S(1)} %shard_map.78.refs_1_), channel_id=1, source_target_pairs={{48,0},{49,1},{50,2},{51,3},{52,4},{53,5},{54,6},{55,7},{56,8},{57... | collective-permute-start | bytes 124424 | tf_op jit(solution)/shard_map/ppermute | solution.py:41
  19.9 8.1 %collective-permute-start.3 = (bf16[18,1152]{1,0:T(8,128)(2,1)S(1)}, bf16[18,1152]{1,0:T(8,128)(2,1)S(1)}, u32[]{:S(2)}, u32[]{:S(2)}) collective-permute-start(bf16[18,1152]{1,0:T(8,128)(2,1)S(1)} %shard_map.78.refs_1_), channel_id=1, source_target_pairs={{24,0},{25,1},{26,2},{27,3},{28,4},{29,5},{30,6},{31,7},{32,8},{33... | collective-permute-start | bytes 124424 | tf_op jit(solution)/shard_map/ppermute | solution.py:41
  28.0 6.0 %collective-permute-start.4 = (bf16[48,1152]{1,0:T(8,128)(2,1)S(1)}, bf16[48,1152]{1,0:T(8,128)(2,1)S(1)}, u32[]{:S(2)}, u32[]{:S(2)}) collective-permute-start(bf16[48,1152]{1,0:T(8,128)(2,1)S(1)} %shard_map.79.refs_0_), channel_id=1, source_target_pairs={{2,0},{65,1},{4,2},{67,3},{6,4},{69,5},{0,6},{71,7},{10,8},{73,9},... | collective-permute-start | bytes 331784 | tf_op jit(solution)/shard_map/ppermute | solution.py:41
  28.1 7.6 %collective-permute-start.5 = (bf16[48,1152]{1,0:T(8,128)(2,1)S(1)}, bf16[48,1152]{1,0:T(8,128)(2,1)S(1)}, u32[]{:S(2)}, u32[]{:S(2)}) collective-permute-start(bf16[48,1152]{1,0:T(8,128)(2,1)S(1)} %shard_map.79.refs_0_), channel_id=1, source_target_pairs={{4,0},{129,1},{6,2},{131,3},{0,4},{133,5},{2,6},{135,7},{12,8},{13... | collective-permute-start | bytes 331784 | tf_op jit(solution)/shard_map/ppermute | solution.py:41
  28.2 10.9 %collective-permute-start.6 = (bf16[48,1152]{1,0:T(8,128)(2,1)S(1)}, bf16[48,1152]{1,0:T(8,128)(2,1)S(1)}, u32[]{:S(2)}, u32[]{:S(2)}) collective-permute-start(bf16[48,1152]{1,0:T(8,128)(2,1)S(1)} %shard_map.79.refs_0_), channel_id=1, source_target_pairs={{6,0},{193,1},{0,2},{195,3},{2,4},{197,5},{4,6},{199,7},{14,8},{20... | collective-permute-start | bytes 331784 | tf_op jit(solution)/shard_map/ppermute | solution.py:41
  39.2 9.6 %collective-permute-start.7 = (bf16[192,1152]{1,0:T(8,128)(2,1)S(1)}, bf16[192,1152]{1,0:T(8,128)(2,1)S(1)}, u32[]{:S(2)}, u32[]{:S(2)}) collective-permute-start(bf16[192,1152]{1,0:T(8,128)(2,1)S(1)} %shard_map.80.refs_0_), channel_id=1, source_target_pairs={{64,0},{3,1},{66,2},{5,3},{68,4},{7,5},{70,6},{1,7},{72,8},{11,9},... | collective-permute-start | bytes 1327112 | tf_op jit(solution)/shard_map/ppermute | solution.py:41
  39.9 14.5 %collective-permute-start.8 = (bf16[192,1152]{1,0:T(8,128)(2,1)S(1)}, bf16[192,1152]{1,0:T(8,128)(2,1)S(1)}, u32[]{:S(2)}, u32[]{:S(2)}) collective-permute-start(bf16[192,1152]{1,0:T(8,128)(2,1)S(1)} %shard_map.80.refs_0_), channel_id=1, source_target_pairs={{128,0},{5,1},{130,2},{7,3},{132,4},{1,5},{134,6},{3,7},{136,8},{1... | collective-permute-start | bytes 1327112 | tf_op jit(solution)/shard_map/ppermute | solution.py:41
  43.4 11.0 %collective-permute-start.9 = (bf16[192,1152]{1,0:T(8,128)(2,1)S(1)}, bf16[192,1152]{1,0:T(8,128)(2,1)S(1)}, u32[]{:S(2)}, u32[]{:S(2)}) collective-permute-start(bf16[192,1152]{1,0:T(8,128)(2,1)S(1)} %shard_map.80.refs_0_), channel_id=1, source_target_pairs={{192,0},{7,1},{194,2},{1,3},{196,4},{3,5},{198,6},{5,7},{200,8},{1... | collective-permute-start | bytes 1327112 | tf_op jit(solution)/shard_map/ppermute | solution.py:41
  43.4 11.6 %collective-permute-start.15 = (bf16[256,1152]{1,0:T(8,128)(2,1)}, bf16[256,1152]{1,0:T(8,128)(2,1)}, u32[]{:S(2)}, u32[]{:S(2)}) collective-permute-start(bf16[256,1152]{1,0:T(8,128)(2,1)} %collective-permute-done.14.t1), channel_id=1, source_target_pairs={{1,0},{2,1},{3,2},{4,3},{5,4},{6,5},{7,6},{8,7},{9,8},{10,9},{11,1... | collective-permute-start | bytes 1769480 | tf_op jit(solution)/shard_map/ppermute | solution.py:41
  43.4 22.5 %collective-permute-start.10 = (bf16[192,1152]{1,0:T(8,128)(2,1)S(1)}, bf16[192,1152]{1,0:T(8,128)(2,1)S(1)}, u32[]{:S(2)}, u32[]{:S(2)}) collective-permute-start(bf16[192,1152]{1,0:T(8,128)(2,1)S(1)} %shard_map.80.refs_0_), channel_id=1, source_target_pairs={{1,0},{0,1},{3,2},{2,3},{5,4},{4,5},{7,6},{6,7},{9,8},{8,9},{11,10... | collective-permute-start | bytes 1327112 | tf_op jit(solution)/shard_map/ppermute | solution.py:41
  48.7 17.2 %collective-permute-start.11 = (bf16[192,1152]{1,0:T(8,128)(2,1)S(1)}, bf16[192,1152]{1,0:T(8,128)(2,1)S(1)}, u32[]{:S(2)}, u32[]{:S(2)}) collective-permute-start(bf16[192,1152]{1,0:T(8,128)(2,1)S(1)} %collective-permute-done.7.refs_1_), channel_id=1, source_target_pairs={{1,0},{0,1},{3,2},{2,3},{5,4},{4,5},{7,6},{6,7},{9,8},{8,9},{11,10... | collective-permute-start | bytes 1327112 | tf_op jit(solution)/shard_map/ppermute | solution.py:41
  54.4 11.5 %collective-permute-start.12 = (bf16[192,1152]{1,0:T(8,128)(2,1)S(1)}, bf16[192,1152]{1,0:T(8,128)(2,1)S(1)}, u32[]{:S(2)}, u32[]{:S(2)}) collective-permute-start(bf16[192,1152]{1,0:T(8,128)(2,1)S(1)} %collective-permute-done.8.refs_2_), channel_id=1, source_target_pairs={{1,0},{0,1},{3,2},{2,3},{5,4},{4,5},{7,6},{6,7},{9,8},{8,9},{11,10... | collective-permute-start | bytes 1327112 | tf_op jit(solution)/shard_map/ppermute | solution.py:41
  54.4 11.5 %collective-permute-start.13 = (bf16[192,1152]{1,0:T(8,128)(2,1)S(1)}, bf16[192,1152]{1,0:T(8,128)(2,1)S(1)}, u32[]{:S(2)}, u32[]{:S(2)}) collective-permute-start(bf16[192,1152]{1,0:T(8,128)(2,1)S(1)} %collective-permute-done.9.refs_3_), channel_id=1, source_target_pairs={{1,0},{0,1},{3,2},{2,3},{5,4},{4,5},{7,6},{6,7},{9,8},{8,9},{11,10... | collective-permute-start | bytes 1327112 | tf_op jit(solution)/shard_map/ppermute | solution.py:41
  55.0 14.1 %collective-permute-start.16 = (bf16[256,1152]{1,0:T(8,128)(2,1)}, bf16[256,1152]{1,0:T(8,128)(2,1)S(1)}, u32[]{:S(2)}, u32[]{:S(2)}) collective-permute-start(bf16[256,1152]{1,0:T(8,128)(2,1)} %collective-permute-done.15.t2), channel_id=1, source_target_pairs={{1,0},{2,1},{3,2},{4,3},{5,4},{6,5},{7,6},{8,7},{9,8},{10,9},{11,1... | collective-permute-start | bytes 1769480 | tf_op jit(solution)/shard_map/ppermute | solution.py:41
  65.9 3.2 %copy-start.1 = (bf16[256,1152]{1,0:T(8,128)(2,1)S(1)}, bf16[256,1152]{1,0:T(8,128)(2,1)}, u32[]{:S(2)}) copy-start(bf16[256,1152]{1,0:T(8,128)(2,1)} %copy-done) | copy-start | bytes 1769476
  67.6 13.6 %collective-permute-start.17 = (bf16[256,1152]{1,0:T(8,128)(2,1)S(1)}, bf16[256,1152]{1,0:T(8,128)(2,1)S(1)}, u32[]{:S(2)}, u32[]{:S(2)}) collective-permute-start(bf16[256,1152]{1,0:T(8,128)(2,1)S(1)} %get-tuple-element.30.low_ref.p0), channel_id=1, source_target_pairs={{255,0},{0,1},{1,2},{2,3},{3,4},{4,5},{5,6},{6,7},{7,8},{8,9},{9,1... | collective-permute-start | bytes 1769480 | tf_op jit(solution)/shard_map/ppermute | solution.py:41
  72.9 8.3 %collective-permute-start.25 = (bf16[192,1152]{1,0:T(8,128)(2,1)S(1)}, bf16[192,1152]{1,0:T(8,128)(2,1)S(1)}, u32[]{:S(2)}, u32[]{:S(2)}) collective-permute-start(bf16[192,1152]{1,0:T(8,128)(2,1)S(1)} %get-tuple-element.42), channel_id=1, source_target_pairs={{1,0},{0,1},{3,2},{2,3},{5,4},{4,5},{7,6},{6,7},{9,8},{8,9},{11,10... | collective-permute-start | bytes 1327112 | tf_op jit(solution)/shard_map/ppermute | solution.py:41
  73.0 14.4 %collective-permute-start.23 = (bf16[192,1152]{1,0:T(8,128)(2,1)S(1)}, bf16[192,1152]{1,0:T(8,128)(2,1)S(1)}, u32[]{:S(2)}, u32[]{:S(2)}) collective-permute-start(bf16[192,1152]{1,0:T(8,128)(2,1)S(1)} %get-tuple-element.41), channel_id=1, source_target_pairs={{1,0},{0,1},{3,2},{2,3},{5,4},{4,5},{7,6},{6,7},{9,8},{8,9},{11,10... | collective-permute-start | bytes 1327112 | tf_op jit(solution)/shard_map/ppermute | solution.py:41
  73.5 21.1 %collective-permute-start.21 = (bf16[192,1152]{1,0:T(8,128)(2,1)S(1)}, bf16[192,1152]{1,0:T(8,128)(2,1)S(1)}, u32[]{:S(2)}, u32[]{:S(2)}) collective-permute-start(bf16[192,1152]{1,0:T(8,128)(2,1)S(1)} %get-tuple-element.40), channel_id=1, source_target_pairs={{1,0},{0,1},{3,2},{2,3},{5,4},{4,5},{7,6},{6,7},{9,8},{8,9},{11,10... | collective-permute-start | bytes 1327112 | tf_op jit(solution)/shard_map/ppermute | solution.py:41
  81.2 15.8 %collective-permute-start.18 = (bf16[256,1152]{1,0:T(8,128)(2,1)S(1)}, bf16[256,1152]{1,0:T(8,128)(2,1)S(1)}, u32[]{:S(2)}, u32[]{:S(2)}) collective-permute-start(bf16[256,1152]{1,0:T(8,128)(2,1)S(1)} %collective-permute-done.17.p1), channel_id=1, source_target_pairs={{255,0},{0,1},{1,2},{2,3},{3,4},{4,5},{5,6},{6,7},{7,8},{8,9},{9,1... | collective-permute-start | bytes 1769480 | tf_op jit(solution)/shard_map/ppermute | solution.py:41
  81.2 15.8 %collective-permute-start.20 = (bf16[192,1152]{1,0:T(8,128)(2,1)S(1)}, bf16[192,1152]{1,0:T(8,128)(2,1)S(1)}, u32[]{:S(2)}, u32[]{:S(2)}) collective-permute-start(bf16[192,1152]{1,0:T(8,128)(2,1)S(1)} %get-tuple-element.39), channel_id=1, source_target_pairs={{1,0},{0,1},{3,2},{2,3},{5,4},{4,5},{7,6},{6,7},{9,8},{8,9},{11,10... | collective-permute-start | bytes 1327112 | tf_op jit(solution)/shard_map/ppermute | solution.py:41
  81.5 17.5 %collective-permute-start.26 = (bf16[192,1152]{1,0:T(8,128)(2,1)S(1)}, bf16[192,1152]{1,0:T(8,128)(2,1)S(1)}, u32[]{:S(2)}, u32[]{:S(2)}) collective-permute-start(bf16[192,1152]{1,0:T(8,128)(2,1)S(1)} %shard_map.88), channel_id=1, source_target_pairs={{64,0},{3,1},{66,2},{5,3},{68,4},{7,5},{70,6},{1,7},{72,8},{11,9},... | collective-permute-start | bytes 1327112 | tf_op jit(solution)/shard_map/ppermute | solution.py:41
  87.7 17.5 %collective-permute-start.24 = (bf16[192,1152]{1,0:T(8,128)(2,1)S(1)}, bf16[192,1152]{1,0:T(8,128)(2,1)S(1)}, u32[]{:S(2)}, u32[]{:S(2)}) collective-permute-start(bf16[192,1152]{1,0:T(8,128)(2,1)S(1)} %shard_map.87), channel_id=1, source_target_pairs={{128,0},{5,1},{130,2},{7,3},{132,4},{1,5},{134,6},{3,7},{136,8},{1... | collective-permute-start | bytes 1327112 | tf_op jit(solution)/shard_map/ppermute | solution.py:41
  94.9 22.5 %collective-permute-start.22 = (bf16[192,1152]{1,0:T(8,128)(2,1)S(1)}, bf16[192,1152]{1,0:T(8,128)(2,1)S(1)}, u32[]{:S(2)}, u32[]{:S(2)}) collective-permute-start(bf16[192,1152]{1,0:T(8,128)(2,1)S(1)} %shard_map.86), channel_id=1, source_target_pairs={{192,0},{7,1},{194,2},{1,3},{196,4},{3,5},{198,6},{5,7},{200,8},{1... | collective-permute-start | bytes 1327112 | tf_op jit(solution)/shard_map/ppermute | solution.py:41
  97.0 39.8 %collective-permute-start.19 = (bf16[256,1152]{1,0:T(8,128)(2,1)S(1)}, bf16[256,1152]{1,0:T(8,128)(2,1)S(1)}, u32[]{:S(2)}, u32[]{:S(2)}) collective-permute-start(bf16[256,1152]{1,0:T(8,128)(2,1)S(1)} %collective-permute-done.18.p2), channel_id=1, source_target_pairs={{255,0},{0,1},{1,2},{2,3},{3,4},{4,5},{5,6},{6,7},{7,8},{8,9},{9,1... | collective-permute-start | bytes 1769480 | tf_op jit(solution)/shard_map/ppermute | solution.py:41
  117.5 8.1 %collective-permute-start.27 = (bf16[48,1152]{1,0:T(8,128)(2,1)S(1)}, bf16[48,1152]{1,0:T(8,128)(2,1)S(1)}, u32[]{:S(2)}, u32[]{:S(2)}) collective-permute-start(bf16[48,1152]{1,0:T(8,128)(2,1)S(1)} %get-tuple-element.44), channel_id=1, source_target_pairs={{6,0},{193,1},{0,2},{195,3},{2,4},{197,5},{4,6},{199,7},{14,8},{20... | collective-permute-start | bytes 331784 | tf_op jit(solution)/shard_map/ppermute | solution.py:41
  117.6 8.0 %collective-permute-start.28 = (bf16[48,1152]{1,0:T(8,128)(2,1)S(1)}, bf16[48,1152]{1,0:T(8,128)(2,1)S(1)}, u32[]{:S(2)}, u32[]{:S(2)}) collective-permute-start(bf16[48,1152]{1,0:T(8,128)(2,1)S(1)} %get-tuple-element.45), channel_id=1, source_target_pairs={{4,0},{129,1},{6,2},{131,3},{0,4},{133,5},{2,6},{135,7},{12,8},{13... | collective-permute-start | bytes 331784 | tf_op jit(solution)/shard_map/ppermute | solution.py:41
  117.7 7.9 %collective-permute-start.29 = (bf16[48,1152]{1,0:T(8,128)(2,1)S(1)}, bf16[48,1152]{1,0:T(8,128)(2,1)S(1)}, u32[]{:S(2)}, u32[]{:S(2)}) collective-permute-start(bf16[48,1152]{1,0:T(8,128)(2,1)S(1)} %get-tuple-element.46), channel_id=1, source_target_pairs={{2,0},{65,1},{4,2},{67,3},{6,4},{69,5},{0,6},{71,7},{10,8},{73,9},... | collective-permute-start | bytes 331784 | tf_op jit(solution)/shard_map/ppermute | solution.py:41
  125.7 7.2 %collective-permute-start.31 = (bf16[18,1152]{1,0:T(8,128)(2,1)S(1)}, bf16[18,1152]{1,0:T(8,128)(2,1)S(1)}, u32[]{:S(2)}, u32[]{:S(2)}) collective-permute-start(bf16[18,1152]{1,0:T(8,128)(2,1)S(1)} %get-tuple-element.49), channel_id=1, source_target_pairs={{40,0},{41,1},{42,2},{43,3},{44,4},{45,5},{46,6},{47,7},{48,8},{49... | collective-permute-start | bytes 124424 | tf_op jit(solution)/shard_map/ppermute | solution.py:41
  125.8 5.3 %collective-permute-start.30 = (bf16[12,1152]{1,0:T(8,128)(2,1)S(1)}, bf16[12,1152]{1,0:T(8,128)(2,1)S(1)}, u32[]{:S(2)}, u32[]{:S(2)}) collective-permute-start(bf16[12,1152]{1,0:T(8,128)(2,1)S(1)} %get-tuple-element.48), channel_id=1, source_target_pairs={{16,0},{17,1},{18,2},{19,3},{20,4},{21,5},{22,6},{23,7},{24,8},{25... | collective-permute-start | bytes 82952 | tf_op jit(solution)/shard_map/ppermute | solution.py:41
  125.9 10.8 %copy-start.3 = (bf16[256,1152]{1,0:T(8,128)(2,1)S(1)}, bf16[256,1152]{1,0:T(8,128)(2,1)}, u32[]{:S(2)}) copy-start(bf16[256,1152]{1,0:T(8,128)(2,1)} %copy-done.2) | copy-start | bytes 1769476
  133.0 7.0 %collective-permute-start.32 = (bf16[6,1152]{1,0:T(8,128)(2,1)S(1)}, bf16[6,1152]{1,0:T(8,128)(2,1)S(1)}, u32[]{:S(2)}, u32[]{:S(2)}) collective-permute-start(bf16[6,1152]{1,0:T(8,128)(2,1)S(1)} %get-tuple-element.51), channel_id=1, source_target_pairs={{8,0},{9,1},{10,2},{11,3},{12,4},{13,5},{14,6},{15,7},{16,8},{17,9... | collective-permute-start | bytes 41480 | tf_op jit(solution)/shard_map/ppermute | solution.py:41
  136.7 5.0 %collective-permute-start.33 = (bf16[6,1152]{1,0:T(8,128)(2,1)S(1)}, bf16[6,1152]{1,0:T(8,128)(2,1)S(1)}, u32[]{:S(2)}, u32[]{:S(2)}) collective-permute-start(bf16[6,1152]{1,0:T(8,128)(2,1)S(1)} %get-tuple-element.52), channel_id=1, source_target_pairs={{56,0},{57,1},{58,2},{59,3},{60,4},{61,5},{62,6},{63,7},{0,8},{1,9... | collective-permute-start | bytes 41480 | tf_op jit(solution)/shard_map/ppermute | solution.py:41

commit v5 on v4

--- a/solution.py
+++ b/solution.py
@@ -156,7 +156,7 @@
     return (-scale * polarity * jax.nn.sigmoid(-polarity * logits)).astype(BF16)
 
 
-def image_body(scalar_ref, low_ref, unit_ref, length_ref, t0, t1, t2, t3, xpt_ref, eg_ref, s0, s1, s2, s3, grad, pair):
+def image_body(scalar_ref, low_ref, unit_ref, length_ref, t0, t1, t2, t3, eg_ref, grad, pair):
     scale, bias = scalar_ref[0], scalar_ref[1]
     texts = (t0, t1, t2, t3)
     for k, text in enumerate(texts):
@@ -170,8 +170,10 @@
         grad[:, cols] = part
         inner = inner + jnp.sum(part * unit_ref[:, cols], axis=1, keepdims=True)
     eg_ref[...] = ((grad[...] - unit_ref[...] * inner) / length_ref[...]).astype(BF16)
-    for i, out in enumerate((s0, s1, s2, s3)):
-        out[...] = mm(xpt_ref[pl.ds(HALF + i * PIECE, PIECE), :], eg_ref[...]).astype(BF16)
+
+
+def sibling_body(xpt_ref, eg_ref, out, *, piece):
+    out[...] = mm(xpt_ref[pl.ds(HALF + piece * PIECE, PIECE), :], eg_ref[...]).astype(BF16)
 
 
 def weight_body(xpt_ref, eg_ref, came_ref, out, *, piece):
@@ -201,18 +203,27 @@
         out_ref[:, cols] = mm(mixed[...], pick_ref[:, cols]).astype(BF16)
 
 
-def text_grad_body(scalar_ref, raw_ref, low_ref, p0, p1, p2, p3, out_ref, grad, pair):
+def text_part_body(scalar_ref, low_ref, p0, p1, p2, grad_ref, pair):
     scale, bias = scalar_ref[0], scalar_ref[1]
-    images = (p0, p1, p2, p3)
+    images = (p0, p1, p2)
     for k, image in enumerate(images):
         pair[k] = derivative(low_ref[...], image[...], scale, bias, k == 0)
+    for at in range(0, E, COLS):
+        cols = pl.ds(at, COLS)
+        part = mm(pair[0], p0[:, cols])
+        for k in range(1, S - 1):
+            part = part + mm(pair[k], images[k][:, cols])
+        grad_ref[:, cols] = part
+
+
+def text_grad_body(scalar_ref, raw_ref, low_ref, p3, part_ref, out_ref, grad):
+    scale, bias = scalar_ref[0], scalar_ref[1]
+    pair = derivative(low_ref[...], p3[...], scale, bias, False)
     length = length_of(raw_ref[...].astype(F32))
     inner = jnp.zeros((R, 1), F32)
     for at in range(0, E, COLS):
         cols = pl.ds(at, COLS)
-        part = mm(pair[0], p0[:, cols])
-        for k in range(1, S):
-            part = part + mm(pair[k], images[k][:, cols])
+        part = part_ref[:, cols] + mm(pair, p3[:, cols])
         grad[:, cols] = part
         inner = inner + jnp.sum(part * (raw_ref[:, cols].astype(F32) / length), axis=1, keepdims=True)
     out_ref[...] = ((grad[...] - raw_ref[...].astype(F32) / length * inner) / length).astype(BF16)
@@ -292,11 +303,14 @@
     for _ in range(1, S):
         images.append(fetch(images[-1], along_blocks(-1)))
     work = [pltpu.VMEM((R, E), F32), pltpu.VMEM((S, R, R), BF16)]
-    eg, *sent = call(
-        image_body, [((R, E), BF16)] + [((PIECE, E), BF16)] * 4, scalars, low, unit, length, *texts, xpt,
-        flops=16 * R * R * E + 2 * R * HALF * E, scratch=work, smem=(0,),
-    )
-    came = [fetch(piece, sibling) for piece in sent]
+    (eg,) = call(
+        image_body, [((R, E), BF16)], scalars, low, unit, length, *texts,
+        flops=16 * R * R * E, scratch=work, smem=(0,),
+    )
+    came = []
+    for i in range(4):
+        (sent,) = call(functools.partial(sibling_body, piece=i), [((PIECE, E), BF16)], xpt, eg, flops=2 * R * PIECE * E)
+        came.append(fetch(sent, sibling))
     (grad_features,) = call(
         features_body, [((R, D), BF16)], eg, full, pick, flops=2 * R * D * E + 2 * R * D * D,
         scratch=[pltpu.VMEM((R, D), BF16)], final=True,
@@ -307,9 +321,13 @@
             functools.partial(weight_body, piece=i), [((PIECE, E), BF16)], xpt, eg, came[i], flops=2 * R * PIECE * E
         )
     grad_weight = scatter_weight(pieces)
+    (part,) = call(
+        text_part_body, [((R, E), F32)], scalars, text_low, *images[:3],
+        flops=12 * R * R * E, scratch=[pltpu.VMEM((S - 1, R, R), BF16)], smem=(0,),
+    )
     (grad_text,) = call(
-        text_grad_body, [((R, E), BF16)], scalars, text_raw, text_low, *images,
-        flops=16 * R * R * E, scratch=work, smem=(0,), final=True,
+        text_grad_body, [((R, E), BF16)], scalars, text_raw, text_low, images[3], part,
+        flops=4 * R * R * E, scratch=work[:1], smem=(0,), final=True,
     )
     return grad_features, grad_text, grad_weight
 

time: 142 us -> 135 us (0.951)
  the two profiles are of different devices: /device:TPU:24 before, /device:TPU:6 now
where the time goes in v5:
time: 135 us
  starting transfers between devices  62.7 us (46%)
  waiting for transfers between devices  43.2 us (32%)
  Pallas kernels  25.9 us (19%)
  between operations  2.18 us (2%)
    ppermute x34, starting transfers between devices, fetch(): lax.ppermute(value, AXES, [(index(*where(*coords(i))), i) for i in range(...  62.7 us
    ppermute x34, waiting for transfers between devices, fetch(): lax.ppermute(value, AXES, [(index(*where(*coords(i))), i) for i in range(...  43.2 us
    pallas_call x21, Pallas kernels, call(): pl.pallas_call(body, out_shape=[jax.ShapeDtypeStruct(s, d) if final else...  25.9 us
  transfers between devices with their start and end apart: 34, of which 17 were waited for; matrix products, arithmetic and copies ran while one was open for 1% of the time, Pallas kernels for 16%

profile of v5, /device:TPU:6, one launch (start us, length us, event | category | flops | bytes accessed | tf_op | source)
XLA Modules:
  0.0 134.8 jit_solution(17332987607027754359)
XLA Ops:
  0.6 1.3 shard_map.77
  2.0 0.3 collective-permute-start.14
  2.3 1.9 %collective-permute-start = (bf16[6,1152]{1,0:T(8,128)(2,1)}, bf16[6,1152]{1,0:T(8,128)(2,1)S(1)}, u32[]{:S(2)}, u32[]{:S(2)}) collective-permute-start(bf16[6,1152]{1,0:T(8,128)(2,1)} %w_source.1), channel_id=1, source_target_pairs={{56,0},{57,1},{58,2},{59,3},{60,4},{61,5},{62,6},{63,7},{0,8},{1,9... | collective-permute-start | bytes 41480 | tf_op jit(solution)/shard_map/ppermute | solution.py:41
  4.2 3.9 %collective-permute-start.1 = (bf16[6,1152]{1,0:T(8,128)(2,1)}, bf16[6,1152]{1,0:T(8,128)(2,1)S(1)}, u32[]{:S(2)}, u32[]{:S(2)}) collective-permute-start(bf16[6,1152]{1,0:T(8,128)(2,1)} %w_source.1), channel_id=1, source_target_pairs={{8,0},{9,1},{10,2},{11,3},{12,4},{13,5},{14,6},{15,7},{16,8},{17,9... | collective-permute-start | bytes 41480 | tf_op jit(solution)/shard_map/ppermute | solution.py:41
  8.2 1.9 %collective-permute-done.refs_0_ = bf16[6,1152]{1,0:T(8,128)(2,1)S(1)} collective-permute-done((bf16[6,1152]{1,0:T(8,128)(2,1)}, bf16[6,1152]{1,0:T(8,128)(2,1)S(1)}, u32[]{:S(2)}, u32[]{:S(2)}) %collective-permute-start) | collective-permute-done | bytes 13856 | tf_op jit(solution)/shard_map/ppermute | solution.py:41
  10.1 2.6 %collective-permute-start.2 = (bf16[18,1152]{1,0:T(8,128)(2,1)S(1)}, bf16[18,1152]{1,0:T(8,128)(2,1)S(1)}, u32[]{:S(2)}, u32[]{:S(2)}) collective-permute-start(bf16[18,1152]{1,0:T(8,128)(2,1)S(1)} %shard_map.78.refs_1_), channel_id=1, source_target_pairs={{48,0},{49,1},{50,2},{51,3},{52,4},{53,5},{54,6},{55,7},{56,8},{57... | collective-permute-start | bytes 124424 | tf_op jit(solution)/shard_map/ppermute | solution.py:41
  12.7 3.1 %collective-permute-start.3 = (bf16[18,1152]{1,0:T(8,128)(2,1)S(1)}, bf16[18,1152]{1,0:T(8,128)(2,1)S(1)}, u32[]{:S(2)}, u32[]{:S(2)}) collective-permute-start(bf16[18,1152]{1,0:T(8,128)(2,1)S(1)} %shard_map.78.refs_1_), channel_id=1, source_target_pairs={{24,0},{25,1},{26,2},{27,3},{28,4},{29,5},{30,6},{31,7},{32,8},{33... | collective-permute-start | bytes 124424 | tf_op jit(solution)/shard_map/ppermute | solution.py:41
  15.8 0.7 collective-permute-done.2.refs_0_
  16.5 2.2 %collective-permute-done.3.refs_2_ = bf16[18,1152]{1,0:T(8,128)(2,1)S(1)} collective-permute-done((bf16[18,1152]{1,0:T(8,128)(2,1)S(1)}, bf16[18,1152]{1,0:T(8,128)(2,1)S(1)}, u32[]{:S(2)}, u32[]{:S(2)}) %collective-permute-start.3) | collective-permute-done | bytes 41504 | tf_op jit(solution)/shard_map/ppermute | solution.py:41
  18.8 0.8 collective-permute-start.4
  19.6 11.9 %collective-permute-start.5 = (bf16[48,1152]{1,0:T(8,128)(2,1)S(1)}, bf16[48,1152]{1,0:T(8,128)(2,1)S(1)}, u32[]{:S(2)}, u32[]{:S(2)}) collective-permute-start(bf16[48,1152]{1,0:T(8,128)(2,1)S(1)} %shard_map.79.refs_0_), channel_id=1, source_target_pairs={{4,0},{129,1},{6,2},{131,3},{0,4},{133,5},{2,6},{135,7},{12,8},{13... | collective-permute-start | bytes 331784 | tf_op jit(solution)/shard_map/ppermute | solution.py:41
  31.4 1.2 collective-permute-done.4.refs_1_
  32.7 4.2 %collective-permute-done.5.refs_2_ = bf16[48,1152]{1,0:T(8,128)(2,1)S(1)} collective-permute-done((bf16[48,1152]{1,0:T(8,128)(2,1)S(1)}, bf16[48,1152]{1,0:T(8,128)(2,1)S(1)}, u32[]{:S(2)}, u32[]{:S(2)}) %collective-permute-start.5) | collective-permute-done | bytes 110624 | tf_op jit(solution)/shard_map/ppermute | solution.py:41
  36.9 1.0 collective-permute-start.7
  37.9 0.6 collective-permute-start.8
  38.4 1.0 collective-permute-start.9
  39.4 6.0 %collective-permute-done.7.refs_1_ = bf16[192,1152]{1,0:T(8,128)(2,1)} collective-permute-done((bf16[192,1152]{1,0:T(8,128)(2,1)S(1)}, bf16[192,1152]{1,0:T(8,128)(2,1)}, u32[]{:S(2)}, u32[]{:S(2)}) %collective-permute-start.7) | collective-permute-done | bytes 442400 | tf_op jit(solution)/shard_map/ppermute | solution.py:41
  45.4 1.0 collective-permute-start.11
  46.4 1.5 %collective-permute-done.8.refs_2_ = bf16[192,1152]{1,0:T(8,128)(2,1)} collective-permute-done((bf16[192,1152]{1,0:T(8,128)(2,1)S(1)}, bf16[192,1152]{1,0:T(8,128)(2,1)}, u32[]{:S(2)}, u32[]{:S(2)}) %collective-permute-start.8) | collective-permute-done | bytes 442400 | tf_op jit(solution)/shard_map/ppermute | solution.py:41
  47.9 3.2 %collective-permute-start.12 = (bf16[192,1152]{1,0:T(8,128)(2,1)}, bf16[192,1152]{1,0:T(8,128)(2,1)}, u32[]{:S(2)}, u32[]{:S(2)}) collective-permute-start(bf16[192,1152]{1,0:T(8,128)(2,1)} %collective-permute-done.8.refs_2_), channel_id=1, source_target_pairs={{1,0},{0,1},{3,2},{2,3},{5,4},{4,5},{7,6},{6,7},{9,8},{8,9},{11,10... | collective-permute-start | bytes 1327112 | tf_op jit(solution)/shard_map/ppermute | solution.py:41
  51.1 1.5 %collective-permute-done.9.refs_3_ = bf16[192,1152]{1,0:T(8,128)(2,1)} collective-permute-done((bf16[192,1152]{1,0:T(8,128)(2,1)S(1)}, bf16[192,1152]{1,0:T(8,128)(2,1)}, u32[]{:S(2)}, u32[]{:S(2)}) %collective-permute-start.9) | collective-permute-done | bytes 442400 | tf_op jit(solution)/shard_map/ppermute | solution.py:41
  54.0 6.2 %shard_map.76 = (bf16[1536,1536]{1,0:T(8,128)(2,1)S(1)}, bf16[256,1536]{1,0:T(8,128)(2,1)S(1)}, bf16[1536,256]{1,0:T(8,128)(2,1)S(1)}) custom-call(s32[4]{0:T(128)S(1)} %pad_add_fusion.coord_ref, bf16[256,1536]{1,0:T(8,128)(2,1)} %source_ref.1), custom_call_target="tpu_custom_call" | custom-call | flops 2415919104 | tf_op jit(solution)/shard_map/pallas_call | solution.py:68
  60.2 3.4 %shard_map.81 = (bf16[1536,1152]{1,0:T(8,128)(2,1)S(1)}, f32[256,1152]{1,0:T(8,128)S(1)}, bf16[256,1152]{1,0:T(8,128)(2,1)S(1)}, f32[256,1]{1,0:T(8,128)S(1)}) custom-call(bf16[256,1536]{1,0:T(8,128)(2,1)S(1)} %get-tuple-element.23.xp_ref, bf16[192,1152]{1,0:T(8,128)(2,1)S(1)} %shard_map.80.refs_0_, bf16[192,1152]{1,0:T(8,128)(2,1)} %collective-permute-done.7.refs_1_, ...), custom_call_target="tpu_custom_call" | custom-call | flops 905969664 | tf_op jit(solution)/shard_map/pallas_call | solution.py:68
  63.7 0.6 collective-permute-start.17
  64.4 2.4 %shard_map.82.eg_ref = bf16[256,1152]{1,0:T(8,128)(2,1)S(1)} custom-call(f32[2]{0:T(128)S(1)} %pad_maximum_fusion.scalar_ref, bf16[256,1152]{1,0:T(8,128)(2,1)S(1)} %get-tuple-element.25.low_ref.p0, f32[256,1152]{1,0:T(8,128)S(1)} %get-tuple-element.26.unit_ref, f32[256,1]{1,0:T(8,128)S(1)} %get-tuple-element.27.length_ref, ...), custom_call_target="tpu_custom_call" | custom-call | flops 1207959552 | tf_op jit(solution)/shard_map/pallas_call | solution.py:68
  67.1 3.9 %collective-permute-start.25 = (bf16[192,1152]{1,0:T(8,128)(2,1)S(1)}, bf16[192,1152]{1,0:T(8,128)(2,1)S(1)}, u32[]{:S(2)}, u32[]{:S(2)}) collective-permute-start(bf16[192,1152]{1,0:T(8,128)(2,1)S(1)} %shard_map.92), channel_id=1, source_target_pairs={{1,0},{0,1},{3,2},{2,3},{5,4},{4,5},{7,6},{6,7},{9,8},{8,9},{11,10... | collective-permute-start | bytes 1327112 | tf_op jit(solution)/shard_map/ppermute | solution.py:41
  71.7 0.6 collective-permute-start.21
  72.3 0.8 collective-permute-done.17.p1
  73.1 1.9 %collective-permute-start.18 = (bf16[256,1152]{1,0:T(8,128)(2,1)S(1)}, bf16[256,1152]{1,0:T(8,128)(2,1)S(1)}, u32[]{:S(2)}, u32[]{:S(2)}) collective-permute-start(bf16[256,1152]{1,0:T(8,128)(2,1)S(1)} %collective-permute-done.17.p1), channel_id=1, source_target_pairs={{255,0},{0,1},{1,2},{2,3},{3,4},{4,5},{5,6},{6,7},{7,8},{8,9},{9,1... | collective-permute-start | bytes 1769480 | tf_op jit(solution)/shard_map/ppermute | solution.py:41
  75.3 4.7 %collective-permute-start.20 = (bf16[192,1152]{1,0:T(8,128)(2,1)S(1)}, bf16[192,1152]{1,0:T(8,128)(2,1)S(1)}, u32[]{:S(2)}, u32[]{:S(2)}) collective-permute-start(bf16[192,1152]{1,0:T(8,128)(2,1)S(1)} %shard_map.86), channel_id=1, source_target_pairs={{1,0},{0,1},{3,2},{2,3},{5,4},{4,5},{7,6},{6,7},{9,8},{8,9},{11,10... | collective-permute-start | bytes 1327112 | tf_op jit(solution)/shard_map/ppermute | solution.py:41
  80.2 0.7 collective-permute-start.26
  81.2 0.7 collective-permute-start.24
  82.2 1.2 collective-permute-start.22
  83.7 4.9 %collective-permute-done.26.refs_3_ = bf16[192,1152]{1,0:T(8,128)(2,1)S(1)} collective-permute-done((bf16[192,1152]{1,0:T(8,128)(2,1)S(1)}, bf16[192,1152]{1,0:T(8,128)(2,1)S(1)}, u32[]{:S(2)}, u32[]{:S(2)}) %collective-permute-start.26) | collective-permute-done | bytes 442400 | tf_op jit(solution)/shard_map/ppermute | solution.py:41
  88.6 2.6 %collective-permute-done.24.refs_2_ = bf16[192,1152]{1,0:T(8,128)(2,1)S(1)} collective-permute-done((bf16[192,1152]{1,0:T(8,128)(2,1)S(1)}, bf16[192,1152]{1,0:T(8,128)(2,1)S(1)}, u32[]{:S(2)}, u32[]{:S(2)}) %collective-permute-start.24) | collective-permute-done | bytes 442400 | tf_op jit(solution)/shard_map/ppermute | solution.py:41
  91.2 4.6 %collective-permute-done.22.refs_1_ = bf16[192,1152]{1,0:T(8,128)(2,1)S(1)} collective-permute-done((bf16[192,1152]{1,0:T(8,128)(2,1)S(1)}, bf16[192,1152]{1,0:T(8,128)(2,1)S(1)}, u32[]{:S(2)}, u32[]{:S(2)}) %collective-permute-start.22) | collective-permute-done | bytes 442400 | tf_op jit(solution)/shard_map/ppermute | solution.py:41
  96.1 12.3 %collective-permute-start.27 = (bf16[48,1152]{1,0:T(8,128)(2,1)S(1)}, bf16[48,1152]{1,0:T(8,128)(2,1)S(1)}, u32[]{:S(2)}, u32[]{:S(2)}) collective-permute-start(bf16[48,1152]{1,0:T(8,128)(2,1)S(1)} %get-tuple-element.34), channel_id=1, source_target_pairs={{6,0},{193,1},{0,2},{195,3},{2,4},{197,5},{4,6},{199,7},{14,8},{20... | collective-permute-start | bytes 331784 | tf_op jit(solution)/shard_map/ppermute | solution.py:41
  108.4 1.0 collective-permute-start.29
  109.4 2.5 %collective-permute-done.27.refs_1_ = bf16[48,1152]{1,0:T(8,128)(2,1)S(1)} collective-permute-done((bf16[48,1152]{1,0:T(8,128)(2,1)S(1)}, bf16[48,1152]{1,0:T(8,128)(2,1)S(1)}, u32[]{:S(2)}, u32[]{:S(2)}) %collective-permute-start.27) | collective-permute-done | bytes 110624 | tf_op jit(solution)/shard_map/ppermute | solution.py:41
  111.9 2.9 %collective-permute-done.28.refs_2_ = bf16[48,1152]{1,0:T(8,128)(2,1)S(1)} collective-permute-done((bf16[48,1152]{1,0:T(8,128)(2,1)S(1)}, bf16[48,1152]{1,0:T(8,128)(2,1)S(1)}, u32[]{:S(2)}, u32[]{:S(2)}) %collective-permute-start.28) | collective-permute-done | bytes 110624 | tf_op jit(solution)/shard_map/ppermute | solution.py:41
  114.8 0.8 collective-permute-done.29.refs_3_
  115.8 5.2 %shard_map.83 = bf16[256,1536]{1,0:T(8,128)(2,1)} custom-call(bf16[256,1152]{1,0:T(8,128)(2,1)S(1)} %shard_map.82.eg_ref, bf16[1536,1152]{1,0:T(8,128)(2,1)S(1)} %get-tuple-element.29.w_ref, bf16[1536,1536]{1,0:T(8,128)(2,1)S(1)} %get-tuple-element.30.pick_ref), custom_call_target="tpu_custom_call" | custom-call | flops 2113929216 | tf_op jit(solution)/shard_map/pallas_call | solution.py:68
  121.0 1.9 %collective-permute-done.31.high_ref = bf16[18,1152]{1,0:T(8,128)(2,1)S(1)} collective-permute-done((bf16[18,1152]{1,0:T(8,128)(2,1)S(1)}, bf16[18,1152]{1,0:T(8,128)(2,1)S(1)}, u32[]{:S(2)}, u32[]{:S(2)}) %collective-permute-start.31) | collective-permute-done | bytes 41504 | tf_op jit(solution)/shard_map/ppermute | solution.py:41
  122.9 3.7 %collective-permute-start.32 = (bf16[6,1152]{1,0:T(8,128)(2,1)S(1)}, bf16[6,1152]{1,0:T(8,128)(2,1)S(1)}, u32[]{:S(2)}, u32[]{:S(2)}) collective-permute-start(bf16[6,1152]{1,0:T(8,128)(2,1)S(1)} %get-tuple-element.41), channel_id=1, source_target_pairs={{8,0},{9,1},{10,2},{11,3},{12,4},{13,5},{14,6},{15,7},{16,8},{17,9... | collective-permute-start | bytes 41480 | tf_op jit(solution)/shard_map/ppermute | solution.py:41
  126.6 1.9 %shard_map.84.part_ref = f32[256,1152]{1,0:T(8,128)S(1)} custom-call(f32[2]{0:T(128)S(1)} %pad_maximum_fusion.scalar_ref, bf16[256,1152]{1,0:T(8,128)(2,1)S(1)} %get-tuple-element.28.t0.low_ref, bf16[256,1152]{1,0:T(8,128)(2,1)S(1)} %get-tuple-element.25.low_ref.p0, bf16[256,1152]{1,0:T(8,128)(2,1)S(1)} %collective-permute-done.17.p1, ...), custom_call_target="tpu_custom_call" | custom-call | flops 905969664 | tf_op jit(solution)/shard_map/pallas_call | solution.py:68
  128.5 3.0 %collective-permute-done.33 = bf16[6,1152]{1,0:T(8,128)(2,1)S(1)} collective-permute-done((bf16[6,1152]{1,0:T(8,128)(2,1)S(1)}, bf16[6,1152]{1,0:T(8,128)(2,1)S(1)}, u32[]{:S(2)}, u32[]{:S(2)}) %collective-permute-start.33) | collective-permute-done | bytes 13856 | tf_op jit(solution)/shard_map/ppermute | solution.py:41
  131.6 0.6 convert_add_fusion
  132.2 2.6 %shard_map.85 = bf16[256,1152]{1,0:T(8,128)(2,1)} custom-call(f32[2]{0:T(128)S(1)} %pad_maximum_fusion.scalar_ref, bf16[256,1152]{1,0:T(8,128)(2,1)S(1)} %get-tuple-element.31.raw_ref, bf16[256,1152]{1,0:T(8,128)(2,1)S(1)} %get-tuple-element.28.t0.low_ref, bf16[256,1152]{1,0:T(8,128)(2,1)S(1)} %collective-permute-done.19.p3, f32[256,1152]{1,0:T(8,128)S(1)} %shard_map.84.part_ref), custom_call_target="tpu_custom_call" | custom-call | flops 301989888 | tf_op jit(solution)/shard_map/pallas_call | solution.py:68
  (44 shorter events, 3.3 us)
Async XLA Ops:
  2.0 29.5 %collective-permute-start.14 = (bf16[256,1152]{1,0:T(8,128)(2,1)S(1)}, bf16[256,1152]{1,0:T(8,128)(2,1)S(1)}, u32[]{:S(2)}, u32[]{:S(2)}) collective-permute-start(bf16[256,1152]{1,0:T(8,128)(2,1)S(1)} %get-tuple-element.28.t0.low_ref), channel_id=1, source_target_pairs={{1,0},{2,1},{3,2},{4,3},{5,4},{6,5},{7,6},{8,7},{9,8},{10,9},{11,1... | collective-permute-start | bytes 1769480 | tf_op jit(solution)/shard_map/ppermute | solution.py:41
  2.3 7.8 %collective-permute-start = (bf16[6,1152]{1,0:T(8,128)(2,1)}, bf16[6,1152]{1,0:T(8,128)(2,1)S(1)}, u32[]{:S(2)}, u32[]{:S(2)}) collective-permute-start(bf16[6,1152]{1,0:T(8,128)(2,1)} %w_source.1), channel_id=1, source_target_pairs={{56,0},{57,1},{58,2},{59,3},{60,4},{61,5},{62,6},{63,7},{0,8},{1,9... | collective-permute-start | bytes 41480 | tf_op jit(solution)/shard_map/ppermute | solution.py:41
  4.2 5.9 %collective-permute-start.1 = (bf16[6,1152]{1,0:T(8,128)(2,1)}, bf16[6,1152]{1,0:T(8,128)(2,1)S(1)}, u32[]{:S(2)}, u32[]{:S(2)}) collective-permute-start(bf16[6,1152]{1,0:T(8,128)(2,1)} %w_source.1), channel_id=1, source_target_pairs={{8,0},{9,1},{10,2},{11,3},{12,4},{13,5},{14,6},{15,7},{16,8},{17,9... | collective-permute-start | bytes 41480 | tf_op jit(solution)/shard_map/ppermute | solution.py:41
  10.1 6.4 %collective-permute-start.2 = (bf16[18,1152]{1,0:T(8,128)(2,1)S(1)}, bf16[18,1152]{1,0:T(8,128)(2,1)S(1)}, u32[]{:S(2)}, u32[]{:S(2)}) collective-permute-start(bf16[18,1152]{1,0:T(8,128)(2,1)S(1)} %shard_map.78.refs_1_), channel_id=1, source_target_pairs={{48,0},{49,1},{50,2},{51,3},{52,4},{53,5},{54,6},{55,7},{56,8},{57... | collective-permute-start | bytes 124424 | tf_op jit(solution)/shard_map/ppermute | solution.py:41
  12.7 6.0 %collective-permute-start.3 = (bf16[18,1152]{1,0:T(8,128)(2,1)S(1)}, bf16[18,1152]{1,0:T(8,128)(2,1)S(1)}, u32[]{:S(2)}, u32[]{:S(2)}) collective-permute-start(bf16[18,1152]{1,0:T(8,128)(2,1)S(1)} %shard_map.78.refs_1_), channel_id=1, source_target_pairs={{24,0},{25,1},{26,2},{27,3},{28,4},{29,5},{30,6},{31,7},{32,8},{33... | collective-permute-start | bytes 124424 | tf_op jit(solution)/shard_map/ppermute | solution.py:41
  18.8 13.9 %collective-permute-start.4 = (bf16[48,1152]{1,0:T(8,128)(2,1)S(1)}, bf16[48,1152]{1,0:T(8,128)(2,1)S(1)}, u32[]{:S(2)}, u32[]{:S(2)}) collective-permute-start(bf16[48,1152]{1,0:T(8,128)(2,1)S(1)} %shard_map.79.refs_0_), channel_id=1, source_target_pairs={{2,0},{65,1},{4,2},{67,3},{6,4},{69,5},{0,6},{71,7},{10,8},{73,9},... | collective-permute-start | bytes 331784 | tf_op jit(solution)/shard_map/ppermute | solution.py:41
  19.6 17.3 %collective-permute-start.5 = (bf16[48,1152]{1,0:T(8,128)(2,1)S(1)}, bf16[48,1152]{1,0:T(8,128)(2,1)S(1)}, u32[]{:S(2)}, u32[]{:S(2)}) collective-permute-start(bf16[48,1152]{1,0:T(8,128)(2,1)S(1)} %shard_map.79.refs_0_), channel_id=1, source_target_pairs={{4,0},{129,1},{6,2},{131,3},{0,4},{133,5},{2,6},{135,7},{12,8},{13... | collective-permute-start | bytes 331784 | tf_op jit(solution)/shard_map/ppermute | solution.py:41
  31.4 5.4 %collective-permute-start.6 = (bf16[48,1152]{1,0:T(8,128)(2,1)S(1)}, bf16[48,1152]{1,0:T(8,128)(2,1)S(1)}, u32[]{:S(2)}, u32[]{:S(2)}) collective-permute-start(bf16[48,1152]{1,0:T(8,128)(2,1)S(1)} %shard_map.79.refs_0_), channel_id=1, source_target_pairs={{6,0},{193,1},{0,2},{195,3},{2,4},{197,5},{4,6},{199,7},{14,8},{20... | collective-permute-start | bytes 331784 | tf_op jit(solution)/shard_map/ppermute | solution.py:41
  31.4 21.1 %collective-permute-start.15 = (bf16[256,1152]{1,0:T(8,128)(2,1)S(1)}, bf16[256,1152]{1,0:T(8,128)(2,1)S(1)}, u32[]{:S(2)}, u32[]{:S(2)}) collective-permute-start(bf16[256,1152]{1,0:T(8,128)(2,1)S(1)} %collective-permute-done.14.t1), channel_id=1, source_target_pairs={{1,0},{2,1},{3,2},{4,3},{5,4},{6,5},{7,6},{8,7},{9,8},{10,9},{11,1... | collective-permute-start | bytes 1769480 | tf_op jit(solution)/shard_map/ppermute | solution.py:41
  36.9 8.5 %collective-permute-start.7 = (bf16[192,1152]{1,0:T(8,128)(2,1)S(1)}, bf16[192,1152]{1,0:T(8,128)(2,1)}, u32[]{:S(2)}, u32[]{:S(2)}) collective-permute-start(bf16[192,1152]{1,0:T(8,128)(2,1)S(1)} %shard_map.80.refs_0_), channel_id=1, source_target_pairs={{64,0},{3,1},{66,2},{5,3},{68,4},{7,5},{70,6},{1,7},{72,8},{11,9},... | collective-permute-start | bytes 1327112 | tf_op jit(solution)/shard_map/ppermute | solution.py:41
  37.9 10.0 %collective-permute-start.8 = (bf16[192,1152]{1,0:T(8,128)(2,1)S(1)}, bf16[192,1152]{1,0:T(8,128)(2,1)}, u32[]{:S(2)}, u32[]{:S(2)}) collective-permute-start(bf16[192,1152]{1,0:T(8,128)(2,1)S(1)} %shard_map.80.refs_0_), channel_id=1, source_target_pairs={{128,0},{5,1},{130,2},{7,3},{132,4},{1,5},{134,6},{3,7},{136,8},{1... | collective-permute-start | bytes 1327112 | tf_op jit(solution)/shard_map/ppermute | solution.py:41
  38.4 14.1 %collective-permute-start.9 = (bf16[192,1152]{1,0:T(8,128)(2,1)S(1)}, bf16[192,1152]{1,0:T(8,128)(2,1)}, u32[]{:S(2)}, u32[]{:S(2)}) collective-permute-start(bf16[192,1152]{1,0:T(8,128)(2,1)S(1)} %shard_map.80.refs_0_), channel_id=1, source_target_pairs={{192,0},{7,1},{194,2},{1,3},{196,4},{3,5},{198,6},{5,7},{200,8},{1... | collective-permute-start | bytes 1327112 | tf_op jit(solution)/shard_map/ppermute | solution.py:41
  39.4 20.8 %collective-permute-start.10 = (bf16[192,1152]{1,0:T(8,128)(2,1)S(1)}, bf16[192,1152]{1,0:T(8,128)(2,1)}, u32[]{:S(2)}, u32[]{:S(2)}) collective-permute-start(bf16[192,1152]{1,0:T(8,128)(2,1)S(1)} %shard_map.80.refs_0_), channel_id=1, source_target_pairs={{1,0},{0,1},{3,2},{2,3},{5,4},{4,5},{7,6},{6,7},{9,8},{8,9},{11,10... | collective-permute-start | bytes 1327112 | tf_op jit(solution)/shard_map/ppermute | solution.py:41
  45.4 14.8 %collective-permute-start.11 = (bf16[192,1152]{1,0:T(8,128)(2,1)}, bf16[192,1152]{1,0:T(8,128)(2,1)}, u32[]{:S(2)}, u32[]{:S(2)}) collective-permute-start(bf16[192,1152]{1,0:T(8,128)(2,1)} %collective-permute-done.7.refs_1_), channel_id=1, source_target_pairs={{1,0},{0,1},{3,2},{2,3},{5,4},{4,5},{7,6},{6,7},{9,8},{8,9},{11,10... | collective-permute-start | bytes 1327112 | tf_op jit(solution)/shard_map/ppermute | solution.py:41
  47.9 12.3 %collective-permute-start.12 = (bf16[192,1152]{1,0:T(8,128)(2,1)}, bf16[192,1152]{1,0:T(8,128)(2,1)}, u32[]{:S(2)}, u32[]{:S(2)}) collective-permute-start(bf16[192,1152]{1,0:T(8,128)(2,1)} %collective-permute-done.8.refs_2_), channel_id=1, source_target_pairs={{1,0},{0,1},{3,2},{2,3},{5,4},{4,5},{7,6},{6,7},{9,8},{8,9},{11,10... | collective-permute-start | bytes 1327112 | tf_op jit(solution)/shard_map/ppermute | solution.py:41
  52.5 7.7 %collective-permute-start.13 = (bf16[192,1152]{1,0:T(8,128)(2,1)}, bf16[192,1152]{1,0:T(8,128)(2,1)}, u32[]{:S(2)}, u32[]{:S(2)}) collective-permute-start(bf16[192,1152]{1,0:T(8,128)(2,1)} %collective-permute-done.9.refs_3_), channel_id=1, source_target_pairs={{1,0},{0,1},{3,2},{2,3},{5,4},{4,5},{7,6},{6,7},{9,8},{8,9},{11,10... | collective-permute-start | bytes 1327112 | tf_op jit(solution)/shard_map/ppermute | solution.py:41
  52.5 11.8 %collective-permute-start.16 = (bf16[256,1152]{1,0:T(8,128)(2,1)S(1)}, bf16[256,1152]{1,0:T(8,128)(2,1)S(1)}, u32[]{:S(2)}, u32[]{:S(2)}) collective-permute-start(bf16[256,1152]{1,0:T(8,128)(2,1)S(1)} %collective-permute-done.15.t2), channel_id=1, source_target_pairs={{1,0},{2,1},{3,2},{4,3},{5,4},{6,5},{7,6},{8,7},{9,8},{10,9},{11,1... | collective-permute-start | bytes 1769480 | tf_op jit(solution)/shard_map/ppermute | solution.py:41
  63.7 9.4 %collective-permute-start.17 = (bf16[256,1152]{1,0:T(8,128)(2,1)S(1)}, bf16[256,1152]{1,0:T(8,128)(2,1)S(1)}, u32[]{:S(2)}, u32[]{:S(2)}) collective-permute-start(bf16[256,1152]{1,0:T(8,128)(2,1)S(1)} %get-tuple-element.25.low_ref.p0), channel_id=1, source_target_pairs={{255,0},{0,1},{1,2},{2,3},{3,4},{4,5},{5,6},{6,7},{7,8},{8,9},{9,1... | collective-permute-start | bytes 1769480 | tf_op jit(solution)/shard_map/ppermute | solution.py:41
  67.1 12.9 %collective-permute-start.25 = (bf16[192,1152]{1,0:T(8,128)(2,1)S(1)}, bf16[192,1152]{1,0:T(8,128)(2,1)S(1)}, u32[]{:S(2)}, u32[]{:S(2)}) collective-permute-start(bf16[192,1152]{1,0:T(8,128)(2,1)S(1)} %shard_map.92), channel_id=1, source_target_pairs={{1,0},{0,1},{3,2},{2,3},{5,4},{4,5},{7,6},{6,7},{9,8},{8,9},{11,10... | collective-permute-start | bytes 1327112 | tf_op jit(solution)/shard_map/ppermute | solution.py:41
  71.3 9.6 %collective-permute-start.23 = (bf16[192,1152]{1,0:T(8,128)(2,1)S(1)}, bf16[192,1152]{1,0:T(8,128)(2,1)S(1)}, u32[]{:S(2)}, u32[]{:S(2)}) collective-permute-start(bf16[192,1152]{1,0:T(8,128)(2,1)S(1)} %shard_map.90), channel_id=1, source_target_pairs={{1,0},{0,1},{3,2},{2,3},{5,4},{4,5},{7,6},{6,7},{9,8},{8,9},{11,10... | collective-permute-start | bytes 1327112 | tf_op jit(solution)/shard_map/ppermute | solution.py:41
  71.7 10.2 %collective-permute-start.21 = (bf16[192,1152]{1,0:T(8,128)(2,1)S(1)}, bf16[192,1152]{1,0:T(8,128)(2,1)S(1)}, u32[]{:S(2)}, u32[]{:S(2)}) collective-permute-start(bf16[192,1152]{1,0:T(8,128)(2,1)S(1)} %shard_map.88), channel_id=1, source_target_pairs={{1,0},{0,1},{3,2},{2,3},{5,4},{4,5},{7,6},{6,7},{9,8},{8,9},{11,10... | collective-permute-start | bytes 1327112 | tf_op jit(solution)/shard_map/ppermute | solution.py:41
  73.1 36.3 %collective-permute-start.18 = (bf16[256,1152]{1,0:T(8,128)(2,1)S(1)}, bf16[256,1152]{1,0:T(8,128)(2,1)S(1)}, u32[]{:S(2)}, u32[]{:S(2)}) collective-permute-start(bf16[256,1152]{1,0:T(8,128)(2,1)S(1)} %collective-permute-done.17.p1), channel_id=1, source_target_pairs={{255,0},{0,1},{1,2},{2,3},{3,4},{4,5},{5,6},{6,7},{7,8},{8,9},{9,1... | collective-permute-start | bytes 1769480 | tf_op jit(solution)/shard_map/ppermute | solution.py:41
  75.3 8.1 %collective-permute-start.20 = (bf16[192,1152]{1,0:T(8,128)(2,1)S(1)}, bf16[192,1152]{1,0:T(8,128)(2,1)S(1)}, u32[]{:S(2)}, u32[]{:S(2)}) collective-permute-start(bf16[192,1152]{1,0:T(8,128)(2,1)S(1)} %shard_map.86), channel_id=1, source_target_pairs={{1,0},{0,1},{3,2},{2,3},{5,4},{4,5},{7,6},{6,7},{9,8},{8,9},{11,10... | collective-permute-start | bytes 1327112 | tf_op jit(solution)/shard_map/ppermute | solution.py:41
  80.2 8.4 %collective-permute-start.26 = (bf16[192,1152]{1,0:T(8,128)(2,1)S(1)}, bf16[192,1152]{1,0:T(8,128)(2,1)S(1)}, u32[]{:S(2)}, u32[]{:S(2)}) collective-permute-start(bf16[192,1152]{1,0:T(8,128)(2,1)S(1)} %shard_map.93), channel_id=1, source_target_pairs={{64,0},{3,1},{66,2},{5,3},{68,4},{7,5},{70,6},{1,7},{72,8},{11,9},... | collective-permute-start | bytes 1327112 | tf_op jit(solution)/shard_map/ppermute | solution.py:41
  81.2 10.0 %collective-permute-start.24 = (bf16[192,1152]{1,0:T(8,128)(2,1)S(1)}, bf16[192,1152]{1,0:T(8,128)(2,1)S(1)}, u32[]{:S(2)}, u32[]{:S(2)}) collective-permute-start(bf16[192,1152]{1,0:T(8,128)(2,1)S(1)} %shard_map.91), channel_id=1, source_target_pairs={{128,0},{5,1},{130,2},{7,3},{132,4},{1,5},{134,6},{3,7},{136,8},{1... | collective-permute-start | bytes 1327112 | tf_op jit(solution)/shard_map/ppermute | solution.py:41
  82.2 13.7 %collective-permute-start.22 = (bf16[192,1152]{1,0:T(8,128)(2,1)S(1)}, bf16[192,1152]{1,0:T(8,128)(2,1)S(1)}, u32[]{:S(2)}, u32[]{:S(2)}) collective-permute-start(bf16[192,1152]{1,0:T(8,128)(2,1)S(1)} %shard_map.89), channel_id=1, source_target_pairs={{192,0},{7,1},{194,2},{1,3},{196,4},{3,5},{198,6},{5,7},{200,8},{1... | collective-permute-start | bytes 1327112 | tf_op jit(solution)/shard_map/ppermute | solution.py:41
  96.1 15.8 %collective-permute-start.27 = (bf16[48,1152]{1,0:T(8,128)(2,1)S(1)}, bf16[48,1152]{1,0:T(8,128)(2,1)S(1)}, u32[]{:S(2)}, u32[]{:S(2)}) collective-permute-start(bf16[48,1152]{1,0:T(8,128)(2,1)S(1)} %get-tuple-element.34), channel_id=1, source_target_pairs={{6,0},{193,1},{0,2},{195,3},{2,4},{197,5},{4,6},{199,7},{14,8},{20... | collective-permute-start | bytes 331784 | tf_op jit(solution)/shard_map/ppermute | solution.py:41
  108.4 6.4 %collective-permute-start.28 = (bf16[48,1152]{1,0:T(8,128)(2,1)S(1)}, bf16[48,1152]{1,0:T(8,128)(2,1)S(1)}, u32[]{:S(2)}, u32[]{:S(2)}) collective-permute-start(bf16[48,1152]{1,0:T(8,128)(2,1)S(1)} %get-tuple-element.35), channel_id=1, source_target_pairs={{4,0},{129,1},{6,2},{131,3},{0,4},{133,5},{2,6},{135,7},{12,8},{13... | collective-permute-start | bytes 331784 | tf_op jit(solution)/shard_map/ppermute | solution.py:41
  108.4 7.1 %collective-permute-start.29 = (bf16[48,1152]{1,0:T(8,128)(2,1)S(1)}, bf16[48,1152]{1,0:T(8,128)(2,1)S(1)}, u32[]{:S(2)}, u32[]{:S(2)}) collective-permute-start(bf16[48,1152]{1,0:T(8,128)(2,1)S(1)} %get-tuple-element.36), channel_id=1, source_target_pairs={{2,0},{65,1},{4,2},{67,3},{6,4},{69,5},{0,6},{71,7},{10,8},{73,9},... | collective-permute-start | bytes 331784 | tf_op jit(solution)/shard_map/ppermute | solution.py:41
  109.4 22.8 %collective-permute-start.19 = (bf16[256,1152]{1,0:T(8,128)(2,1)S(1)}, bf16[256,1152]{1,0:T(8,128)(2,1)S(1)}, u32[]{:S(2)}, u32[]{:S(2)}) collective-permute-start(bf16[256,1152]{1,0:T(8,128)(2,1)S(1)} %collective-permute-done.18.p2), channel_id=1, source_target_pairs={{255,0},{0,1},{1,2},{2,3},{3,4},{4,5},{5,6},{6,7},{7,8},{8,9},{9,1... | collective-permute-start | bytes 1769480 | tf_op jit(solution)/shard_map/ppermute | solution.py:41
  115.6 7.2 %collective-permute-start.31 = (bf16[18,1152]{1,0:T(8,128)(2,1)S(1)}, bf16[18,1152]{1,0:T(8,128)(2,1)S(1)}, u32[]{:S(2)}, u32[]{:S(2)}) collective-permute-start(bf16[18,1152]{1,0:T(8,128)(2,1)S(1)} %get-tuple-element.39), channel_id=1, source_target_pairs={{40,0},{41,1},{42,2},{43,3},{44,4},{45,5},{46,6},{47,7},{48,8},{49... | collective-permute-start | bytes 124424 | tf_op jit(solution)/shard_map/ppermute | solution.py:41
  115.7 5.3 %collective-permute-start.30 = (bf16[12,1152]{1,0:T(8,128)(2,1)S(1)}, bf16[12,1152]{1,0:T(8,128)(2,1)S(1)}, u32[]{:S(2)}, u32[]{:S(2)}) collective-permute-start(bf16[12,1152]{1,0:T(8,128)(2,1)S(1)} %get-tuple-element.38), channel_id=1, source_target_pairs={{16,0},{17,1},{18,2},{19,3},{20,4},{21,5},{22,6},{23,7},{24,8},{25... | collective-permute-start | bytes 82952 | tf_op jit(solution)/shard_map/ppermute | solution.py:41
  122.9 5.6 %collective-permute-start.32 = (bf16[6,1152]{1,0:T(8,128)(2,1)S(1)}, bf16[6,1152]{1,0:T(8,128)(2,1)S(1)}, u32[]{:S(2)}, u32[]{:S(2)}) collective-permute-start(bf16[6,1152]{1,0:T(8,128)(2,1)S(1)} %get-tuple-element.41), channel_id=1, source_target_pairs={{8,0},{9,1},{10,2},{11,3},{12,4},{13,5},{14,6},{15,7},{16,8},{17,9... | collective-permute-start | bytes 41480 | tf_op jit(solution)/shard_map/ppermute | solution.py:41
  126.6 5.0 %collective-permute-start.33 = (bf16[6,1152]{1,0:T(8,128)(2,1)S(1)}, bf16[6,1152]{1,0:T(8,128)(2,1)S(1)}, u32[]{:S(2)}, u32[]{:S(2)}) collective-permute-start(bf16[6,1152]{1,0:T(8,128)(2,1)S(1)} %get-tuple-element.42), channel_id=1, source_target_pairs={{56,0},{57,1},{58,2},{59,3},{60,4},{61,5},{62,6},{63,7},{0,8},{1,9... | collective-permute-start | bytes 41480 | tf_op jit(solution)/shard_map/ppermute | solution.py:41

commit v6 on v5

--- a/solution.py
+++ b/solution.py
@@ -104,7 +104,7 @@
     copy.start()
     y, z, x, c = (coord_ref[i] for i in range(4))
     row = lax.broadcasted_iota(jnp.int32, (SUB, 1), 0)
-    within = (z + row // OWN + (NZ - 3)) % NZ * (NX * NC * OWN) + row % OWN
+    within = (z + row // OWN + (NZ - 4)) % NZ * (NX * NC * OWN) + row % OWN
     lanes = lax.broadcasted_iota(jnp.int32, (SUB, D), 1)
 
     @pl.loop(0, D // COLS)
@@ -128,14 +128,26 @@
         xp_ref[:, rows] = mm(x_ref[...], pick_ref[rows, :], NT).astype(BF16)
 
 
-def embed_body(xp_ref, *refs):
-    pieces, (w_ref, unit_ref, low_ref, length_ref) = refs[:8], refs[8:]
+def stacked(pieces, w_ref):
     for i, piece in enumerate(pieces):
         w_ref[pl.ds(i * PIECE, PIECE), :] = piece[...]
+
+
+def embed_part_body(xp_ref, *refs):
+    pieces, (w_ref, part_ref) = refs[:4], refs[4:]
+    stacked(pieces, w_ref)
+    for at in range(0, E, COLS):
+        cols = pl.ds(at, COLS)
+        part_ref[:, cols] = mm(xp_ref[:, pl.ds(0, HALF)], w_ref[:, cols])
+
+
+def embed_body(xp_ref, part_ref, *refs):
+    pieces, (w_ref, unit_ref, low_ref, length_ref) = refs[:4], refs[4:]
+    stacked(pieces, w_ref)
     squares = jnp.zeros((R, 1), F32)
     for at in range(0, E, COLS):
         cols = pl.ds(at, COLS)
-        part = mm(xp_ref[...], w_ref[:, cols])
+        part = part_ref[:, cols] + mm(xp_ref[:, pl.ds(HALF, HALF)], w_ref[:, cols])
         unit_ref[:, cols] = part
         squares = squares + jnp.sum(part * part, axis=1, keepdims=True)
     length = jnp.sqrt(squares + EPS)
@@ -191,11 +203,11 @@
         refs[-1][pl.ds(i * SUB, SUB), :] = ref[...]
 
 
-def features_body(eg_ref, w_ref, pick_ref, out_ref, mixed):
-    @pl.loop(0, D // COLS)
-    def _(i):
-        rows = pl.ds(pl.multiple_of(i * COLS, COLS), COLS)
-        mixed[:, rows] = mm(eg_ref[...], w_ref[rows, :], NT).astype(BF16)
+def features_body(eg_ref, own_ref, other_ref, pick_ref, out_ref, mixed):
+    for half, w_ref in enumerate((own_ref, other_ref)):
+        for at in range(0, HALF, COLS):
+            part = mm(eg_ref[...], w_ref[pl.ds(at, COLS), :], NT)
+            mixed[:, pl.ds(half * HALF + at, COLS)] = part.astype(BF16)
 
     @pl.loop(0, D // COLS)
     def _(i):
@@ -240,9 +252,9 @@
 
 def near_body(mid_ref, low_ref, high_ref, *outs):
     mid, low, high = (ref[...].astype(F32) for ref in (mid_ref, low_ref, high_ref))
-    outs[0][...] = (mid[:OWN] + low[:OWN] + high[:OWN]).astype(BF16)
-    outs[1][...] = mid[OWN : 2 * OWN] + low[OWN:] + high[OWN : 2 * OWN]
-    outs[2][...] = (mid[2 * OWN :] + high[2 * OWN :]).astype(BF16)
+    outs[0][...] = (mid[:OWN] + low[:OWN]).astype(BF16)
+    outs[1][...] = mid[OWN : 2 * OWN] + low[OWN : 2 * OWN] + high[:OWN]
+    outs[2][...] = (mid[2 * OWN :] + low[2 * OWN :] + high[OWN:]).astype(BF16)
 
 
 def join(rows, *parts):
@@ -252,8 +264,9 @@
 
 def gather_weight(kept, before, after):
     near = join((OWN,) * 3, before, kept, after)
-    high, low = fetch(near, along_z(3)), fetch(near, along_z(-2))
-    ring = join((2 * OWN, 3 * OWN, 3 * OWN), low, near, high)
+    near_high = join((OWN,) * 2, kept, after)
+    low, high = fetch(near, along_z(-3)), fetch(near_high, along_z(2))
+    ring = join((3 * OWN, 3 * OWN, 2 * OWN), low, near, high)
     plane = [fetch(ring, along_first(d)) for d in (1, 2, 3)]
     (plane,) = call(stack_body, [((PIECE, E), BF16)], ring, *plane, flops=10**6)
     half = [plane] + [fetch(plane, along_second(d)) for d in (1, 2, 3)]
@@ -265,11 +278,11 @@
     cuts = [(i * SUB, (i + 1) * SUB) for i in range(4)]
     pieces = call(functools.partial(sum_body, cuts=cuts), [((SUB, E), BF16)] * 4, *got, flops=10**8)
     got = [pieces[0]] + [fetch(pieces[d], along_first(-d)) for d in (1, 2, 3)]
-    cuts = [(0, 2 * OWN), (2 * OWN, 5 * OWN), (5 * OWN, 8 * OWN)]
+    cuts = [(0, 3 * OWN), (3 * OWN, 6 * OWN), (6 * OWN, 8 * OWN)]
     low, mid, high = call(
         functools.partial(sum_body, cuts=cuts), [((hi - lo, E), BF16) for lo, hi in cuts], *got, flops=10**8
     )
-    high, low = fetch(high, along_z(-3)), fetch(low, along_z(2))
+    low, high = fetch(low, along_z(3)), fetch(high, along_z(-2))
     before, own, after = call(
         near_body, [((OWN, E), BF16), ((OWN, E), F32), ((OWN, E), BF16)], mid, low, high, flops=10**8
     )
@@ -295,9 +308,10 @@
         flops=4 * D * D * R, smem=(0,), hbm=(1,),
         scratch=[pltpu.VMEM((R, D), BF16), pltpu.SemaphoreType.DMA(())],
     )
-    full, unit, low, length = call(
-        embed_body, [((D, E), BF16), ((R, E), F32), ((R, E), BF16), ((R, 1), F32)], xp, *weight,
-        flops=2 * R * D * E,
+    own_rows, part = call(embed_part_body, [((HALF, E), BF16), ((R, E), F32)], xp, *weight[:4], flops=2 * R * HALF * E)
+    other_rows, unit, low, length = call(
+        embed_body, [((HALF, E), BF16), ((R, E), F32), ((R, E), BF16), ((R, 1), F32)], xp, part, *weight[4:],
+        flops=2 * R * HALF * E,
     )
     images = [low]
     for _ in range(1, S):
@@ -312,7 +326,7 @@
         (sent,) = call(functools.partial(sibling_body, piece=i), [((PIECE, E), BF16)], xpt, eg, flops=2 * R * PIECE * E)
         came.append(fetch(sent, sibling))
     (grad_features,) = call(
-        features_body, [((R, D), BF16)], eg, full, pick, flops=2 * R * D * E + 2 * R * D * D,
+        features_body, [((R, D), BF16)], eg, own_rows, other_rows, pick, flops=2 * R * D * E + 2 * R * D * D,
         scratch=[pltpu.VMEM((R, D), BF16)], final=True,
     )
     pieces = []

time: 135 us -> 136 us (level)
  the two profiles are of different devices: /device:TPU:6 before, /device:TPU:1 now
where the time goes in v6:
time: 136 us; the launch traced here: 135 us
  starting transfers between devices  70.6 us (52%)
  waiting for transfers between devices  35.5 us (26%)
  Pallas kernels  26.4 us (19%)
  between operations  2.23 us (2%)
    ppermute x34, starting transfers between devices, fetch(): lax.ppermute(value, AXES, [(index(*where(*coords(i))), i) for i in range(...  70.6 us
    ppermute x34, waiting for transfers between devices, fetch(): lax.ppermute(value, AXES, [(index(*where(*coords(i))), i) for i in range(...  35.5 us
    pallas_call x23, Pallas kernels, call(): pl.pallas_call(body, out_shape=[jax.ShapeDtypeStruct(s, d) if final else...  26.4 us
  transfers between devices with their start and end apart: 34, of which 13 were waited for; matrix products, arithmetic and copies ran while one was open for 1% of the time, Pallas kernels for 17%

profile of v6, /device:TPU:1, one launch (start us, length us, event | category | flops | bytes accessed | tf_op | source)
XLA Modules:
  0.0 135.5 jit_solution(5687462284911295308)
XLA Ops:
  0.6 1.3 shard_map.77
  2.0 3.3 %collective-permute-start.14 = (bf16[256,1152]{1,0:T(8,128)(2,1)S(1)}, bf16[256,1152]{1,0:T(8,128)(2,1)S(1)}, u32[]{:S(2)}, u32[]{:S(2)}) collective-permute-start(bf16[256,1152]{1,0:T(8,128)(2,1)S(1)} %get-tuple-element.31.t0.low_ref), channel_id=1, source_target_pairs={{1,0},{2,1},{3,2},{4,3},{5,4},{6,5},{7,6},{8,7},{9,8},{10,9},{11,1... | collective-permute-start | bytes 1769480 | tf_op jit(solution)/shard_map/ppermute | solution.py:41
  5.2 3.9 %collective-permute-start.1 = (bf16[6,1152]{1,0:T(8,128)(2,1)}, bf16[6,1152]{1,0:T(8,128)(2,1)S(1)}, u32[]{:S(2)}, u32[]{:S(2)}) collective-permute-start(bf16[6,1152]{1,0:T(8,128)(2,1)} %w_source.1), channel_id=1, source_target_pairs={{8,0},{9,1},{10,2},{11,3},{12,4},{13,5},{14,6},{15,7},{16,8},{17,9... | collective-permute-start | bytes 41480 | tf_op jit(solution)/shard_map/ppermute | solution.py:41
  9.1 1.1 collective-permute-done.1.refs_2_.refs_1_
  10.2 2.9 %collective-permute-done.refs_0_ = bf16[6,1152]{1,0:T(8,128)(2,1)S(1)} collective-permute-done((bf16[6,1152]{1,0:T(8,128)(2,1)}, bf16[6,1152]{1,0:T(8,128)(2,1)S(1)}, u32[]{:S(2)}, u32[]{:S(2)}) %collective-permute-start) | collective-permute-done | bytes 13856 | tf_op jit(solution)/shard_map/ppermute | solution.py:41
  13.3 8.0 %collective-permute-start.15 = (bf16[256,1152]{1,0:T(8,128)(2,1)S(1)}, bf16[256,1152]{1,0:T(8,128)(2,1)S(1)}, u32[]{:S(2)}, u32[]{:S(2)}) collective-permute-start(bf16[256,1152]{1,0:T(8,128)(2,1)S(1)} %collective-permute-done.14.t1), channel_id=1, source_target_pairs={{1,0},{2,1},{3,2},{4,3},{5,4},{6,5},{7,6},{8,7},{9,8},{10,9},{11,1... | collective-permute-start | bytes 1769480 | tf_op jit(solution)/shard_map/ppermute | solution.py:41
  21.3 1.7 %collective-permute-start.3 = (bf16[12,1152]{1,0:T(8,128)(2,1)S(1)}, bf16[12,1152]{1,0:T(8,128)(2,1)S(1)}, u32[]{:S(2)}, u32[]{:S(2)}) collective-permute-start(bf16[12,1152]{1,0:T(8,128)(2,1)S(1)} %shard_map.79), channel_id=1, source_target_pairs={{16,0},{17,1},{18,2},{19,3},{20,4},{21,5},{22,6},{23,7},{24,8},{25... | collective-permute-start | bytes 82952 | tf_op jit(solution)/shard_map/ppermute | solution.py:41
  23.0 2.5 %collective-permute-done.3.refs_2_ = bf16[12,1152]{1,0:T(8,128)(2,1)S(1)} collective-permute-done((bf16[12,1152]{1,0:T(8,128)(2,1)S(1)}, bf16[12,1152]{1,0:T(8,128)(2,1)S(1)}, u32[]{:S(2)}, u32[]{:S(2)}) %collective-permute-start.3) | collective-permute-done | bytes 27680 | tf_op jit(solution)/shard_map/ppermute | solution.py:41
  25.5 3.0 %collective-permute-start.4 = (bf16[48,1152]{1,0:T(8,128)(2,1)S(1)}, bf16[48,1152]{1,0:T(8,128)(2,1)S(1)}, u32[]{:S(2)}, u32[]{:S(2)}) collective-permute-start(bf16[48,1152]{1,0:T(8,128)(2,1)S(1)} %shard_map.80.refs_0_), channel_id=1, source_target_pairs={{2,0},{65,1},{4,2},{67,3},{6,4},{69,5},{0,6},{71,7},{10,8},{73,9},... | collective-permute-start | bytes 331784 | tf_op jit(solution)/shard_map/ppermute | solution.py:41
  28.6 0.7 collective-permute-start.6
  29.3 2.1 %collective-permute-done.4.refs_1_ = bf16[48,1152]{1,0:T(8,128)(2,1)S(1)} collective-permute-done((bf16[48,1152]{1,0:T(8,128)(2,1)S(1)}, bf16[48,1152]{1,0:T(8,128)(2,1)S(1)}, u32[]{:S(2)}, u32[]{:S(2)}) %collective-permute-start.4) | collective-permute-done | bytes 110624 | tf_op jit(solution)/shard_map/ppermute | solution.py:41
  31.4 2.3 %collective-permute-done.5.refs_2_ = bf16[48,1152]{1,0:T(8,128)(2,1)S(1)} collective-permute-done((bf16[48,1152]{1,0:T(8,128)(2,1)S(1)}, bf16[48,1152]{1,0:T(8,128)(2,1)S(1)}, u32[]{:S(2)}, u32[]{:S(2)}) %collective-permute-start.5) | collective-permute-done | bytes 110624 | tf_op jit(solution)/shard_map/ppermute | solution.py:41
  33.7 0.8 collective-permute-done.6.refs_3_
  34.8 1.4 collective-permute-start.9
  36.2 14.0 %collective-permute-start.10 = (bf16[192,1152]{1,0:T(8,128)(2,1)S(1)}, bf16[192,1152]{1,0:T(8,128)(2,1)}, u32[]{:S(2)}, u32[]{:S(2)}) collective-permute-start(bf16[192,1152]{1,0:T(8,128)(2,1)S(1)} %shard_map.81.refs_0_), channel_id=1, source_target_pairs={{1,0},{0,1},{3,2},{2,3},{5,4},{4,5},{7,6},{6,7},{9,8},{8,9},{11,10... | collective-permute-start | bytes 1327112 | tf_op jit(solution)/shard_map/ppermute | solution.py:41
  50.2 6.2 %collective-permute-start.11 = (bf16[192,1152]{1,0:T(8,128)(2,1)}, bf16[192,1152]{1,0:T(8,128)(2,1)}, u32[]{:S(2)}, u32[]{:S(2)}) collective-permute-start(bf16[192,1152]{1,0:T(8,128)(2,1)} %collective-permute-done.7.refs_1_), channel_id=1, source_target_pairs={{1,0},{0,1},{3,2},{2,3},{5,4},{4,5},{7,6},{6,7},{9,8},{8,9},{11,10... | collective-permute-start | bytes 1327112 | tf_op jit(solution)/shard_map/ppermute | solution.py:41
  56.3 2.4 %collective-permute-start.12 = (bf16[192,1152]{1,0:T(8,128)(2,1)}, bf16[192,1152]{1,0:T(8,128)(2,1)}, u32[]{:S(2)}, u32[]{:S(2)}) collective-permute-start(bf16[192,1152]{1,0:T(8,128)(2,1)} %collective-permute-done.8.refs_2_), channel_id=1, source_target_pairs={{1,0},{0,1},{3,2},{2,3},{5,4},{4,5},{7,6},{6,7},{9,8},{8,9},{11,10... | collective-permute-start | bytes 1327112 | tf_op jit(solution)/shard_map/ppermute | solution.py:41
  58.8 4.6 %collective-permute-start.13 = (bf16[192,1152]{1,0:T(8,128)(2,1)}, bf16[192,1152]{1,0:T(8,128)(2,1)}, u32[]{:S(2)}, u32[]{:S(2)}) collective-permute-start(bf16[192,1152]{1,0:T(8,128)(2,1)} %collective-permute-done.9.refs_3_), channel_id=1, source_target_pairs={{1,0},{0,1},{3,2},{2,3},{5,4},{4,5},{7,6},{6,7},{9,8},{8,9},{11,10... | collective-permute-start | bytes 1327112 | tf_op jit(solution)/shard_map/ppermute | solution.py:41
  64.8 6.2 %shard_map.76 = (bf16[1536,1536]{1,0:T(8,128)(2,1)S(1)}, bf16[256,1536]{1,0:T(8,128)(2,1)S(1)}, bf16[1536,256]{1,0:T(8,128)(2,1)S(1)}) custom-call(s32[4]{0:T(128)S(1)} %pad_add_fusion.coord_ref, bf16[256,1536]{1,0:T(8,128)(2,1)} %source_ref.1), custom_call_target="tpu_custom_call" | custom-call | flops 2415919104 | tf_op jit(solution)/shard_map/pallas_call | solution.py:68
  71.1 2.1 %shard_map.82 = (bf16[768,1152]{1,0:T(8,128)(2,1)S(1)}, f32[256,1152]{1,0:T(8,128)S(1)}) custom-call(bf16[256,1536]{1,0:T(8,128)(2,1)S(1)} %get-tuple-element.25.xp_ref, bf16[192,1152]{1,0:T(8,128)(2,1)S(1)} %shard_map.81.refs_0_, bf16[192,1152]{1,0:T(8,128)(2,1)} %collective-permute-done.7.refs_1_, bf16[192,1152]{1,0:T(8,128)(2,1)} %collective-permute-done.8.refs_2_, ...), custom_call_target="tpu_custom_call" | custom-call | flops 452984832 | tf_op jit(solution)/shard_map/pallas_call | solution.py:68
  73.2 2.4 %shard_map.83 = (bf16[768,1152]{1,0:T(8,128)(2,1)S(1)}, f32[256,1152]{1,0:T(8,128)S(1)}, bf16[256,1152]{1,0:T(8,128)(2,1)S(1)}, f32[256,1]{1,0:T(8,128)S(1)}) custom-call(bf16[256,1536]{1,0:T(8,128)(2,1)S(1)} %get-tuple-element.25.xp_ref, f32[256,1152]{1,0:T(8,128)S(1)} %get-tuple-element.27.part_ref, bf16[192,1152]{1,0:T(8,128)(2,1)} %collective-permute-done.10.refs_0_, ...), custom_call_target="tpu_custom_call" | custom-call | flops 452984832 | tf_op jit(solution)/shard_map/pallas_call | solution.py:68
  75.5 1.8 %collective-permute-start.17 = (bf16[256,1152]{1,0:T(8,128)(2,1)S(1)}, bf16[256,1152]{1,0:T(8,128)(2,1)S(1)}, u32[]{:S(2)}, u32[]{:S(2)}) collective-permute-start(bf16[256,1152]{1,0:T(8,128)(2,1)S(1)} %get-tuple-element.28.low_ref.p0), channel_id=1, source_target_pairs={{255,0},{0,1},{1,2},{2,3},{3,4},{4,5},{5,6},{6,7},{7,8},{8,9},{9,1... | collective-permute-start | bytes 1769480 | tf_op jit(solution)/shard_map/ppermute | solution.py:41
  77.4 2.4 %shard_map.84.eg_ref = bf16[256,1152]{1,0:T(8,128)(2,1)S(1)} custom-call(f32[2]{0:T(128)S(1)} %pad_maximum_fusion.scalar_ref, bf16[256,1152]{1,0:T(8,128)(2,1)S(1)} %get-tuple-element.28.low_ref.p0, f32[256,1152]{1,0:T(8,128)S(1)} %get-tuple-element.29.unit_ref, f32[256,1]{1,0:T(8,128)S(1)} %get-tuple-element.30.length_ref, ...), custom_call_target="tpu_custom_call" | custom-call | flops 1207959552 | tf_op jit(solution)/shard_map/pallas_call | solution.py:68
  80.6 0.6 collective-permute-start.23
  81.6 2.6 %collective-permute-done.17.p1 = bf16[256,1152]{1,0:T(8,128)(2,1)S(1)} collective-permute-done((bf16[256,1152]{1,0:T(8,128)(2,1)S(1)}, bf16[256,1152]{1,0:T(8,128)(2,1)S(1)}, u32[]{:S(2)}, u32[]{:S(2)}) %collective-permute-start.17) | collective-permute-done | bytes 589856 | tf_op jit(solution)/shard_map/ppermute | solution.py:41
  84.2 2.5 %collective-permute-start.18 = (bf16[256,1152]{1,0:T(8,128)(2,1)S(1)}, bf16[256,1152]{1,0:T(8,128)(2,1)S(1)}, u32[]{:S(2)}, u32[]{:S(2)}) collective-permute-start(bf16[256,1152]{1,0:T(8,128)(2,1)S(1)} %collective-permute-done.17.p1), channel_id=1, source_target_pairs={{255,0},{0,1},{1,2},{2,3},{3,4},{4,5},{5,6},{6,7},{7,8},{8,9},{9,1... | collective-permute-start | bytes 1769480 | tf_op jit(solution)/shard_map/ppermute | solution.py:41
  87.0 3.8 %collective-permute-start.20 = (bf16[192,1152]{1,0:T(8,128)(2,1)S(1)}, bf16[192,1152]{1,0:T(8,128)(2,1)S(1)}, u32[]{:S(2)}, u32[]{:S(2)}) collective-permute-start(bf16[192,1152]{1,0:T(8,128)(2,1)S(1)} %shard_map.88), channel_id=1, source_target_pairs={{1,0},{0,1},{3,2},{2,3},{5,4},{4,5},{7,6},{6,7},{9,8},{8,9},{11,10... | collective-permute-start | bytes 1327112 | tf_op jit(solution)/shard_map/ppermute | solution.py:41
  90.8 0.3 shard_map.95
  91.1 0.4 collective-permute-start.26
  91.5 0.3 shard_map.93
  91.9 0.3 shard_map.91
  92.2 1.5 %collective-permute-start.22 = (bf16[192,1152]{1,0:T(8,128)(2,1)S(1)}, bf16[192,1152]{1,0:T(8,128)(2,1)S(1)}, u32[]{:S(2)}, u32[]{:S(2)}) collective-permute-start(bf16[192,1152]{1,0:T(8,128)(2,1)S(1)} %shard_map.91), channel_id=1, source_target_pairs={{192,0},{7,1},{194,2},{1,3},{196,4},{3,5},{198,6},{5,7},{200,8},{1... | collective-permute-start | bytes 1327112 | tf_op jit(solution)/shard_map/ppermute | solution.py:41
  93.6 0.3 shard_map.89.refs_0_
  93.9 4.7 %collective-permute-done.26.refs_3_ = bf16[192,1152]{1,0:T(8,128)(2,1)S(1)} collective-permute-done((bf16[192,1152]{1,0:T(8,128)(2,1)S(1)}, bf16[192,1152]{1,0:T(8,128)(2,1)S(1)}, u32[]{:S(2)}, u32[]{:S(2)}) %collective-permute-start.26) | collective-permute-done | bytes 442400 | tf_op jit(solution)/shard_map/ppermute | solution.py:41
  98.6 8.2 %collective-permute-done.24.refs_2_ = bf16[192,1152]{1,0:T(8,128)(2,1)S(1)} collective-permute-done((bf16[192,1152]{1,0:T(8,128)(2,1)S(1)}, bf16[192,1152]{1,0:T(8,128)(2,1)S(1)}, u32[]{:S(2)}, u32[]{:S(2)}) %collective-permute-start.24) | collective-permute-done | bytes 442400 | tf_op jit(solution)/shard_map/ppermute | solution.py:41
  106.8 4.9 %collective-permute-done.22.refs_1_ = bf16[192,1152]{1,0:T(8,128)(2,1)S(1)} collective-permute-done((bf16[192,1152]{1,0:T(8,128)(2,1)S(1)}, bf16[192,1152]{1,0:T(8,128)(2,1)S(1)}, u32[]{:S(2)}, u32[]{:S(2)}) %collective-permute-start.22) | collective-permute-done | bytes 442400 | tf_op jit(solution)/shard_map/ppermute | solution.py:41
  112.0 1.4 %collective-permute-start.28 = (bf16[48,1152]{1,0:T(8,128)(2,1)S(1)}, bf16[48,1152]{1,0:T(8,128)(2,1)S(1)}, u32[]{:S(2)}, u32[]{:S(2)}) collective-permute-start(bf16[48,1152]{1,0:T(8,128)(2,1)S(1)} %get-tuple-element.39), channel_id=1, source_target_pairs={{4,0},{129,1},{6,2},{131,3},{0,4},{133,5},{2,6},{135,7},{12,8},{13... | collective-permute-start | bytes 331784 | tf_op jit(solution)/shard_map/ppermute | solution.py:41
  113.4 1.2 collective-permute-start.29
  114.7 2.9 %collective-permute-start.19 = (bf16[256,1152]{1,0:T(8,128)(2,1)S(1)}, bf16[256,1152]{1,0:T(8,128)(2,1)S(1)}, u32[]{:S(2)}, u32[]{:S(2)}) collective-permute-start(bf16[256,1152]{1,0:T(8,128)(2,1)S(1)} %collective-permute-done.18.p2), channel_id=1, source_target_pairs={{255,0},{0,1},{1,2},{2,3},{3,4},{4,5},{5,6},{6,7},{7,8},{8,9},{9,1... | collective-permute-start | bytes 1769480 | tf_op jit(solution)/shard_map/ppermute | solution.py:41
  117.6 0.7 collective-permute-done.27.refs_1_
  118.3 0.6 collective-permute-done.29.refs_3_
  119.1 1.1 collective-permute-start.31
  120.2 4.7 %shard_map.85 = bf16[256,1536]{1,0:T(8,128)(2,1)} custom-call(bf16[256,1152]{1,0:T(8,128)(2,1)S(1)} %shard_map.84.eg_ref, bf16[768,1152]{1,0:T(8,128)(2,1)S(1)} %get-tuple-element.32.own_ref, bf16[768,1152]{1,0:T(8,128)(2,1)S(1)} %get-tuple-element.33.other_ref, bf16[1536,1536]{1,0:T(8,128)(2,1)S(1)} %get-tuple-element.34.pick_ref), custom_call_target="tpu_custom_call" | custom-call | flops 2113929216 | tf_op jit(solution)/shard_map/pallas_call | solution.py:68
  124.9 3.5 %collective-permute-start.32 = (bf16[6,1152]{1,0:T(8,128)(2,1)S(1)}, bf16[6,1152]{1,0:T(8,128)(2,1)S(1)}, u32[]{:S(2)}, u32[]{:S(2)}) collective-permute-start(bf16[6,1152]{1,0:T(8,128)(2,1)S(1)} %get-tuple-element.45), channel_id=1, source_target_pairs={{8,0},{9,1},{10,2},{11,3},{12,4},{13,5},{14,6},{15,7},{16,8},{17,9... | collective-permute-start | bytes 41480 | tf_op jit(solution)/shard_map/ppermute | solution.py:41
  128.5 1.9 %shard_map.86.part_ref = f32[256,1152]{1,0:T(8,128)S(1)} custom-call(f32[2]{0:T(128)S(1)} %pad_maximum_fusion.scalar_ref, bf16[256,1152]{1,0:T(8,128)(2,1)S(1)} %get-tuple-element.31.t0.low_ref, bf16[256,1152]{1,0:T(8,128)(2,1)S(1)} %get-tuple-element.28.low_ref.p0, bf16[256,1152]{1,0:T(8,128)(2,1)S(1)} %collective-permute-done.17.p1, ...), custom_call_target="tpu_custom_call" | custom-call | flops 905969664 | tf_op jit(solution)/shard_map/pallas_call | solution.py:68
  130.4 1.9 %collective-permute-done.33 = bf16[6,1152]{1,0:T(8,128)(2,1)S(1)} collective-permute-done((bf16[6,1152]{1,0:T(8,128)(2,1)S(1)}, bf16[6,1152]{1,0:T(8,128)(2,1)S(1)}, u32[]{:S(2)}, u32[]{:S(2)}) %collective-permute-start.33) | collective-permute-done | bytes 13856 | tf_op jit(solution)/shard_map/ppermute | solution.py:41
  132.3 0.6 convert_add_fusion
  132.9 2.6 %shard_map.87 = bf16[256,1152]{1,0:T(8,128)(2,1)} custom-call(f32[2]{0:T(128)S(1)} %pad_maximum_fusion.scalar_ref, bf16[256,1152]{1,0:T(8,128)(2,1)S(1)} %get-tuple-element.35.raw_ref, bf16[256,1152]{1,0:T(8,128)(2,1)S(1)} %get-tuple-element.31.t0.low_ref, bf16[256,1152]{1,0:T(8,128)(2,1)S(1)} %collective-permute-done.19.p3, f32[256,1152]{1,0:T(8,128)S(1)} %shard_map.86.part_ref), custom_call_target="tpu_custom_call" | custom-call | flops 301989888 | tf_op jit(solution)/shard_map/pallas_call | solution.py:68
  (46 shorter events, 2.6 us)
Async XLA Ops:
  2.0 11.3 %collective-permute-start.14 = (bf16[256,1152]{1,0:T(8,128)(2,1)S(1)}, bf16[256,1152]{1,0:T(8,128)(2,1)S(1)}, u32[]{:S(2)}, u32[]{:S(2)}) collective-permute-start(bf16[256,1152]{1,0:T(8,128)(2,1)S(1)} %get-tuple-element.31.t0.low_ref), channel_id=1, source_target_pairs={{1,0},{2,1},{3,2},{4,3},{5,4},{6,5},{7,6},{8,7},{9,8},{10,9},{11,1... | collective-permute-start | bytes 1769480 | tf_op jit(solution)/shard_map/ppermute | solution.py:41
  5.2 5.0 %collective-permute-start.1 = (bf16[6,1152]{1,0:T(8,128)(2,1)}, bf16[6,1152]{1,0:T(8,128)(2,1)S(1)}, u32[]{:S(2)}, u32[]{:S(2)}) collective-permute-start(bf16[6,1152]{1,0:T(8,128)(2,1)} %w_source.1), channel_id=1, source_target_pairs={{8,0},{9,1},{10,2},{11,3},{12,4},{13,5},{14,6},{15,7},{16,8},{17,9... | collective-permute-start | bytes 41480 | tf_op jit(solution)/shard_map/ppermute | solution.py:41
  9.1 4.0 %collective-permute-start = (bf16[6,1152]{1,0:T(8,128)(2,1)}, bf16[6,1152]{1,0:T(8,128)(2,1)S(1)}, u32[]{:S(2)}, u32[]{:S(2)}) collective-permute-start(bf16[6,1152]{1,0:T(8,128)(2,1)} %w_source.1), channel_id=1, source_target_pairs={{56,0},{57,1},{58,2},{59,3},{60,4},{61,5},{62,6},{63,7},{0,8},{1,9... | collective-permute-start | bytes 41480 | tf_op jit(solution)/shard_map/ppermute | solution.py:41
  13.2 12.3 %collective-permute-start.2 = (bf16[18,1152]{1,0:T(8,128)(2,1)S(1)}, bf16[18,1152]{1,0:T(8,128)(2,1)S(1)}, u32[]{:S(2)}, u32[]{:S(2)}) collective-permute-start(bf16[18,1152]{1,0:T(8,128)(2,1)S(1)} %shard_map.78.refs_1_), channel_id=1, source_target_pairs={{40,0},{41,1},{42,2},{43,3},{44,4},{45,5},{46,6},{47,7},{48,8},{49... | collective-permute-start | bytes 124424 | tf_op jit(solution)/shard_map/ppermute | solution.py:41
  13.3 50.1 %collective-permute-start.15 = (bf16[256,1152]{1,0:T(8,128)(2,1)S(1)}, bf16[256,1152]{1,0:T(8,128)(2,1)S(1)}, u32[]{:S(2)}, u32[]{:S(2)}) collective-permute-start(bf16[256,1152]{1,0:T(8,128)(2,1)S(1)} %collective-permute-done.14.t1), channel_id=1, source_target_pairs={{1,0},{2,1},{3,2},{4,3},{5,4},{6,5},{7,6},{8,7},{9,8},{10,9},{11,1... | collective-permute-start | bytes 1769480 | tf_op jit(solution)/shard_map/ppermute | solution.py:41
  21.3 4.2 %collective-permute-start.3 = (bf16[12,1152]{1,0:T(8,128)(2,1)S(1)}, bf16[12,1152]{1,0:T(8,128)(2,1)S(1)}, u32[]{:S(2)}, u32[]{:S(2)}) collective-permute-start(bf16[12,1152]{1,0:T(8,128)(2,1)S(1)} %shard_map.79), channel_id=1, source_target_pairs={{16,0},{17,1},{18,2},{19,3},{20,4},{21,5},{22,6},{23,7},{24,8},{25... | collective-permute-start | bytes 82952 | tf_op jit(solution)/shard_map/ppermute | solution.py:41
  25.5 5.9 %collective-permute-start.4 = (bf16[48,1152]{1,0:T(8,128)(2,1)S(1)}, bf16[48,1152]{1,0:T(8,128)(2,1)S(1)}, u32[]{:S(2)}, u32[]{:S(2)}) collective-permute-start(bf16[48,1152]{1,0:T(8,128)(2,1)S(1)} %shard_map.80.refs_0_), channel_id=1, source_target_pairs={{2,0},{65,1},{4,2},{67,3},{6,4},{69,5},{0,6},{71,7},{10,8},{73,9},... | collective-permute-start | bytes 331784 | tf_op jit(solution)/shard_map/ppermute | solution.py:41
  28.5 5.2 %collective-permute-start.5 = (bf16[48,1152]{1,0:T(8,128)(2,1)S(1)}, bf16[48,1152]{1,0:T(8,128)(2,1)S(1)}, u32[]{:S(2)}, u32[]{:S(2)}) collective-permute-start(bf16[48,1152]{1,0:T(8,128)(2,1)S(1)} %shard_map.80.refs_0_), channel_id=1, source_target_pairs={{4,0},{129,1},{6,2},{131,3},{0,4},{133,5},{2,6},{135,7},{12,8},{13... | collective-permute-start | bytes 331784 | tf_op jit(solution)/shard_map/ppermute | solution.py:41
  28.6 6.0 %collective-permute-start.6 = (bf16[48,1152]{1,0:T(8,128)(2,1)S(1)}, bf16[48,1152]{1,0:T(8,128)(2,1)S(1)}, u32[]{:S(2)}, u32[]{:S(2)}) collective-permute-start(bf16[48,1152]{1,0:T(8,128)(2,1)S(1)} %shard_map.80.refs_0_), channel_id=1, source_target_pairs={{6,0},{193,1},{0,2},{195,3},{2,4},{197,5},{4,6},{199,7},{14,8},{20... | collective-permute-start | bytes 331784 | tf_op jit(solution)/shard_map/ppermute | solution.py:41
  34.6 15.5 %collective-permute-start.7 = (bf16[192,1152]{1,0:T(8,128)(2,1)S(1)}, bf16[192,1152]{1,0:T(8,128)(2,1)}, u32[]{:S(2)}, u32[]{:S(2)}) collective-permute-start(bf16[192,1152]{1,0:T(8,128)(2,1)S(1)} %shard_map.81.refs_0_), channel_id=1, source_target_pairs={{64,0},{3,1},{66,2},{5,3},{68,4},{7,5},{70,6},{1,7},{72,8},{11,9},... | collective-permute-start | bytes 1327112 | tf_op jit(solution)/shard_map/ppermute | solution.py:41
  34.7 21.6 %collective-permute-start.8 = (bf16[192,1152]{1,0:T(8,128)(2,1)S(1)}, bf16[192,1152]{1,0:T(8,128)(2,1)}, u32[]{:S(2)}, u32[]{:S(2)}) collective-permute-start(bf16[192,1152]{1,0:T(8,128)(2,1)S(1)} %shard_map.81.refs_0_), channel_id=1, source_target_pairs={{128,0},{5,1},{130,2},{7,3},{132,4},{1,5},{134,6},{3,7},{136,8},{1... | collective-permute-start | bytes 1327112 | tf_op jit(solution)/shard_map/ppermute | solution.py:41
  34.8 24.0 %collective-permute-start.9 = (bf16[192,1152]{1,0:T(8,128)(2,1)S(1)}, bf16[192,1152]{1,0:T(8,128)(2,1)}, u32[]{:S(2)}, u32[]{:S(2)}) collective-permute-start(bf16[192,1152]{1,0:T(8,128)(2,1)S(1)} %shard_map.81.refs_0_), channel_id=1, source_target_pairs={{192,0},{7,1},{194,2},{1,3},{196,4},{3,5},{198,6},{5,7},{200,8},{1... | collective-permute-start | bytes 1327112 | tf_op jit(solution)/shard_map/ppermute | solution.py:41
  36.2 37.0 %collective-permute-start.10 = (bf16[192,1152]{1,0:T(8,128)(2,1)S(1)}, bf16[192,1152]{1,0:T(8,128)(2,1)}, u32[]{:S(2)}, u32[]{:S(2)}) collective-permute-start(bf16[192,1152]{1,0:T(8,128)(2,1)S(1)} %shard_map.81.refs_0_), channel_id=1, source_target_pairs={{1,0},{0,1},{3,2},{2,3},{5,4},{4,5},{7,6},{6,7},{9,8},{8,9},{11,10... | collective-permute-start | bytes 1327112 | tf_op jit(solution)/shard_map/ppermute | solution.py:41
  50.2 23.0 %collective-permute-start.11 = (bf16[192,1152]{1,0:T(8,128)(2,1)}, bf16[192,1152]{1,0:T(8,128)(2,1)}, u32[]{:S(2)}, u32[]{:S(2)}) collective-permute-start(bf16[192,1152]{1,0:T(8,128)(2,1)} %collective-permute-done.7.refs_1_), channel_id=1, source_target_pairs={{1,0},{0,1},{3,2},{2,3},{5,4},{4,5},{7,6},{6,7},{9,8},{8,9},{11,10... | collective-permute-start | bytes 1327112 | tf_op jit(solution)/shard_map/ppermute | solution.py:41
  56.3 16.8 %collective-permute-start.12 = (bf16[192,1152]{1,0:T(8,128)(2,1)}, bf16[192,1152]{1,0:T(8,128)(2,1)}, u32[]{:S(2)}, u32[]{:S(2)}) collective-permute-start(bf16[192,1152]{1,0:T(8,128)(2,1)} %collective-permute-done.8.refs_2_), channel_id=1, source_target_pairs={{1,0},{0,1},{3,2},{2,3},{5,4},{4,5},{7,6},{6,7},{9,8},{8,9},{11,10... | collective-permute-start | bytes 1327112 | tf_op jit(solution)/shard_map/ppermute | solution.py:41
  58.8 14.4 %collective-permute-start.13 = (bf16[192,1152]{1,0:T(8,128)(2,1)}, bf16[192,1152]{1,0:T(8,128)(2,1)}, u32[]{:S(2)}, u32[]{:S(2)}) collective-permute-start(bf16[192,1152]{1,0:T(8,128)(2,1)} %collective-permute-done.9.refs_3_), channel_id=1, source_target_pairs={{1,0},{0,1},{3,2},{2,3},{5,4},{4,5},{7,6},{6,7},{9,8},{8,9},{11,10... | collective-permute-start | bytes 1327112 | tf_op jit(solution)/shard_map/ppermute | solution.py:41
  63.4 14.0 %collective-permute-start.16 = (bf16[256,1152]{1,0:T(8,128)(2,1)S(1)}, bf16[256,1152]{1,0:T(8,128)(2,1)S(1)}, u32[]{:S(2)}, u32[]{:S(2)}) collective-permute-start(bf16[256,1152]{1,0:T(8,128)(2,1)S(1)} %collective-permute-done.15.t2), channel_id=1, source_target_pairs={{1,0},{2,1},{3,2},{4,3},{5,4},{6,5},{7,6},{8,7},{9,8},{10,9},{11,1... | collective-permute-start | bytes 1769480 | tf_op jit(solution)/shard_map/ppermute | solution.py:41
  75.5 8.6 %collective-permute-start.17 = (bf16[256,1152]{1,0:T(8,128)(2,1)S(1)}, bf16[256,1152]{1,0:T(8,128)(2,1)S(1)}, u32[]{:S(2)}, u32[]{:S(2)}) collective-permute-start(bf16[256,1152]{1,0:T(8,128)(2,1)S(1)} %get-tuple-element.28.low_ref.p0), channel_id=1, source_target_pairs={{255,0},{0,1},{1,2},{2,3},{3,4},{4,5},{5,6},{6,7},{7,8},{8,9},{9,1... | collective-permute-start | bytes 1769480 | tf_op jit(solution)/shard_map/ppermute | solution.py:41
  80.2 10.6 %collective-permute-start.25 = (bf16[192,1152]{1,0:T(8,128)(2,1)S(1)}, bf16[192,1152]{1,0:T(8,128)(2,1)S(1)}, u32[]{:S(2)}, u32[]{:S(2)}) collective-permute-start(bf16[192,1152]{1,0:T(8,128)(2,1)S(1)} %shard_map.94), channel_id=1, source_target_pairs={{1,0},{0,1},{3,2},{2,3},{5,4},{4,5},{7,6},{6,7},{9,8},{8,9},{11,10... | collective-permute-start | bytes 1327112 | tf_op jit(solution)/shard_map/ppermute | solution.py:41
  80.6 10.9 %collective-permute-start.23 = (bf16[192,1152]{1,0:T(8,128)(2,1)S(1)}, bf16[192,1152]{1,0:T(8,128)(2,1)S(1)}, u32[]{:S(2)}, u32[]{:S(2)}) collective-permute-start(bf16[192,1152]{1,0:T(8,128)(2,1)S(1)} %shard_map.92), channel_id=1, source_target_pairs={{1,0},{0,1},{3,2},{2,3},{5,4},{4,5},{7,6},{6,7},{9,8},{8,9},{11,10... | collective-permute-start | bytes 1327112 | tf_op jit(solution)/shard_map/ppermute | solution.py:41
  81.5 10.4 %collective-permute-start.21 = (bf16[192,1152]{1,0:T(8,128)(2,1)S(1)}, bf16[192,1152]{1,0:T(8,128)(2,1)S(1)}, u32[]{:S(2)}, u32[]{:S(2)}) collective-permute-start(bf16[192,1152]{1,0:T(8,128)(2,1)S(1)} %shard_map.90), channel_id=1, source_target_pairs={{1,0},{0,1},{3,2},{2,3},{5,4},{4,5},{7,6},{6,7},{9,8},{8,9},{11,10... | collective-permute-start | bytes 1327112 | tf_op jit(solution)/shard_map/ppermute | solution.py:41
  84.2 30.5 %collective-permute-start.18 = (bf16[256,1152]{1,0:T(8,128)(2,1)S(1)}, bf16[256,1152]{1,0:T(8,128)(2,1)S(1)}, u32[]{:S(2)}, u32[]{:S(2)}) collective-permute-start(bf16[256,1152]{1,0:T(8,128)(2,1)S(1)} %collective-permute-done.17.p1), channel_id=1, source_target_pairs={{255,0},{0,1},{1,2},{2,3},{3,4},{4,5},{5,6},{6,7},{7,8},{8,9},{9,1... | collective-permute-start | bytes 1769480 | tf_op jit(solution)/shard_map/ppermute | solution.py:41
  87.0 6.7 %collective-permute-start.20 = (bf16[192,1152]{1,0:T(8,128)(2,1)S(1)}, bf16[192,1152]{1,0:T(8,128)(2,1)S(1)}, u32[]{:S(2)}, u32[]{:S(2)}) collective-permute-start(bf16[192,1152]{1,0:T(8,128)(2,1)S(1)} %shard_map.88), channel_id=1, source_target_pairs={{1,0},{0,1},{3,2},{2,3},{5,4},{4,5},{7,6},{6,7},{9,8},{8,9},{11,10... | collective-permute-start | bytes 1327112 | tf_op jit(solution)/shard_map/ppermute | solution.py:41
  91.1 7.5 %collective-permute-start.26 = (bf16[192,1152]{1,0:T(8,128)(2,1)S(1)}, bf16[192,1152]{1,0:T(8,128)(2,1)S(1)}, u32[]{:S(2)}, u32[]{:S(2)}) collective-permute-start(bf16[192,1152]{1,0:T(8,128)(2,1)S(1)} %shard_map.95), channel_id=1, source_target_pairs={{64,0},{3,1},{66,2},{5,3},{68,4},{7,5},{70,6},{1,7},{72,8},{11,9},... | collective-permute-start | bytes 1327112 | tf_op jit(solution)/shard_map/ppermute | solution.py:41
  91.8 15.0 %collective-permute-start.24 = (bf16[192,1152]{1,0:T(8,128)(2,1)S(1)}, bf16[192,1152]{1,0:T(8,128)(2,1)S(1)}, u32[]{:S(2)}, u32[]{:S(2)}) collective-permute-start(bf16[192,1152]{1,0:T(8,128)(2,1)S(1)} %shard_map.93), channel_id=1, source_target_pairs={{128,0},{5,1},{130,2},{7,3},{132,4},{1,5},{134,6},{3,7},{136,8},{1... | collective-permute-start | bytes 1327112 | tf_op jit(solution)/shard_map/ppermute | solution.py:41
  92.2 19.5 %collective-permute-start.22 = (bf16[192,1152]{1,0:T(8,128)(2,1)S(1)}, bf16[192,1152]{1,0:T(8,128)(2,1)S(1)}, u32[]{:S(2)}, u32[]{:S(2)}) collective-permute-start(bf16[192,1152]{1,0:T(8,128)(2,1)S(1)} %shard_map.91), channel_id=1, source_target_pairs={{192,0},{7,1},{194,2},{1,3},{196,4},{3,5},{198,6},{5,7},{200,8},{1... | collective-permute-start | bytes 1327112 | tf_op jit(solution)/shard_map/ppermute | solution.py:41
  111.9 6.4 %collective-permute-start.27 = (bf16[48,1152]{1,0:T(8,128)(2,1)S(1)}, bf16[48,1152]{1,0:T(8,128)(2,1)S(1)}, u32[]{:S(2)}, u32[]{:S(2)}) collective-permute-start(bf16[48,1152]{1,0:T(8,128)(2,1)S(1)} %get-tuple-element.38), channel_id=1, source_target_pairs={{6,0},{193,1},{0,2},{195,3},{2,4},{197,5},{4,6},{199,7},{14,8},{20... | collective-permute-start | bytes 331784 | tf_op jit(solution)/shard_map/ppermute | solution.py:41
  112.0 6.3 %collective-permute-start.28 = (bf16[48,1152]{1,0:T(8,128)(2,1)S(1)}, bf16[48,1152]{1,0:T(8,128)(2,1)S(1)}, u32[]{:S(2)}, u32[]{:S(2)}) collective-permute-start(bf16[48,1152]{1,0:T(8,128)(2,1)S(1)} %get-tuple-element.39), channel_id=1, source_target_pairs={{4,0},{129,1},{6,2},{131,3},{0,4},{133,5},{2,6},{135,7},{12,8},{13... | collective-permute-start | bytes 331784 | tf_op jit(solution)/shard_map/ppermute | solution.py:41
  113.4 5.5 %collective-permute-start.29 = (bf16[48,1152]{1,0:T(8,128)(2,1)S(1)}, bf16[48,1152]{1,0:T(8,128)(2,1)S(1)}, u32[]{:S(2)}, u32[]{:S(2)}) collective-permute-start(bf16[48,1152]{1,0:T(8,128)(2,1)S(1)} %get-tuple-element.40), channel_id=1, source_target_pairs={{2,0},{65,1},{4,2},{67,3},{6,4},{69,5},{0,6},{71,7},{10,8},{73,9},... | collective-permute-start | bytes 331784 | tf_op jit(solution)/shard_map/ppermute | solution.py:41
  114.7 18.2 %collective-permute-start.19 = (bf16[256,1152]{1,0:T(8,128)(2,1)S(1)}, bf16[256,1152]{1,0:T(8,128)(2,1)S(1)}, u32[]{:S(2)}, u32[]{:S(2)}) collective-permute-start(bf16[256,1152]{1,0:T(8,128)(2,1)S(1)} %collective-permute-done.18.p2), channel_id=1, source_target_pairs={{255,0},{0,1},{1,2},{2,3},{3,4},{4,5},{5,6},{6,7},{7,8},{8,9},{9,1... | collective-permute-start | bytes 1769480 | tf_op jit(solution)/shard_map/ppermute | solution.py:41
  119.0 5.9 %collective-permute-start.30 = (bf16[18,1152]{1,0:T(8,128)(2,1)S(1)}, bf16[18,1152]{1,0:T(8,128)(2,1)S(1)}, u32[]{:S(2)}, u32[]{:S(2)}) collective-permute-start(bf16[18,1152]{1,0:T(8,128)(2,1)S(1)} %get-tuple-element.42), channel_id=1, source_target_pairs={{24,0},{25,1},{26,2},{27,3},{28,4},{29,5},{30,6},{31,7},{32,8},{33... | collective-permute-start | bytes 124424 | tf_op jit(solution)/shard_map/ppermute | solution.py:41
  119.1 5.8 %collective-permute-start.31 = (bf16[12,1152]{1,0:T(8,128)(2,1)S(1)}, bf16[12,1152]{1,0:T(8,128)(2,1)S(1)}, u32[]{:S(2)}, u32[]{:S(2)}) collective-permute-start(bf16[12,1152]{1,0:T(8,128)(2,1)S(1)} %get-tuple-element.43), channel_id=1, source_target_pairs={{48,0},{49,1},{50,2},{51,3},{52,4},{53,5},{54,6},{55,7},{56,8},{57... | collective-permute-start | bytes 82952 | tf_op jit(solution)/shard_map/ppermute | solution.py:41
  124.9 5.5 %collective-permute-start.32 = (bf16[6,1152]{1,0:T(8,128)(2,1)S(1)}, bf16[6,1152]{1,0:T(8,128)(2,1)S(1)}, u32[]{:S(2)}, u32[]{:S(2)}) collective-permute-start(bf16[6,1152]{1,0:T(8,128)(2,1)S(1)} %get-tuple-element.45), channel_id=1, source_target_pairs={{8,0},{9,1},{10,2},{11,3},{12,4},{13,5},{14,6},{15,7},{16,8},{17,9... | collective-permute-start | bytes 41480 | tf_op jit(solution)/shard_map/ppermute | solution.py:41
  128.5 3.8 %collective-permute-start.33 = (bf16[6,1152]{1,0:T(8,128)(2,1)S(1)}, bf16[6,1152]{1,0:T(8,128)(2,1)S(1)}, u32[]{:S(2)}, u32[]{:S(2)}) collective-permute-start(bf16[6,1152]{1,0:T(8,128)(2,1)S(1)} %get-tuple-element.46), channel_id=1, source_target_pairs={{56,0},{57,1},{58,2},{59,3},{60,4},{61,5},{62,6},{63,7},{0,8},{1,9... | collective-permute-start | bytes 41480 | tf_op jit(solution)/shard_map/ppermute | solution.py:41
